TPU v7x, 512 devices: a whole 4x4x16 slice. The times are simulated.
512 devices in a mesh: dp: 16 (over x, z_hi, core), shard: 32 (over z_lo, y).
Axes of the slice: x: 4, y: 4, z: 16 (z_hi: 2, z_lo: 8; z = z_hi * 8 + z_lo), core: 2. Of those that a mesh axis runs over, the one named last changes fastest.
Arguments:
- tokens: bfloat16 [1024, 6144], P('dp', 'shard'), may hold values from -6 to 6
- cotangent: bfloat16 [1024, 6144], P('dp', 'shard'), may hold values from -12 to 12
- gate_proj: bfloat16 [2, 6144, 16384], P(None, 'dp', 'shard'), may hold values from -0.078125 to 0.078125
- up_proj: bfloat16 [2, 6144, 16384], P(None, 'dp', 'shard'), may hold values from -0.078125 to 0.078125
- down_proj: bfloat16 [2, 16384, 6144], P(None, 'shard', 'dp'), may hold values from -0.046875 to 0.046875
- slot_tokens: int32 [2, 256], P(None, 'dp'), may hold values from 0 to 63, as said below
- gate_weights: float32 [2, 256], P(None, 'dp'), may hold values from 0.1 to 1
- live_counts: int32 [2, 16], P(None, 'dp'), may hold values from 1 to 16, as said below
Outputs:
- grad_tokens: bfloat16 [1024, 6144], P('dp', 'shard')
- grad_gate_proj: bfloat16 [2, 6144, 16384], P(None, 'dp', 'shard')
- grad_up_proj: bfloat16 [2, 6144, 16384], P(None, 'dp', 'shard')
- grad_down_proj: bfloat16 [2, 16384, 6144], P(None, 'shard', 'dp')
Inputs may be any that keep to these rules, and one draw needn't show every extreme that they name: `slot_tokens`: for each expert and each index of dp, the 16 slots name 16 different tokens of that index. `live_counts`: the live slots of an expert at an index of dp are its first ones; 16 is reached at some index of every expert.
All inputs are finite; a program needn't handle non-finite values.
Results may differ from a plain program's by a relative error of at most 0.03.
Values may be sent and summed in bfloat16 or wider, within the bound.
No kernel may reach another device: no remote copies, remote signals or barrier semaphores. Data moves between devices by JAX's collectives and lax.ppermute only.
A program may use at most 64 MiB of HBM per device.

v0:
```python
import jax
import jax.numpy as jnp
from jax import lax
from jax.sharding import PartitionSpec as P


def gather_turned(arrays, axis, dims):
    turned = [jnp.moveaxis(a, dim, 0) for a, dim in zip(arrays, dims)]
    both = jnp.concatenate([t.reshape(len(t), -1) for t in turned], axis=1)
    result, at, outs = (lax.all_gather(both, axis, axis=0, tiled=True), 0, [])
    for t, dim in zip(turned, dims):
        slab = result[:, at : at + t[0].size].reshape(-1, *t.shape[1:])
        outs.append(jnp.moveaxis(slab, 0, dim))
        at += t[0].size
    return tuple(outs)


def in_one_piece(arrays, axis, split_dim, concat_dim, along):
    ends, at = ([], 0)
    for a in arrays[:-1]:
        at += a.shape[along]
        ends.append(at)
    both = jnp.concatenate(arrays, axis=along)
    return tuple(
        jnp.split(
            lax.all_to_all(both, axis, split_axis=split_dim, concat_axis=concat_dim, tiled=True),
            ends,
            axis=along,
        )
    )


def sent_together(arrays, axis, dim, along):
    ends, at = ([], 0)
    for a in arrays[:-1]:
        at += a.shape[along]
        ends.append(at)
    both = jnp.concatenate(arrays, axis=along)
    return tuple(
        jnp.split(lax.psum_scatter(both, axis, scatter_dimension=dim, tiled=True), ends, axis=along)
    )


def side_by_side(arrays, axis, dim, along):
    widths = [a.shape[along] for a in arrays]
    both = jnp.concatenate(arrays, axis=along)
    result = lax.all_gather(both, axis, axis=dim, tiled=True)
    return tuple(jnp.split(result, [sum(widths[:k]) for k in range(1, len(widths))], axis=along))


def cut_along(array, dim, count):
    before, after = (array.shape[:dim], array.shape[dim + 1 :])
    return jnp.moveaxis(array.reshape(*before, count, -1, *after), dim, 0)


def summed_on_arrival(array, axis, dim):
    count = lax.axis_size(axis)
    tiles = lax.all_to_all(cut_along(array, dim, count), axis, 0, 0, tiled=True)
    return jnp.sum(tiles.astype(jnp.float32), axis=0)


def slope_terms(gate_sum, up_sum, cot_hidden):
    sigmoid_part = jax.nn.sigmoid(gate_sum)
    grad_gate = (
        cot_hidden * up_sum * sigmoid_part * (1.0 + gate_sum * (1.0 - sigmoid_part))
    ).astype(jnp.bfloat16)
    grad_up = (cot_hidden * gate_sum * sigmoid_part).astype(jnp.bfloat16)
    return (grad_gate, grad_up)


def on_device(
    tokens, cotangent, gate_proj, up_proj, down_proj, slot_tokens, gate_weights, live_counts
):
    experts_here = slot_tokens.shape[0]
    slot_count = slot_tokens.shape[1]
    token_count = tokens.shape[0]
    position = lax.broadcasted_iota(jnp.int32, slot_tokens.shape, 1)
    alive_mask = (position < live_counts).astype(jnp.float32)
    picked = tokens[slot_tokens]
    weighted = (
        cotangent[slot_tokens].astype(jnp.float32) * (gate_weights * alive_mask)[:, :, None]
    ).astype(jnp.bfloat16)
    full_rows, full_cot = gather_turned((picked, weighted), "shard", (2, 2))
    spread = jnp.broadcast_to(live_counts[:, :, None], (experts_here, 1, lax.axis_size("dp")))
    block_rows, block_cot, heard = (
        *in_one_piece((full_rows, full_cot), "dp", 2, 1, 0),
        lax.all_to_all(spread, "dp", split_axis=2, concat_axis=1, tiled=True),
    )
    totals = jnp.sum(heard, axis=1).astype(jnp.float32)
    gate_part = jnp.einsum(
        "erd,edf->erf", block_rows, gate_proj, preferred_element_type=jnp.float32
    )
    up_part = jnp.einsum("erd,edf->erf", block_rows, up_proj, preferred_element_type=jnp.float32)
    cot_part = jnp.einsum("erd,efd->erf", block_cot, down_proj, preferred_element_type=jnp.float32)
    gate_sum, up_sum, cot_hidden = tuple(
        (
            part.astype(jnp.float32)
            for part in sent_together(
                (
                    gate_part.astype(jnp.bfloat16),
                    up_part.astype(jnp.bfloat16),
                    cot_part.astype(jnp.bfloat16),
                ),
                "dp",
                1,
                0,
            )
        )
    )
    hidden = (jax.nn.silu(gate_sum) * up_sum).astype(jnp.bfloat16)
    grad_gate, grad_up = slope_terms(gate_sum, up_sum, cot_hidden)
    hidden_all, gate_all, up_all = side_by_side((hidden, grad_gate, grad_up), "dp", 1, 0)
    scale_back = totals[:, :, None]
    grad_down_proj = (
        jnp.einsum("erf,erd->efd", hidden_all, block_cot, preferred_element_type=jnp.float32)
        / scale_back
    ).astype(jnp.bfloat16)
    grad_gate_proj = (
        jnp.einsum("erd,erf->edf", block_rows, gate_all, preferred_element_type=jnp.float32)
        / scale_back
    ).astype(jnp.bfloat16)
    grad_up_proj = (
        jnp.einsum("erd,erf->edf", block_rows, up_all, preferred_element_type=jnp.float32)
        / scale_back
    ).astype(jnp.bfloat16)
    back_term = (
        jnp.einsum("erf,edf->erd", gate_all, gate_proj, preferred_element_type=jnp.float32)
        + jnp.einsum("erf,edf->erd", up_all, up_proj, preferred_element_type=jnp.float32)
    ).astype(jnp.bfloat16)
    owned_rows = lax.all_to_all(back_term, "dp", split_axis=1, concat_axis=2, tiled=True)
    row_grads = summed_on_arrival(owned_rows.astype(jnp.float32).astype(jnp.bfloat16), "shard", 2)
    one_hot = (
        slot_tokens[:, :, None]
        == lax.broadcasted_iota(jnp.int32, (experts_here, slot_count, token_count), 2)
    ).astype(jnp.float32)
    grad_tokens = jnp.einsum("ert,erf->tf", one_hot, row_grads).astype(jnp.bfloat16)
    return (grad_tokens, grad_gate_proj, grad_up_proj, grad_down_proj)


def solution(mesh):
    in_specs = (
        P("dp", "shard"),
        P("dp", "shard"),
        P(None, "dp", "shard"),
        P(None, "dp", "shard"),
        P(None, "shard", "dp"),
        P(None, "dp"),
        P(None, "dp"),
        P(None, "dp"),
    )
    out_specs = (
        P("dp", "shard"),
        P(None, "dp", "shard"),
        P(None, "dp", "shard"),
        P(None, "shard", "dp"),
    )
    return jax.shard_map(
        on_device, mesh=mesh, in_specs=in_specs, out_specs=out_specs, check_vma=False
    )
```

profile of v0, /device:TPU:32, one launch (start us, length us, event | category | flops | bytes accessed | tf_op | source)
XLA Modules:
  0.0 493.7 jit_solution(5408034918978574355)
XLA Ops:
  7.2 0.0 copy-start
  7.2 0.0 reduce-scatter.2.cloned.1.call-start
  7.2 0.7 compare_select_fusion
  8.0 0.1 reshape.47
  8.1 1.4 gather_fusion.1
  9.4 1.4 gather_fusion
  10.8 0.8 compare_select_fusion.1
  11.6 0.1 fusion.14
  11.6 113.4 %all-gather = bf16[32,192,64]{1,2,0:T(8,128)(2,1)S(1)} all-gather(bf16[1,192,64]{1,2,0:T(8,128)(2,1)S(1)} %maximum_bitcast_fusion), channel_id=1, replica_groups=mesh['dp'=16,'shard'=32] {'shard'}, dimensions={0}, use_global_device_ids=true | all-gather | bytes 811008 | tf_op jit(solution)/shard_map/all_gather | solution.py:10
  125.1 0.6 copy.39
  125.7 1.1 reshape.67
  126.8 0.1 fusion.17
  126.9 0.1 pad_maximum_fusion.1
  126.9 6.2 %copy.40 = bf16[4,16,6144]{1,0,2:T(4,128)(2,1)} copy(bf16[4,16,6144]{2,1,0:T(8,128)(2,1)S(1)} %pad_maximum_fusion.1) | data formatting | bytes 1572864 | tf_op jit(solution)/shard_map/concatenate | solution.py:23
  133.2 9.3 %reshape.69 = bf16[16,2,12288]{2,1,0:T(2,128)(2,1)S(1)} reshape(bf16[6144,4,16]{2,1,0:T(4,128)(2,1)} %bitcast.53) | data formatting | bytes 1572864
  142.5 45.7 %all_to_all.44 = bf16[16,2,12288]{2,1,0:T(2,128)(2,1)S(1)} all-to-all(bf16[16,2,12288]{2,1,0:T(2,128)(2,1)S(1)} %reshape.69), channel_id=1, replica_groups=mesh['dp'=16,'shard'=32] {'dp'}, dimensions={0} | all-to-all | bytes 1572864 | tf_op jit(solution)/shard_map/all_to_all | solution.py:26
  188.1 5.6 %reshape.70 = bf16[6144,4,16]{2,1,0:T(4,128)(2,1)} reshape(bf16[16,2,12288]{2,1,0:T(2,128)(2,1)S(1)} %all_to_all.44) | data formatting | bytes 1572864
  193.8 6.6 %copy.53 = bf16[4,16,16,384]{3,2,1,0:T(8,128)(2,1)S(1)} copy(bf16[4,16,16,384]{1,0,3,2:T(4,128)(2,1)} %bitcast.54) | data formatting | bytes 1572864 | tf_op jit(solution)/shard_map/all_to_all | solution.py:26
  200.4 0.0 copy-start.2
  200.4 0.1 fusion.16
  200.5 0.1 copy.42
  200.5 0.9 copy-done.2
  201.5 0.4 convolution_convert_fusion.1
  201.9 0.0 copy-done
  201.9 0.0 copy-start.5
  201.9 0.4 convolution_convert_fusion.2
  202.4 0.1 copy.43
  202.5 0.0 copy-start.3
  202.5 0.7 copy-done.3
  203.2 0.0 copy-done.5
  203.2 0.5 convolution_convert_fusion
  203.7 1.3 pad_maximum_fusion
  205.0 0.0 reduce-scatter.2.cloned.1.call-update
  205.0 0.0 all-gather.3.cloned.1.call-start
  205.1 105.9 %reduce-scatter.2.cloned.1.call-done = bf16[6,16,512]{2,1,0:T(8,128)(2,1)} async-done(((bf16[6,256,512]{2,1,0:T(8,128)(2,1)}), bf16[6,16,512]{2,1,0:T(8,128)(2,1)}) %reduce-scatter.2.cloned.1.call-update) | async-done | bytes 98320 | tf_op jit(solution)/shard_map/reduce_scatter | solution.py:40
  311.0 0.8 fusion.4
  311.8 0.7 pad_maximum_fusion.2
  312.5 0.0 all-gather.3.cloned.1.call-update
  312.5 76.3 %all-gather.3.cloned.1.call-done = bf16[6,256,512]{2,1,0:T(8,128)(2,1)} async-done(((bf16[6,16,512]{2,1,0:T(8,128)(2,1)}), bf16[6,256,512]{2,1,0:T(8,128)(2,1)}) %all-gather.3.cloned.1.call-update) | async-done | bytes 1572880 | tf_op jit(solution)/shard_map/all_gather | solution.py:47
  388.8 0.0 copy-start.1
  388.8 1.6 fusion.18
  390.4 0.0 copy-done.1
  390.4 0.5 fusion
  390.9 0.0 copy-start.6
  390.9 0.4 copy.44
  391.3 31.0 %all_to_all.45 = bf16[2,256,384]{2,0,1:T(2,128)(2,1)S(1)} all-to-all(bf16[2,256,384]{2,0,1:T(2,128)(2,1)S(1)} %copy.44), channel_id=1, replica_groups=mesh['dp'=16,'shard'=32] {'dp'}, dimensions={1} | all-to-all | bytes 786432 | tf_op jit(solution)/shard_map/all_to_all | solution.py:130
  422.3 0.0 copy-done.6
  422.3 0.6 broadcast_in_dim.5
  422.9 3.5 all-to-all-start.3
  426.4 0.9 copy.55
  427.3 1.3 reshape.44
  428.6 1.1 copy.46
  429.7 11.3 %all-to-all-done.3 = s32[2,1,16]{0,1,2:T(1,128)S(1)} async-done(((s32[2,1,16]{0,1,2:T(1,128)}), s32[2,1,16]{0,1,2:T(1,128)S(1)}, u32[]{:S(2)}, u32[]{:S(2)}) %all-to-all-start.3) | async-done | bytes 160 | tf_op jit(solution)/shard_map/all_to_all | solution.py:87
  441.1 16.1 %all-to-all-start.2 = ((bf16[32,2,16,192]{3,2,1,0:T(8,128)(2,1)}), bf16[32,2,16,192]{3,2,1,0:T(8,128)(2,1)S(1)}, u32[]{:S(2)}, u32[]{:S(2)}) async-start(bf16[32,2,16,192]{3,2,1,0:T(8,128)(2,1)} %copy.46), calls=%async_computation.3 | async-start | bytes 1048576 | tf_op jit(solution)/shard_map/all_to_all | solution.py:58
  457.3 1.3 divide_convert_fusion.1
  458.6 0.0 copy-start.4
  458.6 1.3 divide_convert_fusion.2
  459.9 0.0 copy-done.4
  459.9 0.0 copy-start.7
  459.9 1.4 divide_convert_fusion
  461.3 24.6 %all-to-all-done.2 = bf16[32,2,16,192]{3,2,1,0:T(8,128)(2,1)S(1)} async-done(((bf16[32,2,16,192]{3,2,1,0:T(8,128)(2,1)}), bf16[32,2,16,192]{3,2,1,0:T(8,128)(2,1)S(1)}, u32[]{:S(2)}, u32[]{:S(2)}) %all-to-all-start.2) | async-done | bytes 393248 | tf_op jit(solution)/shard_map/all_to_all | solution.py:58
  485.9 0.1 convert_reduce_fusion
  486.0 0.0 copy-done.7
  486.0 0.9 fusion.1
  (4 shorter events, 0.1 us)
Async XLA Ops:
  7.2 194.8 %copy-start = (bf16[2,384,512]{2,1,0:T(8,128)(2,1)S(1)}, bf16[2,384,512]{2,1,0:T(8,128)(2,1)}, u32[]{:S(2)}) copy-start(bf16[2,384,512]{2,1,0:T(8,128)(2,1)} %param.10) | copy-start | bytes 2359300
  7.2 303.8 %reduce-scatter.2.cloned.1.call-start = ((), (), s32[]{:S(2)}) async-start(), calls=%async_computation.5 | async-start | bytes 1671168 | tf_op jit(solution)/shard_map/reduce_scatter | solution.py:40
  200.4 1.1 copy-start.2
  201.9 1.3 copy-start.5
  202.5 0.7 copy-start.3
  205.0 183.7 %all-gather.3.cloned.1.call-start = ((), (), s32[]{:S(2)}) async-start(), calls=%async_computation.6 | async-start | bytes 1671168 | tf_op jit(solution)/shard_map/all_gather | solution.py:47
  388.8 1.6 copy-start.1
  390.9 31.4 %copy-start.6 = (s32[2,1]{0,1:T(1,128)S(1)}, s32[2,1]{0,1:T(1,128)}, u32[]{:S(2)}) copy-start(s32[2,1]{0,1:T(1,128)} %param.15) | copy-start | bytes 28
  422.9 18.1 %all-to-all-start.3 = ((s32[2,1,16]{0,1,2:T(1,128)}), s32[2,1,16]{0,1,2:T(1,128)S(1)}, u32[]{:S(2)}, u32[]{:S(2)}) async-start(s32[2,1,16]{0,1,2:T(1,128)} %broadcast_in_dim.5), calls=%async_computation.4 | async-start | bytes 16384 | tf_op jit(solution)/shard_map/all_to_all | solution.py:87
  441.1 44.8 %all-to-all-start.2 = ((bf16[32,2,16,192]{3,2,1,0:T(8,128)(2,1)}), bf16[32,2,16,192]{3,2,1,0:T(8,128)(2,1)S(1)}, u32[]{:S(2)}, u32[]{:S(2)}) async-start(bf16[32,2,16,192]{3,2,1,0:T(8,128)(2,1)} %copy.46), calls=%async_computation.3 | async-start | bytes 1048576 | tf_op jit(solution)/shard_map/all_to_all | solution.py:58
  458.6 1.3 copy-start.4
  459.9 26.2 %copy-start.7 = (s32[2,16]{1,0:T(2,128)S(1)}, s32[2,16]{1,0:T(2,128)}, u32[]{:S(2)}) copy-start(s32[2,16]{1,0:T(2,128)} %param.13) | copy-start | bytes 388
Sparse Core Ops, SparseCore 0:
  205.2 105.7 reduce-scatter.1
  314.9 73.8 all-gather.2
where the time goes:
time: 495 us; the launch traced here: 494 us
  waiting for transfers between devices  218 us (44%)
  blocking collectives  190 us (38%)
  local copies, waits for them, and re-layouts  38.6 us (8%)
  starting transfers between devices  19.7 us (4%)
  between operations  14.3 us (3%)
  matrix products  8.31 us (2%)
    all_gather x1, blocking collectives, gather_turned(): result, at, outs = (lax.all_gather(both, axis, axis=0, tiled=True), 0, [])  113 us
    reduce_scatter x1, waiting for transfers between devices, sent_together(): lax.psum_scatter(both, axis, scatter_dimension=dim, tiled=True)  106 us
    all_gather x1, waiting for transfers between devices, side_by_side(): result = lax.all_gather(both, axis, axis=dim, tiled=True)  76.3 us
    all_to_all x1, blocking collectives, in_one_piece(): lax.all_to_all(both, axis, split_axis=split_dim, concat_axis=concat_dim,...  45.7 us
    all_to_all x1, blocking collectives, on_device(): lax.all_to_all(back_term, 'dp', split_axis=1, concat_axis=2, tiled=True)  31 us
    all_to_all x1, waiting for transfers between devices, summed_on_arrival(): tiles = lax.all_to_all(cut_along(array, dim, count), axis, 0, 0, tiled=True)  24.6 us
    unnamed x19, local copies, waits for them, and re-layouts  17.8 us
    all_to_all x1, starting transfers between devices, summed_on_arrival(): tiles = lax.all_to_all(cut_along(array, dim, count), axis, 0, 0, tiled=True)  16.1 us
  transfers between devices with their start and end apart: 4, of which 4 were waited for; matrix products, arithmetic and copies ran while one was open for 1% of the time, Pallas kernels for 0%

commit v1 on v0

v1 whole, which is shorter than its diff:
```python
import jax
import jax.numpy as jnp
from jax import lax
from jax.experimental import pallas as pl
from jax.experimental.pallas import tpu as pltpu
from jax.sharding import Mesh, PartitionSpec as P

X, ZH, C, ZL, Y = 4, 2, 2, 8, 4
DP = ("x", "zh", "c")
SHARD = ("zl", "y")
EVERY = DP + SHARD
N_SHARD = ZL * Y
HALF = 192
WIDE = 256
R = 16
BF16 = jnp.bfloat16
F32 = jnp.float32


def outward():
    return [
        (k * N_SHARD + s, (s // 2) * N_SHARD + 2 * k + s % 2)
        for k in range(X * ZH * C)
        for s in range(N_SHARD)
    ]


def homeward():
    return [(there, here) for here, there in outward()]


def dot(a, b, dims):
    return lax.dot_general(a, b, (dims, ((), ())), preferred_element_type=F32)


def as_column(row):
    n = row.shape[1]
    eye = lax.broadcasted_iota(jnp.int32, (n, n), 0) == lax.broadcasted_iota(jnp.int32, (n, n), 1)
    return jnp.sum(jnp.where(eye, jnp.broadcast_to(row, (n, n)), 0), axis=1, keepdims=True)


def pick_kernel(tok_ref, cot_ref, slot_ref, gate_ref, live_ref, out_ref):
    tokens = tok_ref[...]
    cot = cot_ref[...]
    spot = lax.broadcasted_iota(jnp.int32, (R, 64), 1)
    row = lax.broadcasted_iota(jnp.int32, (R, 1), 0)
    lane = lax.broadcasted_iota(jnp.int32, (R, WIDE - HALF), 1)
    for e in range(2):
        one_hot = (as_column(slot_ref[e : e + 1, :]) == spot).astype(BF16)
        count = live_ref[e]
        scale = jnp.where(row < count, as_column(gate_ref[e : e + 1, :]), 0.0)
        picked = dot(one_hot, tokens, ((1,), (0,)))
        weighted = dot(one_hot, cot, ((1,), (0,))) * scale
        first = jnp.logical_and(lane == 0, row == 0)
        note = jnp.where(first, count.astype(F32), 0.0)
        blank = jnp.zeros_like(note)
        out_ref[e * R : (e + 1) * R, :] = jnp.concatenate([picked, note], axis=1).astype(BF16)
        out_ref[(2 + e) * R : (3 + e) * R, :] = jnp.concatenate([weighted, blank], axis=1).astype(
            BF16
        )


def both_halves(got_ref, half, m, e):
    at = (2 * m + e) * R
    parts = [got_ref[2 * half + h, :, at : at + R, :][:, :, :HALF] for h in range(2)]
    parts = [part.reshape(ZH * X * R, HALF) for part in parts]
    return jnp.concatenate(parts, axis=1)


def forward_kernel(core_ref, got_ref, gate_ref, up_ref, down_ref, send_ref, keep_ref):
    core = core_ref[0]
    for half, out_ref in ((1 - core, send_ref), (core, keep_ref)):
        for e in range(2):
            rows = both_halves(got_ref, half, 0, e)
            cot = both_halves(got_ref, half, 1, e)
            parts = (
                dot(rows, gate_ref[e], ((1,), (0,))),
                dot(rows, up_ref[e], ((1,), (0,))),
                dot(cot, down_ref[e], ((1,), (1,))),
            )
            for t, part in enumerate(parts):
                out_ref[:, 2 * t + e] = part.astype(BF16).reshape(X, ZH * R, 512)


def back_kernel(core_ref, mine_ref, other_ref, gate_ref, up_ref, out_ref):
    core = core_ref[0]
    blank = jnp.zeros((ZH * X * R, WIDE - HALF), BF16)
    for half, in_ref in ((1 - core, other_ref), (core, mine_ref)):
        for e in range(2):
            grad_gate = in_ref[:, 2 + e].reshape(ZH * X * R, 512)
            grad_up = in_ref[:, 4 + e].reshape(ZH * X * R, 512)
            term = (
                dot(grad_gate, gate_ref[e], ((1,), (1,))) + dot(grad_up, up_ref[e], ((1,), (1,)))
            ).astype(BF16)
            for h in range(2):
                piece = jnp.concatenate([term[:, h * HALF : (h + 1) * HALF], blank], axis=1)
                out_ref[2 * half + h, :, e * R : (e + 1) * R, :] = piece.reshape(ZH * X, R, WIDE)


def weight_kernel(core_ref, got_ref, mine_ref, other_ref, gate_out, up_out, down_out):
    core = core_ref[0]
    for e in range(2):
        count = sum(
            jnp.sum(got_ref[2 * half, :, e * R : (e + 1) * R, :][:, :, HALF:].astype(F32))
            for half in range(2)
        )
        scale = 1.0 / jnp.full((1, 512), count, F32)
        rows = [both_halves(got_ref, half, 0, e) for half in (core, 1 - core)]
        cot = [both_halves(got_ref, half, 1, e) for half in (core, 1 - core)]
        rows = jnp.concatenate(rows, axis=0)
        cot = jnp.concatenate(cot, axis=0)

        def whole(t):
            return jnp.concatenate(
                [ref[:, 2 * t + e].reshape(ZH * X * R, 512) for ref in (mine_ref, other_ref)], axis=0
            )

        gate_out[e] = (dot(rows, whole(1), ((0,), (0,))) * scale).astype(BF16)
        up_out[e] = (dot(rows, whole(2), ((0,), (0,))) * scale).astype(BF16)
        down_out[e] = (dot(whole(0), cot, ((0,), (0,))) * scale[:, :384]).astype(BF16)


def place_kernel(rows_ref, slot_ref, out_ref):
    spot = lax.broadcasted_iota(jnp.int32, (64, R), 0)
    total = jnp.zeros((64, HALF), F32)
    for e in range(2):
        one_hot = (spot == slot_ref[e : e + 1, :]).astype(BF16)
        total = total + dot(one_hot, rows_ref[e * R : (e + 1) * R, :][:, :HALF], ((1,), (0,)))
    out_ref[...] = total.astype(BF16)


VM = pl.BlockSpec(memory_space=pltpu.VMEM)
SM = pl.BlockSpec(memory_space=pltpu.SMEM)


def local(kernel, specs, outs, name):
    shapes = [jax.ShapeDtypeStruct(o, BF16) for o in outs]
    return pl.pallas_call(
        kernel,
        in_specs=specs,
        out_specs=[VM] * len(outs),
        out_shape=shapes,
        name=name,
    )


def on_device(
    tokens, cotangent, gate_proj, up_proj, down_proj, slot_tokens, gate_weights, live_counts
):
    core = lax.axis_index("c").astype(jnp.int32).reshape(1)
    (message,) = local(pick_kernel, [VM, VM, VM, VM, SM], [(64, WIDE)], "pick")(
        tokens, cotangent, slot_tokens, gate_weights, live_counts.reshape(2)
    )
    message = lax.ppermute(message, EVERY, outward())
    copies = jnp.broadcast_to(message[None], (ZL, 64, WIDE))
    column = lax.all_to_all(copies, "zl", 0, 0, tiled=True)
    got = lax.all_gather(column, "y", axis=0, tiled=False)

    stage = (X, 6, ZH * R, 512)
    send, keep = local(forward_kernel, [SM, VM, VM, VM, VM], [stage, stage], "forward")(
        core, got, gate_proj, up_proj, down_proj
    )
    swap = [(0, 1), (1, 0)]
    heard = lax.ppermute(send, "c", swap)
    paired = (keep.astype(F32) + heard.astype(F32)).astype(BF16)
    over_x = lax.all_to_all(paired, "x", 0, 0, tiled=True)
    over_x = jnp.sum(over_x.astype(F32), axis=0).astype(BF16)
    over_zh = lax.all_gather(over_x, "zh", axis=0, tiled=False)
    sums = jnp.sum(over_zh.astype(F32), axis=0)
    gate_sum, up_sum, cot_hidden = sums[0:2], sums[2:4], sums[4:6]
    sigmoid_part = jax.nn.sigmoid(gate_sum)
    hidden = gate_sum * sigmoid_part * up_sum
    grad_gate = cot_hidden * up_sum * sigmoid_part * (1.0 + gate_sum * (1.0 - sigmoid_part))
    grad_up = cot_hidden * gate_sum * sigmoid_part
    acts = jnp.concatenate([hidden, grad_gate, grad_up], axis=0).astype(BF16)
    mine = lax.all_gather(acts, "x", axis=0, tiled=False)
    other = lax.ppermute(mine, "c", swap)

    (back,) = local(back_kernel, [SM, VM, VM, VM, VM], [(C * 2, X * ZH, 2 * R, WIDE)], "back")(
        core, mine, other, gate_proj, up_proj
    )
    over_y = lax.all_to_all(back, "y", 0, 0, tiled=True)
    over_y = jnp.sum(over_y.astype(F32), axis=0).astype(BF16)
    over_zl = lax.all_to_all(over_y, "zl", 0, 0, tiled=True)
    over_zl = jnp.sum(over_zl.astype(F32), axis=0).astype(BF16)
    home = lax.ppermute(over_zl, EVERY, homeward())
    grad_gate_proj, grad_up_proj, grad_down_proj = local(
        weight_kernel,
        [SM, VM, VM, VM],
        [gate_proj.shape, up_proj.shape, down_proj.shape],
        "weights",
    )(core, got, mine, other)
    (grad_tokens,) = local(place_kernel, [VM, VM], [tokens.shape], "place")(home, slot_tokens)
    return (grad_tokens, grad_gate_proj, grad_up_proj, grad_down_proj)


def solution(mesh):
    fine = Mesh(mesh.devices.reshape(X, ZH, C, ZL, Y), EVERY)
    in_specs = (
        P(DP, SHARD),
        P(DP, SHARD),
        P(None, DP, SHARD),
        P(None, DP, SHARD),
        P(None, SHARD, DP),
        P(None, DP),
        P(None, DP),
        P(None, DP),
    )
    out_specs = (
        P(DP, SHARD),
        P(None, DP, SHARD),
        P(None, DP, SHARD),
        P(None, SHARD, DP),
    )
    return jax.shard_map(
        on_device, mesh=fine, in_specs=in_specs, out_specs=out_specs, check_vma=False
    )
```

time: 495 us -> 214 us (0.43)
  waiting for transfers between devices: 218 us -> 40 us
  blocking collectives: 190 us -> 117 us
  local copies, waits for them, and re-layouts: 38.6 us -> 1.51 us
  Pallas kernels: 0 us -> 15.2 us
  matrix products: 8.31 us -> 0 us
    reduce_scatter x1 -> x0, waiting for transfers between devices: 106 us -> none  [sent_together(): lax.psum_scatter(both, axis, scatter_dimension=dim, tiled=True)]
    all_gather x1 -> x2, blocking collectives: 113 us -> 37.1 us  [the longest x1 22.7 us: on_device(): over_zh = lax.all_gather(over_x, 'zh', axis=0, tiled=False)]
    all_gather x1, waiting for transfers between devices: 76.3 us -> 29.7 us  [on_device(): got = lax.all_gather(column, 'y', axis=0, tiled=False)]
    all_to_all x2 -> x0, waiting for transfers between devices: 36 us -> none  [the longest x1 24.6 us: summed_on_arrival(): tiles = lax.all_to_all(cut_along(array, dim, count), axis, 0, 0, tiled=True)]
    ppermute x0 -> x4, starting transfers between devices: none -> 23.9 us  [the longest x1 14.4 us: on_device(): message = lax.ppermute(message, EVERY, outward())]
    all_to_all x2 -> x0, starting transfers between devices: 19.6 us -> none  [the longest x1 16.1 us: summed_on_arrival(): tiles = lax.all_to_all(cut_along(array, dim, count), axis, 0, 0, tiled=True)]
    unnamed x19 -> x6, local copies, waits for them, and re-layouts: 17.8 us -> 1.49 us
    pallas_call x0 -> x5, Pallas kernels: none -> 15.2 us  [the longest x1 4.28 us: on_device(): local(weight_kernel, [SM, VM, VM, VM], [gate_proj.shape, up_proj.shape, d...]
  transfers between devices with their start and end apart: 4 -> 5, of which waited for: 4 -> 5; matrix products, arithmetic and copies ran while one was open for 1% -> 0% of each run, Pallas kernels for 0% -> 2%
where the time goes in v1:
time: 214 us
  blocking collectives  117 us (55%)
  waiting for transfers between devices  40 us (19%)
  starting transfers between devices  23.9 us (11%)
  Pallas kernels  15.2 us (7%)
  between operations  14.1 us (7%)
    all_gather x1, waiting for transfers between devices, on_device(): got = lax.all_gather(column, 'y', axis=0, tiled=False)  29.7 us
    all_to_all x1, blocking collectives, on_device(): column = lax.all_to_all(copies, 'zl', 0, 0, tiled=True)  25.8 us
    all_to_all x1, blocking collectives, on_device(): over_zl = lax.all_to_all(over_y, 'zl', 0, 0, tiled=True)  24.2 us
    all_gather x1, blocking collectives, on_device(): over_zh = lax.all_gather(over_x, 'zh', axis=0, tiled=False)  22.7 us
    all_to_all x1, blocking collectives, on_device(): over_x = lax.all_to_all(paired, 'x', 0, 0, tiled=True)  16.6 us
    ppermute x1, starting transfers between devices, on_device(): message = lax.ppermute(message, EVERY, outward())  14.4 us
    all_gather x1, blocking collectives, on_device(): mine = lax.all_gather(acts, 'x', axis=0, tiled=False)  14.3 us
    all_to_all x1, blocking collectives, on_device(): over_y = lax.all_to_all(back, 'y', 0, 0, tiled=True)  13.5 us
  transfers between devices with their start and end apart: 5, of which 5 were waited for; matrix products, arithmetic and copies ran while one was open for 0% of the time, Pallas kernels for 2%

profile of v1, /device:TPU:32, one launch (start us, length us, event | category | flops | bytes accessed | tf_op | source)
XLA Modules:
  0.0 213.7 jit_solution(8119441508730291428)
XLA Ops:
  7.2 0.0 all-gather.4.cloned.1.call-start
  7.2 1.6 pick.1
  8.8 14.4 %collective-permute-start = (bf16[64,256]{1,0:T(8,128)(2,1)}, bf16[64,256]{1,0:T(8,128)(2,1)S(1)}, u32[]{:S(2)}, u32[]{:S(2)}) collective-permute-start(bf16[64,256]{1,0:T(8,128)(2,1)} %pick.1), channel_id=1, source_target_pairs={{0,0},{1,1},{2,32},{3,33},{4,64},{5,65},{6,96},{7,97},{8,128},{9,1... | collective-permute-start | bytes 98312 | tf_op jit(solution)/shard_map/ppermute | solution.py:154
  23.2 2.1 collective-permute-done
  25.3 25.8 %all_to_all.20 = bf16[8,64,256]{2,1,0:T(8,128)(2,1)} all-to-all(bf16[8,64,256]{2,1,0:T(8,128)(2,1)S(1)} %broadcast_in_dim.2), channel_id=1, replica_groups=mesh['x'=4,'zh'=2,'c'=2,'zl'=8,'y'=4] {'zl'}, dimensions={0} | all-to-all | bytes 524288 | tf_op jit(solution)/shard_map/all_to_all | solution.py:156
  51.1 0.0 all-gather.4.cloned.1.call-update
  51.1 29.7 %all-gather.4.cloned.1.call-done = bf16[32,64,256]{2,1,0:T(8,128)(2,1)} async-done(((bf16[8,64,256]{2,1,0:T(8,128)(2,1)}), bf16[32,64,256]{2,1,0:T(8,128)(2,1)}) %all-gather.4.cloned.1.call-update) | async-done | bytes 1048592 | tf_op jit(solution)/shard_map/all_gather | solution.py:157
  80.8 4.0 %forward.1 = (bf16[4,6,32,512]{3,2,1,0:T(8,128)(2,1)}, bf16[4,6,32,512]{3,2,1,0:T(8,128)(2,1)}) custom-call(s32[1]{0:T(128)} %bitcast.core_ref, bf16[4,8,64,256]{3,2,1,0:T(8,128)(2,1)} %bitcast.11, bf16[2,384,512]{2,1,0:T(8,128)(2,1)} %gate_ref.5, bf16[2,384,512]{2,1,0:T(8,128)(2,1)} %up_ref.3, bf16[2,512,384]{2,1,0:T(8,128)(2,1)} %down_ref.1), custom_call_target="tpu_custom_call" | custom-call | tf_op jit(solution)/shard_map/forward/pallas_call | solution.py:160
  84.9 1.9 collective-permute-start.1
  86.8 2.5 %collective-permute-done.1 = bf16[4,6,32,512]{3,2,1,0:T(8,128)(2,1)S(1)} collective-permute-done((bf16[4,6,32,512]{3,2,1,0:T(8,128)(2,1)}, bf16[4,6,32,512]{3,2,1,0:T(8,128)(2,1)S(1)}, u32[]{:S(2)}, u32[]{:S(2)}) %collective-permute-start.1) | collective-permute-done | bytes 786464 | tf_op jit(solution)/shard_map/ppermute | solution.py:164
  89.3 1.4 add_convert_fusion
  90.7 16.6 %all_to_all.21 = bf16[4,6,32,512]{3,2,1,0:T(8,128)(2,1)S(1)} all-to-all(bf16[4,6,32,512]{3,2,1,0:T(8,128)(2,1)S(1)} %add_convert_fusion), channel_id=1, replica_groups=mesh['x'=4,'zh'=2,'c'=2,'zl'=8,'y'=4] {'x'}, dimensions={0} | all-to-all | bytes 1572864 | tf_op jit(solution)/shard_map/all_to_all | solution.py:166
  107.3 0.1 reduce_sum.45
  107.4 22.7 %all-gather.1 = bf16[12,32,512]{2,1,0:T(8,128)(2,1)S(1)} all-gather(bf16[6,32,512]{2,1,0:T(8,128)(2,1)S(1)} %reduce_sum.45), channel_id=3, replica_groups=mesh['x'=4,'zh'=2,'c'=2,'zl'=8,'y'=4] {'zh'}, dimensions={0}, use_global_device_ids=true | all-gather | bytes 589824 | tf_op jit(solution)/shard_map/all_gather | solution.py:168
  130.2 0.1 convert_reduce_fusion
  130.2 0.1 fusion
  130.4 14.3 %all_gather.20.mine_ref = bf16[4,6,32,512]{3,2,1,0:T(8,128)(2,1)S(1)} all-gather(bf16[1,6,32,512]{3,2,1,0:T(8,128)(2,1)S(1)} %pad_maximum_fusion), channel_id=1, replica_groups=mesh['x'=4,'zh'=2,'c'=2,'zl'=8,'y'=4] {'x'}, dimensions={0}, use_global_device_ids=true | all-gather | bytes 983040 | tf_op jit(solution)/shard_map/all_gather | solution.py:176
  144.7 0.0 copy-start
  144.7 1.9 collective-permute-start.2
  146.6 2.3 %collective-permute-done.2.other_ref = bf16[4,6,32,512]{3,2,1,0:T(8,128)(2,1)S(1)} collective-permute-done((bf16[4,6,32,512]{3,2,1,0:T(8,128)(2,1)S(1)}, bf16[4,6,32,512]{3,2,1,0:T(8,128)(2,1)S(1)}, u32[]{:S(2)}, u32[]{:S(2)}) %collective-permute-start.2) | collective-permute-done | bytes 786464 | tf_op jit(solution)/shard_map/ppermute | solution.py:177
  148.8 0.0 copy-done
  148.8 0.0 copy-start.1
  148.9 0.9 copy-done.1
  149.7 3.7 %back.1 = bf16[4,8,32,256]{3,2,1,0:T(8,128)(2,1)} custom-call(s32[1]{0:T(128)} %bitcast.core_ref, bf16[4,6,32,512]{3,2,1,0:T(8,128)(2,1)} %copy-done, bf16[4,6,32,512]{3,2,1,0:T(8,128)(2,1)} %copy-done.1, bf16[2,384,512]{2,1,0:T(8,128)(2,1)} %gate_ref.5, bf16[2,384,512]{2,1,0:T(8,128)(2,1)} %up_ref.3), custom_call_target="tpu_custom_call" | custom-call | tf_op jit(solution)/shard_map/back/pallas_call | solution.py:179
  153.5 13.5 %all_to_all.22 = bf16[4,8,32,256]{3,2,1,0:T(8,128)(2,1)S(1)} all-to-all(bf16[4,8,32,256]{3,2,1,0:T(8,128)(2,1)} %back.1), channel_id=1, replica_groups=mesh['x'=4,'zh'=2,'c'=2,'zl'=8,'y'=4] {'y'}, dimensions={0} | all-to-all | bytes 1048576 | tf_op jit(solution)/shard_map/all_to_all | solution.py:182
  167.0 0.1 reduce_sum.47
  167.1 24.2 %all_to_all.23 = bf16[8,32,256]{2,1,0:T(8,128)(2,1)S(1)} all-to-all(bf16[8,32,256]{2,1,0:T(8,128)(2,1)S(1)} %reduce_sum.47), channel_id=1, replica_groups=mesh['x'=4,'zh'=2,'c'=2,'zl'=8,'y'=4] {'zl'}, dimensions={0} | all-to-all | bytes 262144 | tf_op jit(solution)/shard_map/all_to_all | solution.py:184
  191.3 5.7 %collective-permute-start.3 = (bf16[32,256]{1,0:T(8,128)(2,1)S(1)}, bf16[32,256]{1,0:T(8,128)(2,1)S(1)}, u32[]{:S(2)}, u32[]{:S(2)}) collective-permute-start(bf16[32,256]{1,0:T(8,128)(2,1)S(1)} %reduce_sum.48), channel_id=1, source_target_pairs={{0,0},{1,1},{32,2},{33,3},{64,4},{65,5},{96,6},{97,7},{128,8},{129... | collective-permute-start | bytes 49160 | tf_op jit(solution)/shard_map/ppermute | solution.py:186
  197.1 4.3 %weights.1 = (bf16[2,384,512]{2,1,0:T(8,128)(2,1)}, bf16[2,384,512]{2,1,0:T(8,128)(2,1)}, bf16[2,512,384]{2,1,0:T(8,128)(2,1)}) custom-call(s32[1]{0:T(128)} %bitcast.core_ref, bf16[4,8,64,256]{3,2,1,0:T(8,128)(2,1)} %bitcast.12, bf16[4,6,32,512]{3,2,1,0:T(8,128)(2,1)} %copy-done, bf16[4,6,32,512]{3,2,1,0:T(8,128)(2,1)} %copy-done.1), custom_call_target="tpu_custom_call" | custom-call | tf_op jit(solution)/shard_map/weights/pallas_call | solution.py:187
  201.3 3.4 %collective-permute-done.3.rows_ref = bf16[32,256]{1,0:T(8,128)(2,1)S(1)} collective-permute-done((bf16[32,256]{1,0:T(8,128)(2,1)S(1)}, bf16[32,256]{1,0:T(8,128)(2,1)S(1)}, u32[]{:S(2)}, u32[]{:S(2)}) %collective-permute-start.3) | collective-permute-done | bytes 16416 | tf_op jit(solution)/shard_map/ppermute | solution.py:186
  204.8 0.0 copy-start.2
  204.8 0.6 copy-done.2
  205.4 1.5 place.1
  (3 shorter events, 0.1 us)
Async XLA Ops:
  7.2 73.7 %all-gather.4.cloned.1.call-start = ((), (), s32[]{:S(2)}) async-start(), calls=%async_computation.4 | async-start | bytes 1310720 | tf_op jit(solution)/shard_map/all_gather | solution.py:157
  8.8 16.5 %collective-permute-start = (bf16[64,256]{1,0:T(8,128)(2,1)}, bf16[64,256]{1,0:T(8,128)(2,1)S(1)}, u32[]{:S(2)}, u32[]{:S(2)}) collective-permute-start(bf16[64,256]{1,0:T(8,128)(2,1)} %pick.1), channel_id=1, source_target_pairs={{0,0},{1,1},{2,32},{3,33},{4,64},{5,65},{6,96},{7,97},{8,128},{9,1... | collective-permute-start | bytes 98312 | tf_op jit(solution)/shard_map/ppermute | solution.py:154
  84.9 4.4 %collective-permute-start.1 = (bf16[4,6,32,512]{3,2,1,0:T(8,128)(2,1)}, bf16[4,6,32,512]{3,2,1,0:T(8,128)(2,1)S(1)}, u32[]{:S(2)}, u32[]{:S(2)}) collective-permute-start(bf16[4,6,32,512]{3,2,1,0:T(8,128)(2,1)} %get-tuple-element.10), channel_id=1, source_target_pairs={{0,32},{32,0},{1,33},{33,1},{2,34},{34,2},{3,35},{35,3},{4,36},{36... | collective-permute-start | bytes 2359304 | tf_op jit(solution)/shard_map/ppermute | solution.py:164
  144.7 4.2 %copy-start = (bf16[4,6,32,512]{3,2,1,0:T(8,128)(2,1)}, bf16[4,6,32,512]{3,2,1,0:T(8,128)(2,1)S(1)}, u32[]{:S(2)}) copy-start(bf16[4,6,32,512]{3,2,1,0:T(8,128)(2,1)S(1)} %all_gather.20.mine_ref) | copy-start | bytes 2359300
  144.7 4.2 %collective-permute-start.2 = (bf16[4,6,32,512]{3,2,1,0:T(8,128)(2,1)S(1)}, bf16[4,6,32,512]{3,2,1,0:T(8,128)(2,1)S(1)}, u32[]{:S(2)}, u32[]{:S(2)}) collective-permute-start(bf16[4,6,32,512]{3,2,1,0:T(8,128)(2,1)S(1)} %all_gather.20.mine_ref), channel_id=1, source_target_pairs={{0,32},{32,0},{1,33},{33,1},{2,34},{34,2},{3,35},{35,3},{4,36},{36... | collective-permute-start | bytes 2359304 | tf_op jit(solution)/shard_map/ppermute | solution.py:177
  148.8 0.9 copy-start.1
  191.3 13.4 %collective-permute-start.3 = (bf16[32,256]{1,0:T(8,128)(2,1)S(1)}, bf16[32,256]{1,0:T(8,128)(2,1)S(1)}, u32[]{:S(2)}, u32[]{:S(2)}) collective-permute-start(bf16[32,256]{1,0:T(8,128)(2,1)S(1)} %reduce_sum.48), channel_id=1, source_target_pairs={{0,0},{1,1},{32,2},{33,3},{64,4},{65,5},{96,6},{97,7},{128,8},{129... | collective-permute-start | bytes 49160 | tf_op jit(solution)/shard_map/ppermute | solution.py:186
  204.8 0.6 copy-start.2
Sparse Core Ops, SparseCore 0:
  51.2 29.5 all-gather.3

commit v2 on v1

v2 whole, which is shorter than its diff:
```python
import jax
import jax.numpy as jnp
from jax import lax
from jax.experimental import pallas as pl
from jax.experimental.pallas import tpu as pltpu
from jax.sharding import Mesh, PartitionSpec as P

X, ZH, C, ZL, Y = 4, 2, 2, 8, 4
DP = ("x", "zh", "c")
SHARD = ("zl", "y")
EVERY = DP + SHARD
N_SHARD = ZL * Y
HALF = 192
R = 16
PACK = 3 * R
MESSAGE = 2 * PACK + 8
BF16 = jnp.bfloat16
F32 = jnp.float32


def outward():
    return [
        (k * N_SHARD + s, (s // 2) * N_SHARD + 2 * k + s % 2)
        for k in range(X * ZH * C)
        for s in range(N_SHARD)
    ]


def homeward():
    return [(there, here) for here, there in outward()]


def dot(a, b, dims):
    return lax.dot_general(a, b, (dims, ((), ())), preferred_element_type=F32)


def as_column(row):
    n = row.shape[1]
    eye = lax.broadcasted_iota(jnp.int32, (n, n), 0) == lax.broadcasted_iota(jnp.int32, (n, n), 1)
    return jnp.sum(jnp.where(eye, jnp.broadcast_to(row, (n, n)), 0), axis=1, keepdims=True)


def pick_kernel(
    tok_hbm, cot_hbm, slot_hbm, gate_hbm, live_hbm, out_ref, tok, cot, slots, gates, live, sems
):
    moves = [
        pltpu.make_async_copy(source, target, sems.at[i])
        for i, (source, target) in enumerate(
            (
                (slot_hbm, slots),
                (gate_hbm, gates),
                (live_hbm, live),
                (tok_hbm, tok),
                (cot_hbm, cot),
            )
        )
    ]
    for move in moves:
        move.start()
    for move in moves:
        move.wait()
    spot = lax.broadcasted_iota(jnp.int32, (R, 64), 1)
    row = lax.broadcasted_iota(jnp.int32, (R, 1), 0)
    one_hot = [(as_column(slots[e : e + 1, :]) == spot).astype(BF16) for e in range(2)]
    scale = [jnp.where(row < live[e], as_column(gates[e : e + 1, :]), 0.0) for e in range(2)]
    for m, in_ref in enumerate((tok, cot)):
        values = in_ref[...]
        rows = [dot(one_hot[e], values, ((1,), (0,))) for e in range(2)]
        if m == 1:
            rows = [rows[e] * scale[e] for e in range(2)]
        out_ref[m * PACK : (m + 1) * PACK, :] = packed([part.astype(BF16) for part in rows])
    lane = lax.broadcasted_iota(jnp.int32, (8, 128), 1)
    line = lax.broadcasted_iota(jnp.int32, (8, 128), 0)
    note = jnp.where(lane == 0, live[0], 0) + jnp.where(lane == 64, live[1], 0)
    out_ref[2 * PACK :, :] = jnp.where(line == 0, note, 0).astype(F32).astype(BF16)


def packed(rows):
    left = jnp.concatenate([part[:, 128:] for part in rows], axis=1)
    return jnp.concatenate([part[:, :128] for part in rows] + [left], axis=0)


def features(got_ref, core, m, e):
    blocks = []
    for half in (core, 1 - core):
        parts = []
        for h in range(2):
            main = got_ref[2 * half + h, :, m * PACK + e * R : m * PACK + (e + 1) * R, :]
            left = got_ref[2 * half + h, :, m * PACK + 2 * R : (m + 1) * PACK, :]
            parts.append(main.reshape(ZH * X * R, 128))
            parts.append(left.reshape(ZH * X * R, 128)[:, e * 64 : (e + 1) * 64])
        blocks.append(jnp.concatenate(parts, axis=1))
    return jnp.concatenate(blocks, axis=0)


def forward_kernel(core_ref, got_ref, gate_ref, up_ref, down_ref, keep_ref, send_ref):
    core = core_ref[0]
    for e in range(2):
        rows = features(got_ref, core, 0, e)
        cot = features(got_ref, core, 1, e)
        parts = (
            dot(rows, gate_ref[e], ((1,), (0,))),
            dot(rows, up_ref[e], ((1,), (0,))),
            dot(cot, down_ref[e], ((1,), (1,))),
        )
        for t, part in enumerate(parts):
            part = part.astype(BF16).reshape(C, X, ZH * R, 512)
            keep_ref[:, 2 * t + e] = part[0]
            send_ref[:, 2 * t + e] = part[1]


def all_rows(mine_ref, other_ref, t, e):
    return jnp.concatenate(
        [ref[:, 2 * t + e].reshape(ZH * X * R, 512) for ref in (mine_ref, other_ref)], axis=0
    )


def back_kernel(core_ref, mine_ref, other_ref, gate_ref, up_ref, out_ref):
    core = core_ref[0]
    terms = []
    for e in range(2):
        grad_gate = all_rows(mine_ref, other_ref, 1, e)
        grad_up = all_rows(mine_ref, other_ref, 2, e)
        term = dot(grad_gate, gate_ref[e], ((1,), (1,))) + dot(grad_up, up_ref[e], ((1,), (1,)))
        terms.append(term.astype(BF16))
    for at, half in enumerate((core, 1 - core)):
        for h in range(2):
            rows = slice(at * ZH * X * R, (at + 1) * ZH * X * R)
            here = [term[rows, h * HALF : (h + 1) * HALF] for term in terms]
            for e in range(2):
                main = here[e][:, :128].reshape(ZH * X, R, 128)
                out_ref[2 * half + h, :, e * R : (e + 1) * R, :] = main
            left = jnp.concatenate([part[:, 128:] for part in here], axis=1)
            out_ref[2 * half + h, :, 2 * R :, :] = left.reshape(ZH * X, R, 128)


def weight_kernel(core_ref, got_ref, mine_ref, other_ref, gate_out, up_out, down_out):
    core = core_ref[0]
    for e in range(2):
        count = sum(
            jnp.sum(got_ref[2 * half, :, 2 * PACK :, :][:, :, e * 64 : (e + 1) * 64].astype(F32))
            for half in range(2)
        )
        scale = 1.0 / jnp.full((1, 512), count, F32)
        rows = features(got_ref, core, 0, e)
        cot = features(got_ref, core, 1, e)
        hidden, grad_gate, grad_up = (all_rows(mine_ref, other_ref, t, e) for t in range(3))
        gate_out[e] = (dot(rows, grad_gate, ((0,), (0,))) * scale).astype(BF16)
        up_out[e] = (dot(rows, grad_up, ((0,), (0,))) * scale).astype(BF16)
        down_out[e] = (dot(hidden, cot, ((0,), (0,))) * scale[:, :384]).astype(BF16)


def place_kernel(rows_ref, slot_ref, out_ref):
    spot = lax.broadcasted_iota(jnp.int32, (64, R), 0)
    total = jnp.zeros((64, HALF), F32)
    left = rows_ref[2 * R :, :]
    for e in range(2):
        one_hot = (spot == slot_ref[e : e + 1, :]).astype(BF16)
        rows = [rows_ref[e * R : (e + 1) * R, :], left[:, e * 64 : (e + 1) * 64]]
        total = total + dot(one_hot, jnp.concatenate(rows, axis=1), ((1,), (0,)))
    out_ref[...] = total.astype(BF16)


VM = pl.BlockSpec(memory_space=pltpu.VMEM)
SM = pl.BlockSpec(memory_space=pltpu.SMEM)
HB = pl.BlockSpec(memory_space=pltpu.HBM)


def in_vmem(x):
    return pltpu.with_memory_space_constraint(x, pltpu.VMEM)


def local(kernel, specs, outs, name, stay=True, scratch=()):
    if stay:
        shapes = [pltpu.VMEM(o, BF16) for o in outs]
    else:
        shapes = [jax.ShapeDtypeStruct(o, BF16) for o in outs]
    return pl.pallas_call(
        kernel,
        in_specs=specs,
        out_specs=[VM] * len(outs),
        out_shape=shapes,
        scratch_shapes=scratch,
        compiler_params=pltpu.CompilerParams(vmem_limit_bytes=16 << 20),
        name=name,
    )


def on_device(
    tokens, cotangent, gate_proj, up_proj, down_proj, slot_tokens, gate_weights, live_counts
):
    core = lax.axis_index("c").astype(jnp.int32).reshape(1)
    gate_proj, up_proj, down_proj = (in_vmem(w) for w in (gate_proj, up_proj, down_proj))
    scratch = [
        pltpu.VMEM(tokens.shape, BF16),
        pltpu.VMEM(cotangent.shape, BF16),
        pltpu.VMEM(slot_tokens.shape, jnp.int32),
        pltpu.VMEM(gate_weights.shape, F32),
        pltpu.SMEM((2,), jnp.int32),
        pltpu.SemaphoreType.DMA((5,)),
    ]
    (message,) = local(pick_kernel, [HB] * 5, [(MESSAGE, 128)], "pick", scratch=scratch)(
        *(
            pltpu.with_memory_space_constraint(a, pltpu.HBM)
            for a in (tokens, cotangent, slot_tokens, gate_weights, live_counts.reshape(2))
        )
    )
    message = lax.ppermute(message, EVERY, outward())
    copies = jnp.broadcast_to(message[None], (ZL, MESSAGE, 128))
    column = lax.all_to_all(copies, "zl", 0, 0, tiled=True)
    got = in_vmem(lax.all_gather(column, "y", axis=0, tiled=False))

    stage = (X, 6, ZH * R, 512)
    keep, send = local(forward_kernel, [SM, VM, VM, VM, VM], [stage, stage], "forward")(
        core, got, gate_proj, up_proj, down_proj
    )
    swap = [(0, 1), (1, 0)]
    heard = lax.ppermute(send, "c", swap)
    paired = (keep.astype(F32) + heard.astype(F32)).astype(BF16)
    over_x = lax.all_to_all(paired, "x", 0, 0, tiled=True)
    over_x = jnp.sum(over_x.astype(F32), axis=0).astype(BF16)
    over_zh = lax.all_gather(over_x, "zh", axis=0, tiled=False)
    sums = jnp.sum(over_zh.astype(F32), axis=0)
    gate_sum, up_sum, cot_hidden = sums[0:2], sums[2:4], sums[4:6]
    sigmoid_part = jax.nn.sigmoid(gate_sum)
    hidden = gate_sum * sigmoid_part * up_sum
    grad_gate = cot_hidden * up_sum * sigmoid_part * (1.0 + gate_sum * (1.0 - sigmoid_part))
    grad_up = cot_hidden * gate_sum * sigmoid_part
    acts = jnp.concatenate([hidden, grad_gate, grad_up], axis=0).astype(BF16)
    mine = lax.all_gather(acts, "x", axis=0, tiled=False)
    other = in_vmem(lax.ppermute(mine, "c", swap))
    mine = in_vmem(mine)

    (back,) = local(back_kernel, [SM, VM, VM, VM, VM], [(C * 2, X * ZH, PACK, 128)], "back")(
        core, mine, other, gate_proj, up_proj
    )
    over_y = lax.all_to_all(back, "y", 0, 0, tiled=True)
    over_y = jnp.sum(over_y.astype(F32), axis=0).astype(BF16)
    over_zl = lax.all_to_all(over_y, "zl", 0, 0, tiled=True)
    over_zl = jnp.sum(over_zl.astype(F32), axis=0).astype(BF16)
    home = in_vmem(lax.ppermute(over_zl, EVERY, homeward()))
    grad_gate_proj, grad_up_proj, grad_down_proj = local(
        weight_kernel,
        [SM, VM, VM, VM],
        [gate_proj.shape, up_proj.shape, down_proj.shape],
        "weights",
        False,
    )(core, got, mine, other)
    (grad_tokens,) = local(place_kernel, [VM, VM], [tokens.shape], "place", False)(
        home, slot_tokens
    )
    return (grad_tokens, grad_gate_proj, grad_up_proj, grad_down_proj)


def solution(mesh):
    fine = Mesh(mesh.devices.reshape(X, ZH, C, ZL, Y), EVERY)
    in_specs = (
        P(DP, SHARD),
        P(DP, SHARD),
        P(None, DP, SHARD),
        P(None, DP, SHARD),
        P(None, SHARD, DP),
        P(None, DP),
        P(None, DP),
        P(None, DP),
    )
    out_specs = (
        P(DP, SHARD),
        P(None, DP, SHARD),
        P(None, DP, SHARD),
        P(None, SHARD, DP),
    )
    return jax.shard_map(
        on_device, mesh=fine, in_specs=in_specs, out_specs=out_specs, check_vma=False
    )
```

time: 214 us -> 167 us (0.78)
  blocking collectives: 117 us -> 97.3 us
  waiting for transfers between devices: 40 us -> 23.1 us
  between operations: 14.1 us -> 0.77 us
  starting transfers between devices: 23.9 us -> 36.4 us
  Pallas kernels: 15.2 us -> 6.25 us
    all_gather x1 -> x0, waiting for transfers between devices: 29.7 us -> none  [on_device(): got = lax.all_gather(column, 'y', axis=0, tiled=False)]
    all_to_all x1 -> x0, blocking collectives: 25.8 us -> none  [on_device(): column = lax.all_to_all(copies, 'zl', 0, 0, tiled=True)]
    all_to_all x0 -> x1, waiting for transfers between devices: none -> 15.3 us  [on_device(): column = lax.all_to_all(copies, 'zl', 0, 0, tiled=True)]
    all_gather x0 -> x1, blocking collectives: none -> 14.5 us  [on_device(): got = in_vmem(lax.all_gather(column, 'y', axis=0, tiled=False))]
    all_to_all x1, blocking collectives: 24.2 us -> 13.4 us  [on_device(): over_zl = lax.all_to_all(over_y, 'zl', 0, 0, tiled=True)]
    all_to_all x0 -> x1, starting transfers between devices: none -> 8.64 us  [on_device(): column = lax.all_to_all(copies, 'zl', 0, 0, tiled=True)]
    pallas_call x3, Pallas kernels: 6.85 us -> 2.74 us  [the longest x1 1.13 us: on_device(): local(pick_kernel, [HB] * 5, [(MESSAGE, 128)], 'pick', scratch=scratch)]
    all_gather x1, blocking collectives: 22.7 us -> 26.5 us  [on_device(): over_zh = lax.all_gather(over_x, 'zh', axis=0, tiled=False)]
where the time goes in v2:
time: 167 us; the launch traced here: 166 us
  blocking collectives  97.3 us (58%)
  starting transfers between devices  36.4 us (22%)
  waiting for transfers between devices  23.1 us (14%)
  Pallas kernels  6.25 us (4%)
  local copies, waits for them, and re-layouts  1.95 us (1%)
    all_gather x1, blocking collectives, on_device(): over_zh = lax.all_gather(over_x, 'zh', axis=0, tiled=False)  26.5 us
    all_to_all x1, blocking collectives, on_device(): over_x = lax.all_to_all(paired, 'x', 0, 0, tiled=True)  17.8 us
    all_to_all x1, waiting for transfers between devices, on_device(): column = lax.all_to_all(copies, 'zl', 0, 0, tiled=True)  15.3 us
    ppermute x1, starting transfers between devices, on_device(): message = lax.ppermute(message, EVERY, outward())  14.5 us
    all_gather x1, blocking collectives, on_device(): got = in_vmem(lax.all_gather(column, 'y', axis=0, tiled=False))  14.5 us
    all_gather x1, blocking collectives, on_device(): mine = lax.all_gather(acts, 'x', axis=0, tiled=False)  14.2 us
    all_to_all x1, blocking collectives, on_device(): over_zl = lax.all_to_all(over_y, 'zl', 0, 0, tiled=True)  13.4 us
    all_to_all x1, blocking collectives, on_device(): over_y = lax.all_to_all(back, 'y', 0, 0, tiled=True)  11 us
  transfers between devices with their start and end apart: 5, of which 5 were waited for; matrix products, arithmetic and copies ran while one was open for 0% of the time, Pallas kernels for 2%

profile of v2, /device:TPU:32, one launch (start us, length us, event | category | flops | bytes accessed | tf_op | source)
XLA Modules:
  0.0 166.4 jit_solution(14432573312759097847)
XLA Ops:
  0.6 1.1 pick.1
  1.8 0.0 copy-start
  1.8 0.0 copy-start.1
  1.8 14.5 %collective-permute-start = (bf16[104,128]{1,0:T(8,128)(2,1)S(1)}, bf16[104,128]{1,0:T(8,128)(2,1)S(1)}, u32[]{:S(2)}, u32[]{:S(2)}) collective-permute-start(bf16[104,128]{1,0:T(8,128)(2,1)S(1)} %pick.1), channel_id=1, source_target_pairs={{0,0},{1,1},{2,32},{3,33},{4,64},{5,65},{6,96},{7,97},{8,128},{9,1... | collective-permute-start | bytes 79880 | tf_op jit(solution)/shard_map/ppermute | solution.py:208
  16.3 1.8 %collective-permute-done = bf16[104,128]{1,0:T(8,128)(2,1)S(1)} collective-permute-done((bf16[104,128]{1,0:T(8,128)(2,1)S(1)}, bf16[104,128]{1,0:T(8,128)(2,1)S(1)}, u32[]{:S(2)}, u32[]{:S(2)}) %collective-permute-start) | collective-permute-done | bytes 26656 | tf_op jit(solution)/shard_map/ppermute | solution.py:208
  18.1 0.7 broadcast_in_dim.2
  18.8 8.6 %all-to-all-start = ((bf16[8,104,128]{2,1,0:T(8,128)(2,1)}), bf16[8,104,128]{2,1,0:T(8,128)(2,1)S(1)}, u32[]{:S(2)}, u32[]{:S(2)}) async-start(bf16[8,104,128]{2,1,0:T(8,128)(2,1)} %broadcast_in_dim.2), calls=%async_computation | async-start | bytes 425984 | tf_op jit(solution)/shard_map/all_to_all | solution.py:210
  27.5 15.3 %all-to-all-done = bf16[8,104,128]{2,1,0:T(8,128)(2,1)S(1)} async-done(((bf16[8,104,128]{2,1,0:T(8,128)(2,1)}), bf16[8,104,128]{2,1,0:T(8,128)(2,1)S(1)}, u32[]{:S(2)}, u32[]{:S(2)}) %all-to-all-start) | async-done | bytes 213024 | tf_op jit(solution)/shard_map/all_to_all | solution.py:210
  42.7 14.5 %all-gather = bf16[32,104,128]{2,1,0:T(8,128)(2,1)S(1)} all-gather(bf16[8,104,128]{2,1,0:T(8,128)(2,1)S(1)} %all-to-all-done), channel_id=2, replica_groups=mesh['x'=4,'zh'=2,'c'=2,'zl'=8,'y'=4] {'y'}, dimensions={0}, use_global_device_ids=true | all-gather | bytes 1064960 | tf_op jit(solution)/shard_map/all_gather | solution.py:211
  57.2 0.0 copy-done
  57.2 0.0 copy-done.1
  57.2 0.0 copy-start.4
  57.2 1.1 copy-done.4
  58.3 1.0 forward.1
  59.4 1.9 %collective-permute-start.1 = (bf16[4,6,32,512]{3,2,1,0:T(8,128)(2,1)S(1)}, bf16[4,6,32,512]{3,2,1,0:T(8,128)(2,1)S(1)}, u32[]{:S(2)}, u32[]{:S(2)}) collective-permute-start(bf16[4,6,32,512]{3,2,1,0:T(8,128)(2,1)S(1)} %get-tuple-element.10), channel_id=1, source_target_pairs={{0,32},{32,0},{1,33},{33,1},{2,34},{34,2},{3,35},{35,3},{4,36},{36... | collective-permute-start | bytes 2359304 | tf_op jit(solution)/shard_map/ppermute | solution.py:218
  61.3 2.3 %collective-permute-done.1 = bf16[4,6,32,512]{3,2,1,0:T(8,128)(2,1)S(1)} collective-permute-done((bf16[4,6,32,512]{3,2,1,0:T(8,128)(2,1)S(1)}, bf16[4,6,32,512]{3,2,1,0:T(8,128)(2,1)S(1)}, u32[]{:S(2)}, u32[]{:S(2)}) %collective-permute-start.1) | collective-permute-done | bytes 786464 | tf_op jit(solution)/shard_map/ppermute | solution.py:218
  63.5 0.3 add_convert_fusion
  63.8 17.8 %all_to_all.20 = bf16[4,6,32,512]{3,2,1,0:T(8,128)(2,1)S(1)} all-to-all(bf16[4,6,32,512]{3,2,1,0:T(8,128)(2,1)S(1)} %add_convert_fusion), channel_id=1, replica_groups=mesh['x'=4,'zh'=2,'c'=2,'zl'=8,'y'=4] {'x'}, dimensions={0} | all-to-all | bytes 1572864 | tf_op jit(solution)/shard_map/all_to_all | solution.py:220
  81.6 0.1 reduce_sum.45
  81.7 26.5 %all-gather.1 = bf16[12,32,512]{2,1,0:T(8,128)(2,1)S(1)} all-gather(bf16[6,32,512]{2,1,0:T(8,128)(2,1)S(1)} %reduce_sum.45), channel_id=3, replica_groups=mesh['x'=4,'zh'=2,'c'=2,'zl'=8,'y'=4] {'zh'}, dimensions={0}, use_global_device_ids=true | all-gather | bytes 589824 | tf_op jit(solution)/shard_map/all_gather | solution.py:222
  108.2 0.1 convert_reduce_fusion
  108.3 0.1 fusion
  108.4 14.2 %all_gather.20.mine_ref = bf16[4,6,32,512]{3,2,1,0:T(8,128)(2,1)S(1)} all-gather(bf16[1,6,32,512]{3,2,1,0:T(8,128)(2,1)S(1)} %pad_maximum_fusion), channel_id=1, replica_groups=mesh['x'=4,'zh'=2,'c'=2,'zl'=8,'y'=4] {'x'}, dimensions={0}, use_global_device_ids=true | all-gather | bytes 983040 | tf_op jit(solution)/shard_map/all_gather | solution.py:230
  122.6 1.9 %collective-permute-start.2 = (bf16[4,6,32,512]{3,2,1,0:T(8,128)(2,1)S(1)}, bf16[4,6,32,512]{3,2,1,0:T(8,128)(2,1)S(1)}, u32[]{:S(2)}, u32[]{:S(2)}) collective-permute-start(bf16[4,6,32,512]{3,2,1,0:T(8,128)(2,1)S(1)} %all_gather.20.mine_ref), channel_id=1, source_target_pairs={{0,32},{32,0},{1,33},{33,1},{2,34},{34,2},{3,35},{35,3},{4,36},{36... | collective-permute-start | bytes 2359304 | tf_op jit(solution)/shard_map/ppermute | solution.py:231
  124.5 2.3 %collective-permute-done.2.other_ref = bf16[4,6,32,512]{3,2,1,0:T(8,128)(2,1)S(1)} collective-permute-done((bf16[4,6,32,512]{3,2,1,0:T(8,128)(2,1)S(1)}, bf16[4,6,32,512]{3,2,1,0:T(8,128)(2,1)S(1)}, u32[]{:S(2)}, u32[]{:S(2)}) %collective-permute-start.2) | collective-permute-done | bytes 786464 | tf_op jit(solution)/shard_map/ppermute | solution.py:231
  126.8 0.0 copy-start.2
  126.8 0.8 back.1
  127.6 0.1 copy-done.2
  127.6 11.0 %all_to_all.21 = bf16[4,8,48,128]{3,2,1,0:T(8,128)(2,1)S(1)} all-to-all(bf16[4,8,48,128]{3,2,1,0:T(8,128)(2,1)S(1)} %back.1), channel_id=1, replica_groups=mesh['x'=4,'zh'=2,'c'=2,'zl'=8,'y'=4] {'y'}, dimensions={0} | all-to-all | bytes 786432 | tf_op jit(solution)/shard_map/all_to_all | solution.py:237
  138.7 0.0 copy-start.3
  138.7 0.1 reduce_sum.47
  138.7 13.4 %all_to_all.22 = bf16[8,48,128]{2,1,0:T(8,128)(2,1)S(1)} all-to-all(bf16[8,48,128]{2,1,0:T(8,128)(2,1)S(1)} %reduce_sum.47), channel_id=1, replica_groups=mesh['x'=4,'zh'=2,'c'=2,'zl'=8,'y'=4] {'zl'}, dimensions={0} | all-to-all | bytes 196608 | tf_op jit(solution)/shard_map/all_to_all | solution.py:239
  152.1 0.0 copy-start.5
  152.2 9.4 %collective-permute-start.3 = (bf16[48,128]{1,0:T(8,128)(2,1)S(1)}, bf16[48,128]{1,0:T(8,128)(2,1)S(1)}, u32[]{:S(2)}, u32[]{:S(2)}) collective-permute-start(bf16[48,128]{1,0:T(8,128)(2,1)S(1)} %reduce_sum.48), channel_id=1, source_target_pairs={{0,0},{1,1},{32,2},{33,3},{64,4},{65,5},{96,6},{97,7},{128,8},{129... | collective-permute-start | bytes 36872 | tf_op jit(solution)/shard_map/ppermute | solution.py:241
  161.5 0.0 copy-done.3
  161.6 2.5 %weights.1 = (bf16[2,384,512]{2,1,0:T(8,128)(2,1)}, bf16[2,384,512]{2,1,0:T(8,128)(2,1)}, bf16[2,512,384]{2,1,0:T(8,128)(2,1)}) custom-call(s32[1]{0:T(128)} %bitcast.core_ref, bf16[4,8,104,128]{3,2,1,0:T(8,128)(2,1)S(1)} %bitcast.12, bf16[4,6,32,512]{3,2,1,0:T(8,128)(2,1)S(1)} %all_gather.20.mine_ref, bf16[4,6,32,512]{3,2,1,0:T(8,128)(2,1)S(1)} %copy-done.3), custom_call_target="tpu_custom_call" | custom-call | tf_op jit(solution)/shard_map/weights/pallas_call | solution.py:242
  164.1 1.5 collective-permute-done.3.rows_ref
  165.6 0.0 copy-done.5
  165.6 0.8 place.1
  (2 shorter events, 0.0 us)
Async XLA Ops:
  1.8 55.4 %copy-start = (bf16[2,384,512]{2,1,0:T(8,128)(2,1)S(1)}, bf16[2,384,512]{2,1,0:T(8,128)(2,1)}, u32[]{:S(2)}) copy-start(bf16[2,384,512]{2,1,0:T(8,128)(2,1)} %gate_ref.3) | copy-start | bytes 2359300
  1.8 55.4 %copy-start.1 = (bf16[2,384,512]{2,1,0:T(8,128)(2,1)S(1)}, bf16[2,384,512]{2,1,0:T(8,128)(2,1)}, u32[]{:S(2)}) copy-start(bf16[2,384,512]{2,1,0:T(8,128)(2,1)} %up_ref.3) | copy-start | bytes 2359300
  1.8 16.3 %collective-permute-start = (bf16[104,128]{1,0:T(8,128)(2,1)S(1)}, bf16[104,128]{1,0:T(8,128)(2,1)S(1)}, u32[]{:S(2)}, u32[]{:S(2)}) collective-permute-start(bf16[104,128]{1,0:T(8,128)(2,1)S(1)} %pick.1), channel_id=1, source_target_pairs={{0,0},{1,1},{2,32},{3,33},{4,64},{5,65},{6,96},{7,97},{8,128},{9,1... | collective-permute-start | bytes 79880 | tf_op jit(solution)/shard_map/ppermute | solution.py:208
  18.8 23.9 %all-to-all-start = ((bf16[8,104,128]{2,1,0:T(8,128)(2,1)}), bf16[8,104,128]{2,1,0:T(8,128)(2,1)S(1)}, u32[]{:S(2)}, u32[]{:S(2)}) async-start(bf16[8,104,128]{2,1,0:T(8,128)(2,1)} %broadcast_in_dim.2), calls=%async_computation | async-start | bytes 425984 | tf_op jit(solution)/shard_map/all_to_all | solution.py:210
  57.2 1.1 copy-start.4
  59.4 4.2 %collective-permute-start.1 = (bf16[4,6,32,512]{3,2,1,0:T(8,128)(2,1)S(1)}, bf16[4,6,32,512]{3,2,1,0:T(8,128)(2,1)S(1)}, u32[]{:S(2)}, u32[]{:S(2)}) collective-permute-start(bf16[4,6,32,512]{3,2,1,0:T(8,128)(2,1)S(1)} %get-tuple-element.10), channel_id=1, source_target_pairs={{0,32},{32,0},{1,33},{33,1},{2,34},{34,2},{3,35},{35,3},{4,36},{36... | collective-permute-start | bytes 2359304 | tf_op jit(solution)/shard_map/ppermute | solution.py:218
  122.6 4.2 %collective-permute-start.2 = (bf16[4,6,32,512]{3,2,1,0:T(8,128)(2,1)S(1)}, bf16[4,6,32,512]{3,2,1,0:T(8,128)(2,1)S(1)}, u32[]{:S(2)}, u32[]{:S(2)}) collective-permute-start(bf16[4,6,32,512]{3,2,1,0:T(8,128)(2,1)S(1)} %all_gather.20.mine_ref), channel_id=1, source_target_pairs={{0,32},{32,0},{1,33},{33,1},{2,34},{34,2},{3,35},{35,3},{4,36},{36... | collective-permute-start | bytes 2359304 | tf_op jit(solution)/shard_map/ppermute | solution.py:231
  126.8 0.9 copy-start.2
  138.7 22.9 %copy-start.3 = (bf16[4,6,32,512]{3,2,1,0:T(8,128)(2,1)S(1)}, bf16[4,6,32,512]{3,2,1,0:T(8,128)(2,1)}, u32[]{:S(2)}) copy-start(bf16[4,6,32,512]{3,2,1,0:T(8,128)(2,1)} %copy-done.2) | copy-start | bytes 2359300
  152.1 13.4 %copy-start.5 = (s32[2,16]{1,0:T(2,128)S(1)}, s32[2,16]{1,0:T(2,128)}, u32[]{:S(2)}) copy-start(s32[2,16]{1,0:T(2,128)} %slot_ref.1) | copy-start | bytes 388
  152.2 13.4 %collective-permute-start.3 = (bf16[48,128]{1,0:T(8,128)(2,1)S(1)}, bf16[48,128]{1,0:T(8,128)(2,1)S(1)}, u32[]{:S(2)}, u32[]{:S(2)}) collective-permute-start(bf16[48,128]{1,0:T(8,128)(2,1)S(1)} %reduce_sum.48), channel_id=1, source_target_pairs={{0,0},{1,1},{32,2},{33,3},{64,4},{65,5},{96,6},{97,7},{128,8},{129... | collective-permute-start | bytes 36872 | tf_op jit(solution)/shard_map/ppermute | solution.py:241

commit v3 on v2

--- a/solution.py
+++ b/solution.py
@@ -18,12 +18,49 @@
 F32 = jnp.float32
 
 
+def ring(a, b, n):
+    return min((a - b) % n, (b - a) % n)
+
+
+def columns(zl):
+    x_here, zh_here = divmod(zl, ZH)
+    by_reach = sorted(range(ZL), key=lambda p: (abs(p - zl), p))
+    by_ring = sorted(range(X), key=lambda x: (-ring(x, x_here, X), x))
+    near = {(x, zh_here): p for x, p in zip(by_ring, by_reach[:4])}
+    far = {(x, 1 - zh_here): p for x, p in zip(by_ring, by_reach[:3:-1])}
+    return near | far
+
+
 def outward():
-    return [
-        (k * N_SHARD + s, (s // 2) * N_SHARD + 2 * k + s % 2)
-        for k in range(X * ZH * C)
-        for s in range(N_SHARD)
-    ]
+    pairs = []
+    for k in range(X * ZH * C):
+        x, zh, c = k // 4, k // 2 % 2, k % 2
+        for s in range(N_SHARD):
+            column = columns(s // Y)[(x, zh)]
+            there, h = s // 2, s % 2
+            line = s % Y if c == 0 else (s % Y // 2 * 2 + 3 - h) % Y
+            pairs.append((k * N_SHARD + s, there * N_SHARD + column * Y + line))
+    return pairs
+
+
+def code_of(zl):
+    return sum(p << 3 * (ZH * x + zh) for (x, zh), p in columns(zl).items())
+
+
+class Slots:
+    def __init__(self, dp_ref):
+        self.core = dp_ref[0] & 1
+        zl = dp_ref[0] >> 1
+        self.code = sum(jnp.where(zl == i, code_of(i), 0) for i in range(ZL))
+
+    def halves(self):
+        return (self.core, 1 - self.core)
+
+    def column(self, j):
+        return (self.code >> 3 * j) & 7
+
+    def line(self, half, h):
+        return jnp.where(half == 0, 2 * self.core + h, (2 * self.core + 3 - h) & 3)
 
 
 def homeward():
@@ -80,33 +117,40 @@
     return jnp.concatenate([part[:, :128] for part in rows] + [left], axis=0)
 
 
-def features(got_ref, core, m, e):
+def features(got_ref, slots, m, e):
     blocks = []
-    for half in (core, 1 - core):
-        parts = []
-        for h in range(2):
-            main = got_ref[2 * half + h, :, m * PACK + e * R : m * PACK + (e + 1) * R, :]
-            left = got_ref[2 * half + h, :, m * PACK + 2 * R : (m + 1) * PACK, :]
-            parts.append(main.reshape(ZH * X * R, 128))
-            parts.append(left.reshape(ZH * X * R, 128)[:, e * 64 : (e + 1) * 64])
-        blocks.append(jnp.concatenate(parts, axis=1))
+    for half in slots.halves():
+        lines = [slots.line(half, h) for h in range(2)]
+        for j in range(ZH * X):
+            parts = []
+            for line in lines:
+                at = got_ref.at[line, slots.column(j)]
+                parts.append(at[m * PACK + e * R : m * PACK + (e + 1) * R, :])
+                left = at[m * PACK + 2 * R : (m + 1) * PACK, :]
+                parts.append(left[:, e * 64 : (e + 1) * 64])
+            blocks.append(jnp.concatenate(parts, axis=1))
     return jnp.concatenate(blocks, axis=0)
 
 
-def forward_kernel(core_ref, got_ref, gate_ref, up_ref, down_ref, keep_ref, send_ref):
-    core = core_ref[0]
-    for e in range(2):
-        rows = features(got_ref, core, 0, e)
-        cot = features(got_ref, core, 1, e)
-        parts = (
-            dot(rows, gate_ref[e], ((1,), (0,))),
-            dot(rows, up_ref[e], ((1,), (0,))),
-            dot(cot, down_ref[e], ((1,), (1,))),
-        )
-        for t, part in enumerate(parts):
-            part = part.astype(BF16).reshape(C, X, ZH * R, 512)
-            keep_ref[:, 2 * t + e] = part[0]
-            send_ref[:, 2 * t + e] = part[1]
+def forward_kernel(
+    dp_ref, got_ref, gate_ref, up_ref, down_hbm, keep_ref, send_ref, down_ref, sem
+):
+    move = pltpu.make_async_copy(down_hbm, down_ref, sem)
+    move.start()
+    slots = Slots(dp_ref)
+
+    def give(t, e, part):
+        part = part.astype(BF16).reshape(C, X, ZH * R, 512)
+        keep_ref[:, 2 * t + e] = part[0]
+        send_ref[:, 2 * t + e] = part[1]
+
+    for e in range(2):
+        rows = features(got_ref, slots, 0, e)
+        give(0, e, dot(rows, gate_ref[e], ((1,), (0,))))
+        give(1, e, dot(rows, up_ref[e], ((1,), (0,))))
+    move.wait()
+    for e in range(2):
+        give(2, e, dot(features(got_ref, slots, 1, e), down_ref[e], ((1,), (1,))))
 
 
 def all_rows(mine_ref, other_ref, t, e):
@@ -115,35 +159,33 @@
     )
 
 
-def back_kernel(core_ref, mine_ref, other_ref, gate_ref, up_ref, out_ref):
-    core = core_ref[0]
+def back_kernel(dp_ref, mine_ref, other_ref, gate_ref, up_ref, out_ref):
+    slots = Slots(dp_ref)
     terms = []
     for e in range(2):
         grad_gate = all_rows(mine_ref, other_ref, 1, e)
         grad_up = all_rows(mine_ref, other_ref, 2, e)
         term = dot(grad_gate, gate_ref[e], ((1,), (1,))) + dot(grad_up, up_ref[e], ((1,), (1,)))
         terms.append(term.astype(BF16))
-    for at, half in enumerate((core, 1 - core)):
+    for i, half in enumerate(slots.halves()):
         for h in range(2):
-            rows = slice(at * ZH * X * R, (at + 1) * ZH * X * R)
-            here = [term[rows, h * HALF : (h + 1) * HALF] for term in terms]
-            for e in range(2):
-                main = here[e][:, :128].reshape(ZH * X, R, 128)
-                out_ref[2 * half + h, :, e * R : (e + 1) * R, :] = main
-            left = jnp.concatenate([part[:, 128:] for part in here], axis=1)
-            out_ref[2 * half + h, :, 2 * R :, :] = left.reshape(ZH * X, R, 128)
-
-
-def weight_kernel(core_ref, got_ref, mine_ref, other_ref, gate_out, up_out, down_out):
-    core = core_ref[0]
-    for e in range(2):
-        count = sum(
-            jnp.sum(got_ref[2 * half, :, 2 * PACK :, :][:, :, e * 64 : (e + 1) * 64].astype(F32))
-            for half in range(2)
-        )
+            line = slots.line(half, h)
+            for j in range(ZH * X):
+                first = (i * ZH * X + j) * R
+                rows = [
+                    term[first : first + R, h * HALF : (h + 1) * HALF] for term in terms
+                ]
+                out_ref[line, slots.column(j)] = packed(rows)
+
+
+def weight_kernel(dp_ref, got_ref, mine_ref, other_ref, gate_out, up_out, down_out):
+    slots = Slots(dp_ref)
+    notes = got_ref[:, :, 2 * PACK :, :].astype(F32).reshape(Y * ZL * 8, 128)
+    for e in range(2):
+        count = 0.5 * jnp.sum(notes[:, e * 64 : (e + 1) * 64])
         scale = 1.0 / jnp.full((1, 512), count, F32)
-        rows = features(got_ref, core, 0, e)
-        cot = features(got_ref, core, 1, e)
+        rows = features(got_ref, slots, 0, e)
+        cot = features(got_ref, slots, 1, e)
         hidden, grad_gate, grad_up = (all_rows(mine_ref, other_ref, t, e) for t in range(3))
         gate_out[e] = (dot(rows, grad_gate, ((0,), (0,))) * scale).astype(BF16)
         up_out[e] = (dot(rows, grad_up, ((0,), (0,))) * scale).astype(BF16)
@@ -168,6 +210,10 @@
 
 def in_vmem(x):
     return pltpu.with_memory_space_constraint(x, pltpu.VMEM)
+
+
+def in_hbm(x):
+    return pltpu.with_memory_space_constraint(x, pltpu.HBM)
 
 
 def local(kernel, specs, outs, name, stay=True, scratch=()):
@@ -189,8 +235,8 @@
 def on_device(
     tokens, cotangent, gate_proj, up_proj, down_proj, slot_tokens, gate_weights, live_counts
 ):
-    core = lax.axis_index("c").astype(jnp.int32).reshape(1)
-    gate_proj, up_proj, down_proj = (in_vmem(w) for w in (gate_proj, up_proj, down_proj))
+    dp = lax.axis_index(DP).astype(jnp.int32).reshape(1)
+    gate_proj, up_proj = in_vmem(gate_proj), in_vmem(up_proj)
     scratch = [
         pltpu.VMEM(tokens.shape, BF16),
         pltpu.VMEM(cotangent.shape, BF16),
@@ -201,7 +247,7 @@
     ]
     (message,) = local(pick_kernel, [HB] * 5, [(MESSAGE, 128)], "pick", scratch=scratch)(
         *(
-            pltpu.with_memory_space_constraint(a, pltpu.HBM)
+            in_hbm(a)
             for a in (tokens, cotangent, slot_tokens, gate_weights, live_counts.reshape(2))
         )
     )
@@ -211,9 +257,10 @@
     got = in_vmem(lax.all_gather(column, "y", axis=0, tiled=False))
 
     stage = (X, 6, ZH * R, 512)
-    keep, send = local(forward_kernel, [SM, VM, VM, VM, VM], [stage, stage], "forward")(
-        core, got, gate_proj, up_proj, down_proj
-    )
+    scratch = [pltpu.VMEM(down_proj.shape, BF16), pltpu.SemaphoreType.DMA]
+    keep, send = local(
+        forward_kernel, [SM, VM, VM, VM, HB], [stage, stage], "forward", scratch=scratch
+    )(dp, got, gate_proj, up_proj, in_hbm(down_proj))
     swap = [(0, 1), (1, 0)]
     heard = lax.ppermute(send, "c", swap)
     paired = (keep.astype(F32) + heard.astype(F32)).astype(BF16)
@@ -232,7 +279,7 @@
     mine = in_vmem(mine)
 
     (back,) = local(back_kernel, [SM, VM, VM, VM, VM], [(C * 2, X * ZH, PACK, 128)], "back")(
-        core, mine, other, gate_proj, up_proj
+        dp, mine, other, gate_proj, up_proj
     )
     over_y = lax.all_to_all(back, "y", 0, 0, tiled=True)
     over_y = jnp.sum(over_y.astype(F32), axis=0).astype(BF16)
@@ -245,7 +292,7 @@
         [gate_proj.shape, up_proj.shape, down_proj.shape],
         "weights",
         False,
-    )(core, got, mine, other)
+    )(dp, got, mine, other)
     (grad_tokens,) = local(place_kernel, [VM, VM], [tokens.shape], "place", False)(
         home, slot_tokens
     )

time: 167 us -> 165 us (0.988)
  starting transfers between devices: 36.4 us -> 27.4 us
  blocking collectives: 97.3 us -> 102 us
  waiting for transfers between devices: 23.1 us -> 25.9 us
    ppermute x1, starting transfers between devices: 9.38 us -> 3.02 us  [on_device(): home = in_vmem(lax.ppermute(over_zl, EVERY, homeward()))]
    ppermute x1, waiting for transfers between devices: 1.5 us -> 4.78 us  [on_device(): home = in_vmem(lax.ppermute(over_zl, EVERY, homeward()))]
    ppermute x1, starting transfers between devices: 14.5 us -> 12.4 us  [on_device(): message = lax.ppermute(message, EVERY, outward())]
    all_to_all x1, blocking collectives: 13.4 us -> 15.3 us  [on_device(): over_zl = lax.all_to_all(over_y, 'zl', 0, 0, tiled=True)]
where the time goes in v3:
time: 165 us
  blocking collectives  102 us (62%)
  starting transfers between devices  27.4 us (17%)
  waiting for transfers between devices  25.9 us (16%)
  Pallas kernels  7.53 us (5%)
    all_gather x1, blocking collectives, on_device(): over_zh = lax.all_gather(over_x, 'zh', axis=0, tiled=False)  26 us
    all_to_all x1, blocking collectives, on_device(): over_x = lax.all_to_all(paired, 'x', 0, 0, tiled=True)  19.3 us
    all_to_all x1, blocking collectives, on_device(): over_zl = lax.all_to_all(over_y, 'zl', 0, 0, tiled=True)  15.3 us
    all_to_all x1, waiting for transfers between devices, on_device(): column = lax.all_to_all(copies, 'zl', 0, 0, tiled=True)  15.1 us
    all_gather x1, blocking collectives, on_device(): got = in_vmem(lax.all_gather(column, 'y', axis=0, tiled=False))  15.1 us
    all_gather x1, blocking collectives, on_device(): mine = lax.all_gather(acts, 'x', axis=0, tiled=False)  14.1 us
    ppermute x1, starting transfers between devices, on_device(): message = lax.ppermute(message, EVERY, outward())  12.4 us
    all_to_all x1, blocking collectives, on_device(): over_y = lax.all_to_all(back, 'y', 0, 0, tiled=True)  11.9 us
  transfers between devices with their start and end apart: 5, of which 5 were waited for; matrix products, arithmetic and copies ran while one was open for 0% of the time, Pallas kernels for 2%

profile of v3, /device:TPU:32, one launch (start us, length us, event | category | flops | bytes accessed | tf_op | source)
XLA Modules:
  0.0 164.5 jit_solution(7648703427150913436)
XLA Ops:
  0.6 1.1 pick.1
  1.8 0.0 copy-start
  1.8 0.0 copy-start.1
  1.8 12.4 %collective-permute-start = (bf16[104,128]{1,0:T(8,128)(2,1)S(1)}, bf16[104,128]{1,0:T(8,128)(2,1)S(1)}, u32[]{:S(2)}, u32[]{:S(2)}) collective-permute-start(bf16[104,128]{1,0:T(8,128)(2,1)S(1)} %pick.1), channel_id=1, source_target_pairs={{0,12},{1,13},{2,46},{3,47},{4,80},{5,81},{6,114},{7,115},{8,132},... | collective-permute-start | bytes 79880 | tf_op jit(solution)/shard_map/ppermute | solution.py:254
  14.2 1.5 collective-permute-done
  15.7 0.7 broadcast_in_dim.2
  16.4 8.2 %all-to-all-start = ((bf16[8,104,128]{2,1,0:T(8,128)(2,1)}), bf16[8,104,128]{2,1,0:T(8,128)(2,1)S(1)}, u32[]{:S(2)}, u32[]{:S(2)}) async-start(bf16[8,104,128]{2,1,0:T(8,128)(2,1)} %broadcast_in_dim.2), calls=%async_computation | async-start | bytes 425984 | tf_op jit(solution)/shard_map/all_to_all | solution.py:256
  24.6 15.1 %all-to-all-done = bf16[8,104,128]{2,1,0:T(8,128)(2,1)S(1)} async-done(((bf16[8,104,128]{2,1,0:T(8,128)(2,1)}), bf16[8,104,128]{2,1,0:T(8,128)(2,1)S(1)}, u32[]{:S(2)}, u32[]{:S(2)}) %all-to-all-start) | async-done | bytes 213024 | tf_op jit(solution)/shard_map/all_to_all | solution.py:256
  39.7 15.1 %all-gather = bf16[32,104,128]{2,1,0:T(8,128)(2,1)S(1)} all-gather(bf16[8,104,128]{2,1,0:T(8,128)(2,1)S(1)} %all-to-all-done), channel_id=2, replica_groups=mesh['x'=4,'zh'=2,'c'=2,'zl'=8,'y'=4] {'y'}, dimensions={0}, use_global_device_ids=true | all-gather | bytes 1064960 | tf_op jit(solution)/shard_map/all_gather | solution.py:257
  54.8 0.0 copy-done
  54.8 0.0 copy-done.1
  54.8 2.2 %forward.1 = (bf16[4,6,32,512]{3,2,1,0:T(8,128)(2,1)S(1)}, bf16[4,6,32,512]{3,2,1,0:T(8,128)(2,1)S(1)}) custom-call(s32[1]{0:T(128)} %bitcast.dp_ref, bf16[4,8,104,128]{3,2,1,0:T(8,128)(2,1)S(1)} %bitcast.11, bf16[2,384,512]{2,1,0:T(8,128)(2,1)S(1)} %copy-done, bf16[2,384,512]{2,1,0:T(8,128)(2,1)S(1)} %copy-done.1, bf16[2,512,384]{2,1,0:T(8,128)(2,1)} %down_hbm.1), custom_call_target="tpu_custom_call" | custom-call | tf_op jit(solution)/shard_map/forward/pallas_call | solution.py:261
  56.9 1.9 %collective-permute-start.1 = (bf16[4,6,32,512]{3,2,1,0:T(8,128)(2,1)S(1)}, bf16[4,6,32,512]{3,2,1,0:T(8,128)(2,1)S(1)}, u32[]{:S(2)}, u32[]{:S(2)}) collective-permute-start(bf16[4,6,32,512]{3,2,1,0:T(8,128)(2,1)S(1)} %get-tuple-element.10), channel_id=1, source_target_pairs={{0,32},{32,0},{1,33},{33,1},{2,34},{34,2},{3,35},{35,3},{4,36},{36... | collective-permute-start | bytes 2359304 | tf_op jit(solution)/shard_map/ppermute | solution.py:265
  58.9 2.3 %collective-permute-done.1 = bf16[4,6,32,512]{3,2,1,0:T(8,128)(2,1)S(1)} collective-permute-done((bf16[4,6,32,512]{3,2,1,0:T(8,128)(2,1)S(1)}, bf16[4,6,32,512]{3,2,1,0:T(8,128)(2,1)S(1)}, u32[]{:S(2)}, u32[]{:S(2)}) %collective-permute-start.1) | collective-permute-done | bytes 786464 | tf_op jit(solution)/shard_map/ppermute | solution.py:265
  61.1 0.3 add_convert_fusion
  61.4 19.3 %all_to_all.20 = bf16[4,6,32,512]{3,2,1,0:T(8,128)(2,1)S(1)} all-to-all(bf16[4,6,32,512]{3,2,1,0:T(8,128)(2,1)S(1)} %add_convert_fusion), channel_id=1, replica_groups=mesh['x'=4,'zh'=2,'c'=2,'zl'=8,'y'=4] {'x'}, dimensions={0} | all-to-all | bytes 1572864 | tf_op jit(solution)/shard_map/all_to_all | solution.py:267
  80.7 0.1 reduce_sum.45
  80.8 26.0 %all-gather.1 = bf16[12,32,512]{2,1,0:T(8,128)(2,1)S(1)} all-gather(bf16[6,32,512]{2,1,0:T(8,128)(2,1)S(1)} %reduce_sum.45), channel_id=3, replica_groups=mesh['x'=4,'zh'=2,'c'=2,'zl'=8,'y'=4] {'zh'}, dimensions={0}, use_global_device_ids=true | all-gather | bytes 589824 | tf_op jit(solution)/shard_map/all_gather | solution.py:269
  106.8 0.1 convert_reduce_fusion
  106.8 0.1 fusion
  106.9 14.1 %all_gather.20.mine_ref = bf16[4,6,32,512]{3,2,1,0:T(8,128)(2,1)S(1)} all-gather(bf16[1,6,32,512]{3,2,1,0:T(8,128)(2,1)S(1)} %pad_maximum_fusion), channel_id=1, replica_groups=mesh['x'=4,'zh'=2,'c'=2,'zl'=8,'y'=4] {'x'}, dimensions={0}, use_global_device_ids=true | all-gather | bytes 983040 | tf_op jit(solution)/shard_map/all_gather | solution.py:277
  121.0 1.9 %collective-permute-start.2 = (bf16[4,6,32,512]{3,2,1,0:T(8,128)(2,1)S(1)}, bf16[4,6,32,512]{3,2,1,0:T(8,128)(2,1)S(1)}, u32[]{:S(2)}, u32[]{:S(2)}) collective-permute-start(bf16[4,6,32,512]{3,2,1,0:T(8,128)(2,1)S(1)} %all_gather.20.mine_ref), channel_id=1, source_target_pairs={{0,32},{32,0},{1,33},{33,1},{2,34},{34,2},{3,35},{35,3},{4,36},{36... | collective-permute-start | bytes 2359304 | tf_op jit(solution)/shard_map/ppermute | solution.py:278
  123.0 2.3 %collective-permute-done.2.other_ref = bf16[4,6,32,512]{3,2,1,0:T(8,128)(2,1)S(1)} collective-permute-done((bf16[4,6,32,512]{3,2,1,0:T(8,128)(2,1)S(1)}, bf16[4,6,32,512]{3,2,1,0:T(8,128)(2,1)S(1)}, u32[]{:S(2)}, u32[]{:S(2)}) %collective-permute-start.2) | collective-permute-done | bytes 786464 | tf_op jit(solution)/shard_map/ppermute | solution.py:278
  125.2 0.0 copy-start.2
  125.2 0.9 back.1
  126.1 0.0 copy-done.2
  126.1 11.9 %all_to_all.21 = bf16[4,8,48,128]{3,2,1,0:T(8,128)(2,1)S(1)} all-to-all(bf16[4,8,48,128]{3,2,1,0:T(8,128)(2,1)S(1)} %back.1), channel_id=1, replica_groups=mesh['x'=4,'zh'=2,'c'=2,'zl'=8,'y'=4] {'y'}, dimensions={0} | all-to-all | bytes 786432 | tf_op jit(solution)/shard_map/all_to_all | solution.py:284
  137.9 0.0 copy-start.3
  137.9 0.1 reduce_sum.47
  138.0 15.3 %all_to_all.22 = bf16[8,48,128]{2,1,0:T(8,128)(2,1)S(1)} all-to-all(bf16[8,48,128]{2,1,0:T(8,128)(2,1)S(1)} %reduce_sum.47), channel_id=1, replica_groups=mesh['x'=4,'zh'=2,'c'=2,'zl'=8,'y'=4] {'zl'}, dimensions={0} | all-to-all | bytes 196608 | tf_op jit(solution)/shard_map/all_to_all | solution.py:286
  153.3 0.0 copy-start.4
  153.3 3.0 %collective-permute-start.3 = (bf16[48,128]{1,0:T(8,128)(2,1)S(1)}, bf16[48,128]{1,0:T(8,128)(2,1)S(1)}, u32[]{:S(2)}, u32[]{:S(2)}) collective-permute-start(bf16[48,128]{1,0:T(8,128)(2,1)S(1)} %reduce_sum.48), channel_id=1, source_target_pairs={{12,0},{13,1},{46,2},{47,3},{80,4},{81,5},{114,6},{115,7},{132,8},... | collective-permute-start | bytes 36872 | tf_op jit(solution)/shard_map/ppermute | solution.py:288
  156.3 0.0 copy-done.3
  156.3 2.6 %weights.1 = (bf16[2,384,512]{2,1,0:T(8,128)(2,1)}, bf16[2,384,512]{2,1,0:T(8,128)(2,1)}, bf16[2,512,384]{2,1,0:T(8,128)(2,1)}) custom-call(s32[1]{0:T(128)} %bitcast.dp_ref, bf16[4,8,104,128]{3,2,1,0:T(8,128)(2,1)S(1)} %bitcast.12, bf16[4,6,32,512]{3,2,1,0:T(8,128)(2,1)S(1)} %all_gather.20.mine_ref, bf16[4,6,32,512]{3,2,1,0:T(8,128)(2,1)S(1)} %copy-done.3), custom_call_target="tpu_custom_call" | custom-call | tf_op jit(solution)/shard_map/weights/pallas_call | solution.py:289
  158.9 4.8 %collective-permute-done.3.rows_ref = bf16[48,128]{1,0:T(8,128)(2,1)S(1)} collective-permute-done((bf16[48,128]{1,0:T(8,128)(2,1)S(1)}, bf16[48,128]{1,0:T(8,128)(2,1)S(1)}, u32[]{:S(2)}, u32[]{:S(2)}) %collective-permute-start.3) | collective-permute-done | bytes 12320 | tf_op jit(solution)/shard_map/ppermute | solution.py:288
  163.7 0.0 copy-done.4
  163.7 0.8 place.1
  (2 shorter events, 0.0 us)
Async XLA Ops:
  1.8 53.0 %copy-start = (bf16[2,384,512]{2,1,0:T(8,128)(2,1)S(1)}, bf16[2,384,512]{2,1,0:T(8,128)(2,1)}, u32[]{:S(2)}) copy-start(bf16[2,384,512]{2,1,0:T(8,128)(2,1)} %gate_ref.3) | copy-start | bytes 2359300
  1.8 53.0 %copy-start.1 = (bf16[2,384,512]{2,1,0:T(8,128)(2,1)S(1)}, bf16[2,384,512]{2,1,0:T(8,128)(2,1)}, u32[]{:S(2)}) copy-start(bf16[2,384,512]{2,1,0:T(8,128)(2,1)} %up_ref.3) | copy-start | bytes 2359300
  1.8 13.9 %collective-permute-start = (bf16[104,128]{1,0:T(8,128)(2,1)S(1)}, bf16[104,128]{1,0:T(8,128)(2,1)S(1)}, u32[]{:S(2)}, u32[]{:S(2)}) collective-permute-start(bf16[104,128]{1,0:T(8,128)(2,1)S(1)} %pick.1), channel_id=1, source_target_pairs={{0,12},{1,13},{2,46},{3,47},{4,80},{5,81},{6,114},{7,115},{8,132},... | collective-permute-start | bytes 79880 | tf_op jit(solution)/shard_map/ppermute | solution.py:254
  16.4 23.3 %all-to-all-start = ((bf16[8,104,128]{2,1,0:T(8,128)(2,1)}), bf16[8,104,128]{2,1,0:T(8,128)(2,1)S(1)}, u32[]{:S(2)}, u32[]{:S(2)}) async-start(bf16[8,104,128]{2,1,0:T(8,128)(2,1)} %broadcast_in_dim.2), calls=%async_computation | async-start | bytes 425984 | tf_op jit(solution)/shard_map/all_to_all | solution.py:256
  56.9 4.2 %collective-permute-start.1 = (bf16[4,6,32,512]{3,2,1,0:T(8,128)(2,1)S(1)}, bf16[4,6,32,512]{3,2,1,0:T(8,128)(2,1)S(1)}, u32[]{:S(2)}, u32[]{:S(2)}) collective-permute-start(bf16[4,6,32,512]{3,2,1,0:T(8,128)(2,1)S(1)} %get-tuple-element.10), channel_id=1, source_target_pairs={{0,32},{32,0},{1,33},{33,1},{2,34},{34,2},{3,35},{35,3},{4,36},{36... | collective-permute-start | bytes 2359304 | tf_op jit(solution)/shard_map/ppermute | solution.py:265
  121.0 4.2 %collective-permute-start.2 = (bf16[4,6,32,512]{3,2,1,0:T(8,128)(2,1)S(1)}, bf16[4,6,32,512]{3,2,1,0:T(8,128)(2,1)S(1)}, u32[]{:S(2)}, u32[]{:S(2)}) collective-permute-start(bf16[4,6,32,512]{3,2,1,0:T(8,128)(2,1)S(1)} %all_gather.20.mine_ref), channel_id=1, source_target_pairs={{0,32},{32,0},{1,33},{33,1},{2,34},{34,2},{3,35},{35,3},{4,36},{36... | collective-permute-start | bytes 2359304 | tf_op jit(solution)/shard_map/ppermute | solution.py:278
  125.2 0.9 copy-start.2
  137.9 18.4 %copy-start.3 = (bf16[4,6,32,512]{3,2,1,0:T(8,128)(2,1)S(1)}, bf16[4,6,32,512]{3,2,1,0:T(8,128)(2,1)}, u32[]{:S(2)}) copy-start(bf16[4,6,32,512]{3,2,1,0:T(8,128)(2,1)} %copy-done.2) | copy-start | bytes 2359300
  153.3 10.4 %copy-start.4 = (s32[2,16]{1,0:T(2,128)S(1)}, s32[2,16]{1,0:T(2,128)}, u32[]{:S(2)}) copy-start(s32[2,16]{1,0:T(2,128)} %slot_ref.1) | copy-start | bytes 388
  153.3 10.4 %collective-permute-start.3 = (bf16[48,128]{1,0:T(8,128)(2,1)S(1)}, bf16[48,128]{1,0:T(8,128)(2,1)S(1)}, u32[]{:S(2)}, u32[]{:S(2)}) collective-permute-start(bf16[48,128]{1,0:T(8,128)(2,1)S(1)} %reduce_sum.48), channel_id=1, source_target_pairs={{12,0},{13,1},{46,2},{47,3},{80,4},{81,5},{114,6},{115,7},{132,8},... | collective-permute-start | bytes 36872 | tf_op jit(solution)/shard_map/ppermute | solution.py:288

commit v4 on v3

--- a/solution.py
+++ b/solution.py
@@ -36,10 +36,9 @@
     for k in range(X * ZH * C):
         x, zh, c = k // 4, k // 2 % 2, k % 2
         for s in range(N_SHARD):
-            column = columns(s // Y)[(x, zh)]
-            there, h = s // 2, s % 2
-            line = s % Y if c == 0 else (s % Y // 2 * 2 + 3 - h) % Y
-            pairs.append((k * N_SHARD + s, there * N_SHARD + column * Y + line))
+            zl, y = divmod(s, Y)
+            there = zl * C + c
+            pairs.append((k * N_SHARD + s, there * N_SHARD + columns(zl)[(x, zh)] * Y + y))
     return pairs
 
 
@@ -58,9 +57,6 @@
 
     def column(self, j):
         return (self.code >> 3 * j) & 7
-
-    def line(self, half, h):
-        return jnp.where(half == 0, 2 * self.core + h, (2 * self.core + 3 - h) & 3)
 
 
 def homeward():
@@ -117,76 +113,89 @@
     return jnp.concatenate([part[:, :128] for part in rows] + [left], axis=0)
 
 
-def features(got_ref, slots, m, e):
+def features(at, slots, m, e):
     blocks = []
-    for half in slots.halves():
-        lines = [slots.line(half, h) for h in range(2)]
-        for j in range(ZH * X):
-            parts = []
-            for line in lines:
-                at = got_ref.at[line, slots.column(j)]
-                parts.append(at[m * PACK + e * R : m * PACK + (e + 1) * R, :])
-                left = at[m * PACK + 2 * R : (m + 1) * PACK, :]
-                parts.append(left[:, e * 64 : (e + 1) * 64])
-            blocks.append(jnp.concatenate(parts, axis=1))
+    for j in range(ZH * X):
+        parts = []
+        for h in range(2):
+            block = at(h, slots.column(j))
+            parts.append(block[m * PACK + e * R : m * PACK + (e + 1) * R, :])
+            left = block[m * PACK + 2 * R : (m + 1) * PACK, :]
+            parts.append(left[:, e * 64 : (e + 1) * 64])
+        blocks.append(jnp.concatenate(parts, axis=1))
     return jnp.concatenate(blocks, axis=0)
 
 
-def forward_kernel(
-    dp_ref, got_ref, gate_ref, up_ref, down_hbm, keep_ref, send_ref, down_ref, sem
-):
-    move = pltpu.make_async_copy(down_hbm, down_ref, sem)
-    move.start()
+def lines_of(got_ref, half):
+    return lambda h, column: got_ref.at[2 * half + h, column]
+
+
+def forward_kernel(dp_ref, got_ref, *refs):
+    *weights, out_ref, loan_ref, down_a, down_b, sems = refs
+    moves = [
+        pltpu.make_async_copy(weights[4 + i], target, sems.at[i])
+        for i, target in enumerate((down_a, down_b))
+    ]
+    for move in moves:
+        move.start()
     slots = Slots(dp_ref)
 
-    def give(t, e, part):
-        part = part.astype(BF16).reshape(C, X, ZH * R, 512)
-        keep_ref[:, 2 * t + e] = part[0]
-        send_ref[:, 2 * t + e] = part[1]
+    def give(t, e, rows, pair, dims):
+        part = dot(rows[0], pair[0][e], dims) + dot(rows[1], pair[1][e], dims)
+        out_ref[:, 2 * t + e] = part.astype(BF16).reshape(X, ZH * R, 512)
+
+    def both(m, e):
+        return [features(lines_of(got_ref, half), slots, m, e) for half in slots.halves()]
 
     for e in range(2):
-        rows = features(got_ref, slots, 0, e)
-        give(0, e, dot(rows, gate_ref[e], ((1,), (0,))))
-        give(1, e, dot(rows, up_ref[e], ((1,), (0,))))
-    move.wait()
+        rows = both(0, e)
+        give(0, e, rows, weights[0:2], ((1,), (0,)))
+        give(1, e, rows, weights[2:4], ((1,), (0,)))
+    for h in range(2):
+        loan_ref[h] = got_ref[2 * (1 - slots.core) + h]
+    for move in moves:
+        move.wait()
     for e in range(2):
-        give(2, e, dot(features(got_ref, slots, 1, e), down_ref[e], ((1,), (1,))))
-
-
-def all_rows(mine_ref, other_ref, t, e):
-    return jnp.concatenate(
-        [ref[:, 2 * t + e].reshape(ZH * X * R, 512) for ref in (mine_ref, other_ref)], axis=0
-    )
-
-
-def back_kernel(dp_ref, mine_ref, other_ref, gate_ref, up_ref, out_ref):
+        give(2, e, both(1, e), (down_a, down_b), ((1,), (1,)))
+
+
+def all_rows(refs, t, e):
+    return jnp.concatenate([ref[:, 2 * t + e].reshape(ZH * X * R, 512) for ref in refs], axis=0)
+
+
+def back_kernel(dp_ref, mine_ref, *refs):
+    *weights, out_ref = refs
     slots = Slots(dp_ref)
-    terms = []
+    grads = [[all_rows((mine_ref,), t, e) for t in (1, 2)] for e in range(2)]
+    for i, half in enumerate(slots.halves()):
+        terms = [
+            sum(dot(grads[e][t], weights[2 * t + i][e], ((1,), (1,))) for t in range(2)).astype(BF16)
+            for e in range(2)
+        ]
+        for h in range(2):
+            for j in range(ZH * X):
+                rows = [term[j * R : (j + 1) * R, h * HALF : (h + 1) * HALF] for term in terms]
+                out_ref[2 * half + h, slots.column(j)] = packed(rows)
+
+
+def weight_kernel(dp_ref, got_ref, lent_ref, mine_ref, other_ref, gate_out, up_out, down_out):
+    slots = Slots(dp_ref)
+    notes = [ref[0, :, 2 * PACK :, :].astype(F32).reshape(ZL * 8, 128) for ref in (got_ref, lent_ref)]
+    notes = jnp.concatenate(notes, axis=0)
+    acts = (mine_ref, other_ref)
     for e in range(2):
-        grad_gate = all_rows(mine_ref, other_ref, 1, e)
-        grad_up = all_rows(mine_ref, other_ref, 2, e)
-        term = dot(grad_gate, gate_ref[e], ((1,), (1,))) + dot(grad_up, up_ref[e], ((1,), (1,)))
-        terms.append(term.astype(BF16))
-    for i, half in enumerate(slots.halves()):
-        for h in range(2):
-            line = slots.line(half, h)
-            for j in range(ZH * X):
-                first = (i * ZH * X + j) * R
-                rows = [
-                    term[first : first + R, h * HALF : (h + 1) * HALF] for term in terms
-                ]
-                out_ref[line, slots.column(j)] = packed(rows)
-
-
-def weight_kernel(dp_ref, got_ref, mine_ref, other_ref, gate_out, up_out, down_out):
-    slots = Slots(dp_ref)
-    notes = got_ref[:, :, 2 * PACK :, :].astype(F32).reshape(Y * ZL * 8, 128)
-    for e in range(2):
-        count = 0.5 * jnp.sum(notes[:, e * 64 : (e + 1) * 64])
-        scale = 1.0 / jnp.full((1, 512), count, F32)
-        rows = features(got_ref, slots, 0, e)
-        cot = features(got_ref, slots, 1, e)
-        hidden, grad_gate, grad_up = (all_rows(mine_ref, other_ref, t, e) for t in range(3))
+        scale = 1.0 / jnp.full((1, 512), jnp.sum(notes[:, e * 64 : (e + 1) * 64]), F32)
+        rows, cot = (
+            jnp.concatenate(
+                [
+                    features(lines_of(got_ref, slots.core), slots, m, e),
+                    features(lines_of(lent_ref, 0), slots, m, e),
+                ],
+                axis=0,
+            )
+            for m in range(2)
+        )
+        hidden, grad_gate, grad_up = (all_rows(acts, t, e) for t in range(3))
         gate_out[e] = (dot(rows, grad_gate, ((0,), (0,))) * scale).astype(BF16)
         up_out[e] = (dot(rows, grad_up, ((0,), (0,))) * scale).astype(BF16)
         down_out[e] = (dot(hidden, cot, ((0,), (0,))) * scale[:, :384]).astype(BF16)
@@ -216,7 +225,7 @@
     return pltpu.with_memory_space_constraint(x, pltpu.HBM)
 
 
-def local(kernel, specs, outs, name, stay=True, scratch=()):
+def local(kernel, specs, outs, stay=True, scratch=()):
     if stay:
         shapes = [pltpu.VMEM(o, BF16) for o in outs]
     else:
@@ -228,15 +237,13 @@
         out_shape=shapes,
         scratch_shapes=scratch,
         compiler_params=pltpu.CompilerParams(vmem_limit_bytes=16 << 20),
-        name=name,
-    )
-
-
-def on_device(
+    )
+
+
+def layer(
     tokens, cotangent, gate_proj, up_proj, down_proj, slot_tokens, gate_weights, live_counts
 ):
     dp = lax.axis_index(DP).astype(jnp.int32).reshape(1)
-    gate_proj, up_proj = in_vmem(gate_proj), in_vmem(up_proj)
     scratch = [
         pltpu.VMEM(tokens.shape, BF16),
         pltpu.VMEM(cotangent.shape, BF16),
@@ -245,26 +252,30 @@
         pltpu.SMEM((2,), jnp.int32),
         pltpu.SemaphoreType.DMA((5,)),
     ]
-    (message,) = local(pick_kernel, [HB] * 5, [(MESSAGE, 128)], "pick", scratch=scratch)(
+    (message,) = local(pick_kernel, [HB] * 5, [(MESSAGE, 128)], scratch=scratch)(
         *(
             in_hbm(a)
             for a in (tokens, cotangent, slot_tokens, gate_weights, live_counts.reshape(2))
         )
     )
+    swap = [(0, 1), (1, 0)]
     message = lax.ppermute(message, EVERY, outward())
+    pairs = [
+        (place(w), place(lax.ppermute(w, "c", swap)))
+        for w, place in ((gate_proj, in_vmem), (up_proj, in_vmem), (down_proj, in_hbm))
+    ]
     copies = jnp.broadcast_to(message[None], (ZL, MESSAGE, 128))
     column = lax.all_to_all(copies, "zl", 0, 0, tiled=True)
     got = in_vmem(lax.all_gather(column, "y", axis=0, tiled=False))
 
-    stage = (X, 6, ZH * R, 512)
-    scratch = [pltpu.VMEM(down_proj.shape, BF16), pltpu.SemaphoreType.DMA]
-    keep, send = local(
-        forward_kernel, [SM, VM, VM, VM, HB], [stage, stage], "forward", scratch=scratch
-    )(dp, got, gate_proj, up_proj, in_hbm(down_proj))
-    swap = [(0, 1), (1, 0)]
-    heard = lax.ppermute(send, "c", swap)
-    paired = (keep.astype(F32) + heard.astype(F32)).astype(BF16)
-    over_x = lax.all_to_all(paired, "x", 0, 0, tiled=True)
+    parts, loan = local(
+        forward_kernel,
+        [SM] + [VM] * 5 + [HB] * 2,
+        [(X, 6, ZH * R, 512), (2, ZL, MESSAGE, 128)],
+        scratch=[pltpu.VMEM(down_proj.shape, BF16)] * 2 + [pltpu.SemaphoreType.DMA((2,))],
+    )(dp, got, *pairs[0], *pairs[1], *pairs[2])
+    lent = lax.ppermute(loan, "c", swap)
+    over_x = lax.all_to_all(parts, "x", 0, 0, tiled=True)
     over_x = jnp.sum(over_x.astype(F32), axis=0).astype(BF16)
     over_zh = lax.all_gather(over_x, "zh", axis=0, tiled=False)
     sums = jnp.sum(over_zh.astype(F32), axis=0)
@@ -275,27 +286,25 @@
     grad_up = cot_hidden * gate_sum * sigmoid_part
     acts = jnp.concatenate([hidden, grad_gate, grad_up], axis=0).astype(BF16)
     mine = lax.all_gather(acts, "x", axis=0, tiled=False)
-    other = in_vmem(lax.ppermute(mine, "c", swap))
+    other = lax.ppermute(mine, "c", swap)
     mine = in_vmem(mine)
 
-    (back,) = local(back_kernel, [SM, VM, VM, VM, VM], [(C * 2, X * ZH, PACK, 128)], "back")(
-        dp, mine, other, gate_proj, up_proj
+    (back,) = local(back_kernel, [SM] + [VM] * 5, [(Y, ZL, PACK, 128)], False)(
+        dp, mine, *pairs[0], *pairs[1]
     )
     over_y = lax.all_to_all(back, "y", 0, 0, tiled=True)
     over_y = jnp.sum(over_y.astype(F32), axis=0).astype(BF16)
     over_zl = lax.all_to_all(over_y, "zl", 0, 0, tiled=True)
     over_zl = jnp.sum(over_zl.astype(F32), axis=0).astype(BF16)
-    home = in_vmem(lax.ppermute(over_zl, EVERY, homeward()))
+    home = lax.ppermute(over_zl, EVERY, homeward())
+    home = in_vmem(home)
     grad_gate_proj, grad_up_proj, grad_down_proj = local(
         weight_kernel,
-        [SM, VM, VM, VM],
+        [SM, VM, VM, VM, VM],
         [gate_proj.shape, up_proj.shape, down_proj.shape],
-        "weights",
         False,
-    )(dp, got, mine, other)
-    (grad_tokens,) = local(place_kernel, [VM, VM], [tokens.shape], "place", False)(
-        home, slot_tokens
-    )
+    )(dp, got, lent, mine, other)
+    (grad_tokens,) = local(place_kernel, [VM, VM], [tokens.shape], False)(home, slot_tokens)
     return (grad_tokens, grad_gate_proj, grad_up_proj, grad_down_proj)
 
 
@@ -317,6 +326,4 @@
         P(None, DP, SHARD),
         P(None, SHARD, DP),
     )
-    return jax.shard_map(
-        on_device, mesh=fine, in_specs=in_specs, out_specs=out_specs, check_vma=False
-    )
+    return jax.shard_map(layer, mesh=fine, in_specs=in_specs, out_specs=out_specs, check_vma=False)

time: 165 us -> 159 us (0.964)
  blocking collectives: 102 us -> 80.6 us
  starting transfers between devices: 27.4 us -> 38.1 us
  Pallas kernels: 7.53 us -> 12 us
  waiting for transfers between devices: 25.9 us -> 22.2 us
  local copies, waits for them, and re-layouts: 0.76 us -> 3.99 us
    all_to_all x3 -> x2, blocking collectives: 46.4 us -> 29.2 us  [the longest x1 16.7 us: layer(): over_x = lax.all_to_all(parts, 'x', 0, 0, tiled=True)]
    ppermute x4 -> x7, starting transfers between devices: 19.3 us -> 25.9 us  [the longest x1 12.3 us: layer(): message = lax.ppermute(message, EVERY, outward())]
    pallas_call x5, Pallas kernels: 7.53 us -> 12 us  [the longest x1 4.04 us: layer(): local(forward_kernel, [SM] + [VM] * 5 + [HB] * 2, [(X, 6, ZH * R, 512), (...]
    all_to_all x1 -> x2, starting transfers between devices: 8.18 us -> 12.2 us  [the longest x1 8.6 us: layer(): column = lax.all_to_all(copies, 'zl', 0, 0, tiled=True)]
    all_gather x3, blocking collectives: 55.1 us -> 51.4 us  [the longest x1 23.4 us: layer(): over_zh = lax.all_gather(over_x, 'zh', axis=0, tiled=False)]
    unnamed x10 -> x20, local copies, waits for them, and re-layouts: 0.05 us -> 3.28 us
    ppermute x4 -> x7, waiting for transfers between devices: 10.8 us -> 8.89 us  [the longest x1 7.36 us: layer(): home = lax.ppermute(over_zl, EVERY, homeward())]
    all_to_all x1 -> x2, waiting for transfers between devices: 15.1 us -> 13.3 us  [the longest x1 6.79 us: layer(): column = lax.all_to_all(copies, 'zl', 0, 0, tiled=True)]
  transfers between devices with their start and end apart: 5 -> 9, of which waited for: 5 -> 4; matrix products, arithmetic and copies ran while one was open for 0% -> 0% of each run, Pallas kernels for 2% -> 2%
where the time goes in v4:
time: 159 us; the launch traced here: 158 us
  blocking collectives  80.6 us (51%)
  starting transfers between devices  38.1 us (24%)
  waiting for transfers between devices  22.2 us (14%)
  Pallas kernels  12 us (8%)
  local copies, waits for them, and re-layouts  3.99 us (3%)
    all_gather x1, blocking collectives, layer(): over_zh = lax.all_gather(over_x, 'zh', axis=0, tiled=False)  23.4 us
    all_to_all x1, blocking collectives, layer(): over_x = lax.all_to_all(parts, 'x', 0, 0, tiled=True)  16.7 us
    all_gather x1, blocking collectives, layer(): got = in_vmem(lax.all_gather(column, 'y', axis=0, tiled=False))  14.5 us
    all_gather x1, blocking collectives, layer(): mine = lax.all_gather(acts, 'x', axis=0, tiled=False)  13.4 us
    all_to_all x1, blocking collectives, layer(): over_zl = lax.all_to_all(over_y, 'zl', 0, 0, tiled=True)  12.5 us
    ppermute x1, starting transfers between devices, layer(): message = lax.ppermute(message, EVERY, outward())  12.3 us
    all_to_all x1, starting transfers between devices, layer(): column = lax.all_to_all(copies, 'zl', 0, 0, tiled=True)  8.6 us
    ppermute x1, waiting for transfers between devices, layer(): home = lax.ppermute(over_zl, EVERY, homeward())  7.36 us
  transfers between devices with their start and end apart: 9, of which 4 were waited for; matrix products, arithmetic and copies ran while one was open for 0% of the time, Pallas kernels for 2%

profile of v4, /device:TPU:32, one launch (start us, length us, event | category | flops | bytes accessed | tf_op | source)
XLA Modules:
  0.0 158.1 jit_solution(7051042218414870831)
XLA Ops:
  0.6 1.1 shard_map.111
  1.8 12.3 %collective-permute-start = (bf16[104,128]{1,0:T(8,128)(2,1)S(1)}, bf16[104,128]{1,0:T(8,128)(2,1)S(1)}, u32[]{:S(2)}, u32[]{:S(2)}) collective-permute-start(bf16[104,128]{1,0:T(8,128)(2,1)S(1)} %shard_map.111), channel_id=1, source_target_pairs={{0,12},{1,13},{2,14},{3,15},{4,80},{5,81},{6,82},{7,83},{8,132},{9... | collective-permute-start | bytes 79880 | tf_op jit(solution)/shard_map/ppermute | solution.py:262
  14.1 1.5 collective-permute-done
  15.6 0.0 copy-start.1
  15.6 0.7 broadcast_in_dim.2
  16.3 0.0 copy-start
  16.3 8.6 %all-to-all-start = ((bf16[8,104,128]{2,1,0:T(8,128)(2,1)}), bf16[8,104,128]{2,1,0:T(8,128)(2,1)S(1)}, u32[]{:S(2)}, u32[]{:S(2)}) async-start(bf16[8,104,128]{2,1,0:T(8,128)(2,1)} %broadcast_in_dim.2), calls=%async_computation | async-start | bytes 425984 | tf_op jit(solution)/shard_map/all_to_all | solution.py:268
  24.9 1.9 %collective-permute-start.3 = (bf16[2,512,384]{2,1,0:T(8,128)(2,1)}, bf16[2,512,384]{2,1,0:T(8,128)(2,1)}, u32[]{:S(2)}, u32[]{:S(2)}) collective-permute-start(bf16[2,512,384]{2,1,0:T(8,128)(2,1)} %refs_4_.1), channel_id=1, source_target_pairs={{0,32},{32,0},{1,33},{33,1},{2,34},{34,2},{3,35},{35,3},{4,36},{36... | collective-permute-start | bytes 2359304 | tf_op jit(solution)/shard_map/ppermute | solution.py:264
  26.8 2.4 %collective-permute-start.1 = (bf16[2,384,512]{2,1,0:T(8,128)(2,1)}, bf16[2,384,512]{2,1,0:T(8,128)(2,1)S(1)}, u32[]{:S(2)}, u32[]{:S(2)}) collective-permute-start(bf16[2,384,512]{2,1,0:T(8,128)(2,1)} %refs_0_.3), channel_id=1, source_target_pairs={{0,32},{32,0},{1,33},{33,1},{2,34},{34,2},{3,35},{35,3},{4,36},{36... | collective-permute-start | bytes 2359304 | tf_op jit(solution)/shard_map/ppermute | solution.py:264
  29.2 1.9 %collective-permute-start.2 = (bf16[2,384,512]{2,1,0:T(8,128)(2,1)}, bf16[2,384,512]{2,1,0:T(8,128)(2,1)}, u32[]{:S(2)}, u32[]{:S(2)}) collective-permute-start(bf16[2,384,512]{2,1,0:T(8,128)(2,1)} %refs_2_.3), channel_id=1, source_target_pairs={{0,32},{32,0},{1,33},{33,1},{2,34},{34,2},{3,35},{35,3},{4,36},{36... | collective-permute-start | bytes 2359304 | tf_op jit(solution)/shard_map/ppermute | solution.py:264
  31.2 6.8 %all-to-all-done = bf16[8,104,128]{2,1,0:T(8,128)(2,1)S(1)} async-done(((bf16[8,104,128]{2,1,0:T(8,128)(2,1)}), bf16[8,104,128]{2,1,0:T(8,128)(2,1)S(1)}, u32[]{:S(2)}, u32[]{:S(2)}) %all-to-all-start) | async-done | bytes 213024 | tf_op jit(solution)/shard_map/all_to_all | solution.py:268
  38.0 14.5 %all-gather = bf16[32,104,128]{2,1,0:T(8,128)(2,1)S(1)} all-gather(bf16[8,104,128]{2,1,0:T(8,128)(2,1)S(1)} %all-to-all-done), channel_id=2, replica_groups=mesh['x'=4,'zh'=2,'c'=2,'zl'=8,'y'=4] {'y'}, dimensions={0}, use_global_device_ids=true | all-gather | bytes 1064960 | tf_op jit(solution)/shard_map/all_gather | solution.py:269
  52.4 0.0 collective-permute-done.3.refs_5_
  52.5 0.0 collective-permute-done.1.refs_1_
  52.5 0.0 copy-start.2
  52.5 0.0 collective-permute-done.2.refs_3_
  52.5 0.0 copy-done.1
  52.5 0.0 copy-done
  52.5 4.0 %shard_map.112 = (bf16[4,6,32,512]{3,2,1,0:T(8,128)(2,1)S(1)}, bf16[2,8,104,128]{3,2,1,0:T(8,128)(2,1)S(1)}) custom-call(s32[1]{0:T(128)} %bitcast.dp_ref, bf16[4,8,104,128]{3,2,1,0:T(8,128)(2,1)S(1)} %bitcast.11, bf16[2,384,512]{2,1,0:T(8,128)(2,1)S(1)} %copy-done, bf16[2,384,512]{2,1,0:T(8,128)(2,1)S(1)} %collective-permute-done.1.refs_1_, ...), custom_call_target="tpu_custom_call" | custom-call | tf_op jit(solution)/shard_map/pallas_call | solution.py:271
  56.5 0.0 copy-done.2
  56.5 0.0 copy-start.8
  56.6 0.7 copy-done.8
  57.3 16.7 %all_to_all.20 = bf16[4,6,32,512]{3,2,1,0:T(8,128)(2,1)S(1)} all-to-all(bf16[4,6,32,512]{3,2,1,0:T(8,128)(2,1)S(1)} %get-tuple-element.9), channel_id=1, replica_groups=mesh['x'=4,'zh'=2,'c'=2,'zl'=8,'y'=4] {'x'}, dimensions={0} | all-to-all | bytes 1572864 | tf_op jit(solution)/shard_map/all_to_all | solution.py:278
  74.0 0.1 reduce_sum.45
  74.1 23.4 %all-gather.1 = bf16[12,32,512]{2,1,0:T(8,128)(2,1)S(1)} all-gather(bf16[6,32,512]{2,1,0:T(8,128)(2,1)S(1)} %reduce_sum.45), channel_id=3, replica_groups=mesh['x'=4,'zh'=2,'c'=2,'zl'=8,'y'=4] {'zh'}, dimensions={0}, use_global_device_ids=true | all-gather | bytes 589824 | tf_op jit(solution)/shard_map/all_gather | solution.py:280
  97.6 0.1 convert_reduce_fusion
  97.6 0.1 fusion
  97.7 0.0 copy-start.3
  97.8 13.4 %all_gather.20.mine_ref = bf16[4,6,32,512]{3,2,1,0:T(8,128)(2,1)S(1)} all-gather(bf16[1,6,32,512]{3,2,1,0:T(8,128)(2,1)S(1)} %pad_maximum_fusion), channel_id=1, replica_groups=mesh['x'=4,'zh'=2,'c'=2,'zl'=8,'y'=4] {'x'}, dimensions={0}, use_global_device_ids=true | all-gather | bytes 983040 | tf_op jit(solution)/shard_map/all_gather | solution.py:288
  111.2 1.9 %collective-permute-start.6 = (bf16[4,6,32,512]{3,2,1,0:T(8,128)(2,1)S(1)}, bf16[4,6,32,512]{3,2,1,0:T(8,128)(2,1)}, u32[]{:S(2)}, u32[]{:S(2)}) collective-permute-start(bf16[4,6,32,512]{3,2,1,0:T(8,128)(2,1)S(1)} %all_gather.20.mine_ref), channel_id=1, source_target_pairs={{0,32},{32,0},{1,33},{33,1},{2,34},{34,2},{3,35},{35,3},{4,36},{36... | collective-permute-start | bytes 2359304 | tf_op jit(solution)/shard_map/ppermute | solution.py:289
  113.1 0.0 copy-done.3
  113.1 2.3 %shard_map.113 = bf16[4,8,48,128]{3,2,1,0:T(8,128)(2,1)S(1)} custom-call(s32[1]{0:T(128)} %bitcast.dp_ref, bf16[4,6,32,512]{3,2,1,0:T(8,128)(2,1)S(1)} %all_gather.20.mine_ref, bf16[2,384,512]{2,1,0:T(8,128)(2,1)S(1)} %copy-done, bf16[2,384,512]{2,1,0:T(8,128)(2,1)S(1)} %copy-done.3, bf16[2,384,512]{2,1,0:T(8,128)(2,1)S(1)} %copy-done.1, ...), custom_call_target="tpu_custom_call" | custom-call | tf_op jit(solution)/shard_map/pallas_call | solution.py:292
  115.5 0.0 copy-start.4
  115.5 0.7 copy-done.4
  116.2 0.0 copy-start.9
  116.2 3.6 %all-to-all-start.2 = ((bf16[4,8,48,128]{3,2,1,0:T(8,128)(2,1)}), bf16[4,8,48,128]{3,2,1,0:T(8,128)(2,1)S(1)}, u32[]{:S(2)}, u32[]{:S(2)}) async-start(bf16[4,8,48,128]{3,2,1,0:T(8,128)(2,1)} %copy-done.4), calls=%async_computation.2 | async-start | bytes 786432 | tf_op jit(solution)/shard_map/all_to_all | solution.py:295
  119.8 0.0 copy-done.9
  119.8 2.4 %collective-permute-start.5 = (bf16[2,8,104,128]{3,2,1,0:T(8,128)(2,1)S(1)}, bf16[2,8,104,128]{3,2,1,0:T(8,128)(2,1)S(1)}, u32[]{:S(2)}, u32[]{:S(2)}) collective-permute-start(bf16[2,8,104,128]{3,2,1,0:T(8,128)(2,1)S(1)} %copy-done.9), channel_id=1, source_target_pairs={{0,32},{32,0},{1,33},{33,1},{2,34},{34,2},{3,35},{35,3},{4,36},{36... | collective-permute-start | bytes 1277960 | tf_op jit(solution)/shard_map/ppermute | solution.py:277
  122.2 6.6 %all-to-all-done.2 = bf16[4,8,48,128]{3,2,1,0:T(8,128)(2,1)S(1)} async-done(((bf16[4,8,48,128]{3,2,1,0:T(8,128)(2,1)}), bf16[4,8,48,128]{3,2,1,0:T(8,128)(2,1)S(1)}, u32[]{:S(2)}, u32[]{:S(2)}) %all-to-all-start.2) | async-done | bytes 393248 | tf_op jit(solution)/shard_map/all_to_all | solution.py:295
  128.8 0.1 reduce_sum.47
  128.9 12.5 %all_to_all.21 = bf16[8,48,128]{2,1,0:T(8,128)(2,1)S(1)} all-to-all(bf16[8,48,128]{2,1,0:T(8,128)(2,1)S(1)} %reduce_sum.47), channel_id=1, replica_groups=mesh['x'=4,'zh'=2,'c'=2,'zl'=8,'y'=4] {'zl'}, dimensions={0} | all-to-all | bytes 196608 | tf_op jit(solution)/shard_map/all_to_all | solution.py:297
  141.4 0.0 copy-start.7
  141.4 3.0 %collective-permute-start.4 = (bf16[48,128]{1,0:T(8,128)(2,1)S(1)}, bf16[48,128]{1,0:T(8,128)(2,1)S(1)}, u32[]{:S(2)}, u32[]{:S(2)}) collective-permute-start(bf16[48,128]{1,0:T(8,128)(2,1)S(1)} %reduce_sum.48), channel_id=1, source_target_pairs={{12,0},{13,1},{14,2},{15,3},{80,4},{81,5},{82,6},{83,7},{132,8},{1... | collective-permute-start | bytes 36872 | tf_op jit(solution)/shard_map/ppermute | solution.py:299
  144.5 7.4 %collective-permute-done.4.rows_ref = bf16[48,128]{1,0:T(8,128)(2,1)S(1)} collective-permute-done((bf16[48,128]{1,0:T(8,128)(2,1)S(1)}, bf16[48,128]{1,0:T(8,128)(2,1)S(1)}, u32[]{:S(2)}, u32[]{:S(2)}) %collective-permute-start.4) | collective-permute-done | bytes 12320 | tf_op jit(solution)/shard_map/ppermute | solution.py:299
  151.8 0.0 copy-done.7
  151.8 0.8 shard_map.114
  152.6 0.0 collective-permute-done.5.lent_ref
  152.6 0.0 copy-start.5
  152.6 0.8 copy-done.5
  153.4 0.0 collective-permute-done.6.other_ref
  153.4 0.0 copy-start.6
  153.4 1.0 copy-done.6
  154.4 3.7 %shard_map.115 = (bf16[2,384,512]{2,1,0:T(8,128)(2,1)}, bf16[2,384,512]{2,1,0:T(8,128)(2,1)}, bf16[2,512,384]{2,1,0:T(8,128)(2,1)}) custom-call(s32[1]{0:T(128)} %bitcast.dp_ref, bf16[4,8,104,128]{3,2,1,0:T(8,128)(2,1)S(1)} %bitcast.12, bf16[2,8,104,128]{3,2,1,0:T(8,128)(2,1)S(1)} %copy-done.6, bf16[4,6,32,512]{3,2,1,0:T(8,128)(2,1)S(1)} %all_gather.20.mine_ref, ...), custom_call_target="tpu_custom_call" | custom-call | tf_op jit(solution)/shard_map/pallas_call | solution.py:301
  (2 shorter events, 0.0 us)
Async XLA Ops:
  1.8 13.8 %collective-permute-start = (bf16[104,128]{1,0:T(8,128)(2,1)S(1)}, bf16[104,128]{1,0:T(8,128)(2,1)S(1)}, u32[]{:S(2)}, u32[]{:S(2)}) collective-permute-start(bf16[104,128]{1,0:T(8,128)(2,1)S(1)} %shard_map.111), channel_id=1, source_target_pairs={{0,12},{1,13},{2,14},{3,15},{4,80},{5,81},{6,82},{7,83},{8,132},{9... | collective-permute-start | bytes 79880 | tf_op jit(solution)/shard_map/ppermute | solution.py:262
  15.6 36.9 %copy-start.1 = (bf16[2,384,512]{2,1,0:T(8,128)(2,1)S(1)}, bf16[2,384,512]{2,1,0:T(8,128)(2,1)}, u32[]{:S(2)}) copy-start(bf16[2,384,512]{2,1,0:T(8,128)(2,1)} %refs_2_.3) | copy-start | bytes 2359300
  16.3 36.2 %copy-start = (bf16[2,384,512]{2,1,0:T(8,128)(2,1)S(1)}, bf16[2,384,512]{2,1,0:T(8,128)(2,1)}, u32[]{:S(2)}) copy-start(bf16[2,384,512]{2,1,0:T(8,128)(2,1)} %refs_0_.3) | copy-start | bytes 2359300
  16.3 21.7 %all-to-all-start = ((bf16[8,104,128]{2,1,0:T(8,128)(2,1)}), bf16[8,104,128]{2,1,0:T(8,128)(2,1)S(1)}, u32[]{:S(2)}, u32[]{:S(2)}) async-start(bf16[8,104,128]{2,1,0:T(8,128)(2,1)} %broadcast_in_dim.2), calls=%async_computation | async-start | bytes 425984 | tf_op jit(solution)/shard_map/all_to_all | solution.py:268
  24.9 27.6 %collective-permute-start.3 = (bf16[2,512,384]{2,1,0:T(8,128)(2,1)}, bf16[2,512,384]{2,1,0:T(8,128)(2,1)}, u32[]{:S(2)}, u32[]{:S(2)}) collective-permute-start(bf16[2,512,384]{2,1,0:T(8,128)(2,1)} %refs_4_.1), channel_id=1, source_target_pairs={{0,32},{32,0},{1,33},{33,1},{2,34},{34,2},{3,35},{35,3},{4,36},{36... | collective-permute-start | bytes 2359304 | tf_op jit(solution)/shard_map/ppermute | solution.py:264
  26.8 25.6 %collective-permute-start.1 = (bf16[2,384,512]{2,1,0:T(8,128)(2,1)}, bf16[2,384,512]{2,1,0:T(8,128)(2,1)S(1)}, u32[]{:S(2)}, u32[]{:S(2)}) collective-permute-start(bf16[2,384,512]{2,1,0:T(8,128)(2,1)} %refs_0_.3), channel_id=1, source_target_pairs={{0,32},{32,0},{1,33},{33,1},{2,34},{34,2},{3,35},{35,3},{4,36},{36... | collective-permute-start | bytes 2359304 | tf_op jit(solution)/shard_map/ppermute | solution.py:264
  29.2 23.2 %collective-permute-start.2 = (bf16[2,384,512]{2,1,0:T(8,128)(2,1)}, bf16[2,384,512]{2,1,0:T(8,128)(2,1)}, u32[]{:S(2)}, u32[]{:S(2)}) collective-permute-start(bf16[2,384,512]{2,1,0:T(8,128)(2,1)} %refs_2_.3), channel_id=1, source_target_pairs={{0,32},{32,0},{1,33},{33,1},{2,34},{34,2},{3,35},{35,3},{4,36},{36... | collective-permute-start | bytes 2359304 | tf_op jit(solution)/shard_map/ppermute | solution.py:264
  52.5 4.1 %copy-start.2 = (bf16[2,384,512]{2,1,0:T(8,128)(2,1)}, bf16[2,384,512]{2,1,0:T(8,128)(2,1)S(1)}, u32[]{:S(2)}) copy-start(bf16[2,384,512]{2,1,0:T(8,128)(2,1)S(1)} %collective-permute-done.1.refs_1_) | copy-start | bytes 2359300
  56.5 0.8 copy-start.8
  97.7 15.4 %copy-start.3 = (bf16[2,384,512]{2,1,0:T(8,128)(2,1)S(1)}, bf16[2,384,512]{2,1,0:T(8,128)(2,1)}, u32[]{:S(2)}) copy-start(bf16[2,384,512]{2,1,0:T(8,128)(2,1)} %copy-done.2) | copy-start | bytes 2359300
  111.2 42.2 %collective-permute-start.6 = (bf16[4,6,32,512]{3,2,1,0:T(8,128)(2,1)S(1)}, bf16[4,6,32,512]{3,2,1,0:T(8,128)(2,1)}, u32[]{:S(2)}, u32[]{:S(2)}) collective-permute-start(bf16[4,6,32,512]{3,2,1,0:T(8,128)(2,1)S(1)} %all_gather.20.mine_ref), channel_id=1, source_target_pairs={{0,32},{32,0},{1,33},{33,1},{2,34},{34,2},{3,35},{35,3},{4,36},{36... | collective-permute-start | bytes 2359304 | tf_op jit(solution)/shard_map/ppermute | solution.py:289
  115.5 0.7 copy-start.4
  116.2 3.6 %copy-start.9 = (bf16[2,8,104,128]{3,2,1,0:T(8,128)(2,1)S(1)}, bf16[2,8,104,128]{3,2,1,0:T(8,128)(2,1)}, u32[]{:S(2)}) copy-start(bf16[2,8,104,128]{3,2,1,0:T(8,128)(2,1)} %copy-done.8) | copy-start | bytes 1277956
  116.2 12.6 %all-to-all-start.2 = ((bf16[4,8,48,128]{3,2,1,0:T(8,128)(2,1)}), bf16[4,8,48,128]{3,2,1,0:T(8,128)(2,1)S(1)}, u32[]{:S(2)}, u32[]{:S(2)}) async-start(bf16[4,8,48,128]{3,2,1,0:T(8,128)(2,1)} %copy-done.4), calls=%async_computation.2 | async-start | bytes 786432 | tf_op jit(solution)/shard_map/all_to_all | solution.py:295
  119.8 32.8 %collective-permute-start.5 = (bf16[2,8,104,128]{3,2,1,0:T(8,128)(2,1)S(1)}, bf16[2,8,104,128]{3,2,1,0:T(8,128)(2,1)S(1)}, u32[]{:S(2)}, u32[]{:S(2)}) collective-permute-start(bf16[2,8,104,128]{3,2,1,0:T(8,128)(2,1)S(1)} %copy-done.9), channel_id=1, source_target_pairs={{0,32},{32,0},{1,33},{33,1},{2,34},{34,2},{3,35},{35,3},{4,36},{36... | collective-permute-start | bytes 1277960 | tf_op jit(solution)/shard_map/ppermute | solution.py:277
  141.4 10.4 %copy-start.7 = (s32[2,16]{1,0:T(2,128)S(1)}, s32[2,16]{1,0:T(2,128)}, u32[]{:S(2)}) copy-start(s32[2,16]{1,0:T(2,128)} %slot_ref.1) | copy-start | bytes 388
  141.4 10.4 %collective-permute-start.4 = (bf16[48,128]{1,0:T(8,128)(2,1)S(1)}, bf16[48,128]{1,0:T(8,128)(2,1)S(1)}, u32[]{:S(2)}, u32[]{:S(2)}) collective-permute-start(bf16[48,128]{1,0:T(8,128)(2,1)S(1)} %reduce_sum.48), channel_id=1, source_target_pairs={{12,0},{13,1},{14,2},{15,3},{80,4},{81,5},{82,6},{83,7},{132,8},{1... | collective-permute-start | bytes 36872 | tf_op jit(solution)/shard_map/ppermute | solution.py:299
  152.6 0.8 copy-start.5
  153.4 1.0 copy-start.6

commit v5 on v4

--- a/solution.py
+++ b/solution.py
@@ -130,33 +130,59 @@
     return lambda h, column: got_ref.at[2 * half + h, column]
 
 
-def forward_kernel(dp_ref, got_ref, *refs):
-    *weights, out_ref, loan_ref, down_a, down_b, sems = refs
+def forward_kernel(
+    dp_ref,
+    got_ref,
+    gate_ref,
+    up_ref,
+    gate_hbm,
+    up_hbm,
+    down_hbm,
+    far_down_hbm,
+    out_ref,
+    loan_ref,
+    far_gate,
+    far_up,
+    down_ref,
+    far_down,
+    sems,
+):
     moves = [
-        pltpu.make_async_copy(weights[4 + i], target, sems.at[i])
-        for i, target in enumerate((down_a, down_b))
+        pltpu.make_async_copy(source, target, sems.at[i])
+        for i, (source, target) in enumerate(
+            (
+                (gate_hbm, far_gate),
+                (up_hbm, far_up),
+                (down_hbm, down_ref),
+                (far_down_hbm, far_down),
+            )
+        )
     ]
     for move in moves:
         move.start()
     slots = Slots(dp_ref)
 
-    def give(t, e, rows, pair, dims):
-        part = dot(rows[0], pair[0][e], dims) + dot(rows[1], pair[1][e], dims)
+    def give(t, e, part):
         out_ref[:, 2 * t + e] = part.astype(BF16).reshape(X, ZH * R, 512)
 
     def both(m, e):
         return [features(lines_of(got_ref, half), slots, m, e) for half in slots.halves()]
 
-    for e in range(2):
-        rows = both(0, e)
-        give(0, e, rows, weights[0:2], ((1,), (0,)))
-        give(1, e, rows, weights[2:4], ((1,), (0,)))
+    rows = [both(0, e) for e in range(2)]
+    inward = ((1,), (0,))
+    near = [[dot(rows[e][0], ref[e], inward) for e in range(2)] for ref in (gate_ref, up_ref)]
+    for t, ref in enumerate((far_gate, far_up)):
+        moves[t].wait()
+        for e in range(2):
+            give(t, e, near[t][e] + dot(rows[e][1], ref[e], inward))
     for h in range(2):
         loan_ref[h] = got_ref[2 * (1 - slots.core) + h]
-    for move in moves:
-        move.wait()
+    moves[2].wait()
+    moves[3].wait()
     for e in range(2):
-        give(2, e, both(1, e), (down_a, down_b), ((1,), (1,)))
+        rows = both(1, e)
+        across = ((1,), (1,))
+        give(2, e, dot(rows[0], down_ref[e], across) + dot(rows[1], far_down[e], across))
 
 
 def all_rows(refs, t, e):
@@ -229,7 +255,7 @@
     if stay:
         shapes = [pltpu.VMEM(o, BF16) for o in outs]
     else:
-        shapes = [jax.ShapeDtypeStruct(o, BF16) for o in outs]
+        shapes = [pltpu.HBM(o, BF16) for o in outs]
     return pl.pallas_call(
         kernel,
         in_specs=specs,
@@ -260,20 +286,18 @@
     )
     swap = [(0, 1), (1, 0)]
     message = lax.ppermute(message, EVERY, outward())
-    pairs = [
-        (place(w), place(lax.ppermute(w, "c", swap)))
-        for w, place in ((gate_proj, in_vmem), (up_proj, in_vmem), (down_proj, in_hbm))
-    ]
+    far = [lax.ppermute(w, "c", swap) for w in (gate_proj, up_proj, down_proj)]
+    gate, up = in_vmem(gate_proj), in_vmem(up_proj)
     copies = jnp.broadcast_to(message[None], (ZL, MESSAGE, 128))
     column = lax.all_to_all(copies, "zl", 0, 0, tiled=True)
     got = in_vmem(lax.all_gather(column, "y", axis=0, tiled=False))
 
-    parts, loan = local(
+    parts, loan, far_gate, far_up = local(
         forward_kernel,
-        [SM] + [VM] * 5 + [HB] * 2,
-        [(X, 6, ZH * R, 512), (2, ZL, MESSAGE, 128)],
-        scratch=[pltpu.VMEM(down_proj.shape, BF16)] * 2 + [pltpu.SemaphoreType.DMA((2,))],
-    )(dp, got, *pairs[0], *pairs[1], *pairs[2])
+        [SM] + [VM] * 3 + [HB] * 4,
+        [(X, 6, ZH * R, 512), (2, ZL, MESSAGE, 128), gate.shape, up.shape],
+        scratch=[pltpu.VMEM(down_proj.shape, BF16)] * 2 + [pltpu.SemaphoreType.DMA((4,))],
+    )(dp, got, gate, up, *(in_hbm(w) for w in (far[0], far[1], down_proj, far[2])))
     lent = lax.ppermute(loan, "c", swap)
     over_x = lax.all_to_all(parts, "x", 0, 0, tiled=True)
     over_x = jnp.sum(over_x.astype(F32), axis=0).astype(BF16)
@@ -290,7 +314,7 @@
     mine = in_vmem(mine)
 
     (back,) = local(back_kernel, [SM] + [VM] * 5, [(Y, ZL, PACK, 128)], False)(
-        dp, mine, *pairs[0], *pairs[1]
+        dp, mine, gate, far_gate, up, far_up
     )
     over_y = lax.all_to_all(back, "y", 0, 0, tiled=True)
     over_y = jnp.sum(over_y.astype(F32), axis=0).astype(BF16)

time: 159 us -> 158 us (level)
  Pallas kernels: 12 us -> 10.3 us
where the time goes in v5:
time: 158 us; the launch traced here: 157 us
  blocking collectives  80.7 us (51%)
  starting transfers between devices  38.1 us (24%)
  waiting for transfers between devices  22.2 us (14%)
  Pallas kernels  10.3 us (7%)
  local copies, waits for them, and re-layouts  3.23 us (2%)
    all_gather x1, blocking collectives, layer(): over_zh = lax.all_gather(over_x, 'zh', axis=0, tiled=False)  23.4 us
    all_to_all x1, blocking collectives, layer(): over_x = lax.all_to_all(parts, 'x', 0, 0, tiled=True)  16.8 us
    all_gather x1, blocking collectives, layer(): got = in_vmem(lax.all_gather(column, 'y', axis=0, tiled=False))  14.5 us
    all_gather x1, blocking collectives, layer(): mine = lax.all_gather(acts, 'x', axis=0, tiled=False)  13.4 us
    all_to_all x1, blocking collectives, layer(): over_zl = lax.all_to_all(over_y, 'zl', 0, 0, tiled=True)  12.5 us
    ppermute x1, starting transfers between devices, layer(): message = lax.ppermute(message, EVERY, outward())  12.3 us
    all_to_all x1, starting transfers between devices, layer(): column = lax.all_to_all(copies, 'zl', 0, 0, tiled=True)  8.6 us
    ppermute x1, waiting for transfers between devices, layer(): home = lax.ppermute(over_zl, EVERY, homeward())  7.37 us
  transfers between devices with their start and end apart: 9, of which 4 were waited for; matrix products, arithmetic and copies ran while one was open for 0% of the time, Pallas kernels for 2%

profile of v5, /device:TPU:32, one launch (start us, length us, event | category | flops | bytes accessed | tf_op | source)
XLA Modules:
  0.0 156.9 jit_solution(3784630006113728946)
XLA Ops:
  0.6 1.1 shard_map.111
  1.8 12.3 %collective-permute-start = (bf16[104,128]{1,0:T(8,128)(2,1)S(1)}, bf16[104,128]{1,0:T(8,128)(2,1)S(1)}, u32[]{:S(2)}, u32[]{:S(2)}) collective-permute-start(bf16[104,128]{1,0:T(8,128)(2,1)S(1)} %shard_map.111), channel_id=1, source_target_pairs={{0,12},{1,13},{2,14},{3,15},{4,80},{5,81},{6,82},{7,83},{8,132},{9... | collective-permute-start | bytes 79880 | tf_op jit(solution)/shard_map/ppermute | solution.py:288
  14.1 1.5 collective-permute-done
  15.6 0.0 copy-start.1
  15.6 0.7 broadcast_in_dim.2
  16.3 0.0 copy-start
  16.3 8.6 %all-to-all-start = ((bf16[8,104,128]{2,1,0:T(8,128)(2,1)}), bf16[8,104,128]{2,1,0:T(8,128)(2,1)S(1)}, u32[]{:S(2)}, u32[]{:S(2)}) async-start(bf16[8,104,128]{2,1,0:T(8,128)(2,1)} %broadcast_in_dim.2), calls=%async_computation | async-start | bytes 425984 | tf_op jit(solution)/shard_map/all_to_all | solution.py:292
  24.9 1.9 %collective-permute-start.3 = (bf16[2,512,384]{2,1,0:T(8,128)(2,1)}, bf16[2,512,384]{2,1,0:T(8,128)(2,1)S(1)}, u32[]{:S(2)}, u32[]{:S(2)}) collective-permute-start(bf16[2,512,384]{2,1,0:T(8,128)(2,1)} %down_hbm.1), channel_id=1, source_target_pairs={{0,32},{32,0},{1,33},{33,1},{2,34},{34,2},{3,35},{35,3},{4,36},{36... | collective-permute-start | bytes 2359304 | tf_op jit(solution)/shard_map/ppermute | solution.py:289
  26.8 2.4 %collective-permute-start.1 = (bf16[2,384,512]{2,1,0:T(8,128)(2,1)}, bf16[2,384,512]{2,1,0:T(8,128)(2,1)}, u32[]{:S(2)}, u32[]{:S(2)}) collective-permute-start(bf16[2,384,512]{2,1,0:T(8,128)(2,1)} %refs_0_.1), channel_id=1, source_target_pairs={{0,32},{32,0},{1,33},{33,1},{2,34},{34,2},{3,35},{35,3},{4,36},{36... | collective-permute-start | bytes 2359304 | tf_op jit(solution)/shard_map/ppermute | solution.py:289
  29.2 1.9 %collective-permute-start.2 = (bf16[2,384,512]{2,1,0:T(8,128)(2,1)}, bf16[2,384,512]{2,1,0:T(8,128)(2,1)}, u32[]{:S(2)}, u32[]{:S(2)}) collective-permute-start(bf16[2,384,512]{2,1,0:T(8,128)(2,1)} %refs_2_.1), channel_id=1, source_target_pairs={{0,32},{32,0},{1,33},{33,1},{2,34},{34,2},{3,35},{35,3},{4,36},{36... | collective-permute-start | bytes 2359304 | tf_op jit(solution)/shard_map/ppermute | solution.py:289
  31.2 6.8 %all-to-all-done = bf16[8,104,128]{2,1,0:T(8,128)(2,1)S(1)} async-done(((bf16[8,104,128]{2,1,0:T(8,128)(2,1)}), bf16[8,104,128]{2,1,0:T(8,128)(2,1)S(1)}, u32[]{:S(2)}, u32[]{:S(2)}) %all-to-all-start) | async-done | bytes 213024 | tf_op jit(solution)/shard_map/all_to_all | solution.py:292
  38.0 14.5 %all-gather = bf16[32,104,128]{2,1,0:T(8,128)(2,1)S(1)} all-gather(bf16[8,104,128]{2,1,0:T(8,128)(2,1)S(1)} %all-to-all-done), channel_id=2, replica_groups=mesh['x'=4,'zh'=2,'c'=2,'zl'=8,'y'=4] {'y'}, dimensions={0}, use_global_device_ids=true | all-gather | bytes 1064960 | tf_op jit(solution)/shard_map/all_gather | solution.py:293
  52.4 0.0 collective-permute-done.3.far_down_hbm
  52.5 0.0 copy-start.9
  52.5 0.0 collective-permute-done.1.gate_hbm
  52.5 0.0 collective-permute-done.2.up_hbm
  52.5 0.9 copy-done.9
  53.3 0.0 copy-done.1
  53.3 0.0 copy-done
  53.3 2.8 %shard_map.112 = (bf16[4,6,32,512]{3,2,1,0:T(8,128)(2,1)S(1)}, bf16[2,8,104,128]{3,2,1,0:T(8,128)(2,1)S(1)}, bf16[2,384,512]{2,1,0:T(8,128)(2,1)S(1)}, bf16[2,384,512]{2,1,0:T(8,128)(2,1)S(1)}) custom-call(s32[1]{0:T(128)} %bitcast.dp_ref, bf16[4,8,104,128]{3,2,1,0:T(8,128)(2,1)S(1)} %bitcast.11, bf16[2,384,512]{2,1,0:T(8,128)(2,1)S(1)} %copy-done, ...), custom_call_target="tpu_custom_call" | custom-call | tf_op jit(solution)/shard_map/pallas_call | solution.py:295
  56.1 0.0 copy-start.2
  56.1 0.9 copy-done.2
  57.0 0.0 copy-start.7
  57.0 0.8 copy-done.7
  57.7 0.0 copy-start.4
  57.7 16.8 %all_to_all.20 = bf16[4,6,32,512]{3,2,1,0:T(8,128)(2,1)} all-to-all(bf16[4,6,32,512]{3,2,1,0:T(8,128)(2,1)S(1)} %get-tuple-element.11), channel_id=1, replica_groups=mesh['x'=4,'zh'=2,'c'=2,'zl'=8,'y'=4] {'x'}, dimensions={0} | all-to-all | bytes 1572864 | tf_op jit(solution)/shard_map/all_to_all | solution.py:302
  74.6 0.0 copy-done.4
  74.6 1.3 reduce_sum.45
  75.9 23.4 %all-gather.1 = bf16[12,32,512]{2,1,0:T(8,128)(2,1)S(1)} all-gather(bf16[6,32,512]{2,1,0:T(8,128)(2,1)S(1)} %reduce_sum.45), channel_id=3, replica_groups=mesh['x'=4,'zh'=2,'c'=2,'zl'=8,'y'=4] {'zh'}, dimensions={0}, use_global_device_ids=true | all-gather | bytes 589824 | tf_op jit(solution)/shard_map/all_gather | solution.py:304
  99.3 0.1 convert_reduce_fusion
  99.4 0.0 copy-start.5
  99.4 0.1 fusion
  99.5 0.0 copy-start.3
  99.5 13.4 %all_gather.20.mine_ref = bf16[4,6,32,512]{3,2,1,0:T(8,128)(2,1)S(1)} all-gather(bf16[1,6,32,512]{3,2,1,0:T(8,128)(2,1)S(1)} %pad_maximum_fusion), channel_id=1, replica_groups=mesh['x'=4,'zh'=2,'c'=2,'zl'=8,'y'=4] {'x'}, dimensions={0}, use_global_device_ids=true | all-gather | bytes 983040 | tf_op jit(solution)/shard_map/all_gather | solution.py:312
  112.9 1.9 %collective-permute-start.6 = (bf16[4,6,32,512]{3,2,1,0:T(8,128)(2,1)S(1)}, bf16[4,6,32,512]{3,2,1,0:T(8,128)(2,1)}, u32[]{:S(2)}, u32[]{:S(2)}) collective-permute-start(bf16[4,6,32,512]{3,2,1,0:T(8,128)(2,1)S(1)} %all_gather.20.mine_ref), channel_id=1, source_target_pairs={{0,32},{32,0},{1,33},{33,1},{2,34},{34,2},{3,35},{35,3},{4,36},{36... | collective-permute-start | bytes 2359304 | tf_op jit(solution)/shard_map/ppermute | solution.py:313
  114.9 0.0 copy-done.5
  114.9 0.0 copy-done.3
  114.9 1.9 %shard_map.113 = bf16[4,8,48,128]{3,2,1,0:T(8,128)(2,1)} custom-call(s32[1]{0:T(128)} %bitcast.dp_ref, bf16[4,6,32,512]{3,2,1,0:T(8,128)(2,1)S(1)} %all_gather.20.mine_ref, bf16[2,384,512]{2,1,0:T(8,128)(2,1)S(1)} %copy-done, bf16[2,384,512]{2,1,0:T(8,128)(2,1)S(1)} %copy-done.3, bf16[2,384,512]{2,1,0:T(8,128)(2,1)S(1)} %copy-done.1, ...), custom_call_target="tpu_custom_call" | custom-call | tf_op jit(solution)/shard_map/pallas_call | solution.py:316
  116.8 0.0 copy-start.8
  116.8 3.6 %all-to-all-start.2 = ((bf16[4,8,48,128]{3,2,1,0:T(8,128)(2,1)}), bf16[4,8,48,128]{3,2,1,0:T(8,128)(2,1)S(1)}, u32[]{:S(2)}, u32[]{:S(2)}) async-start(bf16[4,8,48,128]{3,2,1,0:T(8,128)(2,1)} %shard_map.113), calls=%async_computation.2 | async-start | bytes 786432 | tf_op jit(solution)/shard_map/all_to_all | solution.py:319
  120.4 0.0 copy-done.8
  120.4 2.4 %collective-permute-start.5 = (bf16[2,8,104,128]{3,2,1,0:T(8,128)(2,1)S(1)}, bf16[2,8,104,128]{3,2,1,0:T(8,128)(2,1)S(1)}, u32[]{:S(2)}, u32[]{:S(2)}) collective-permute-start(bf16[2,8,104,128]{3,2,1,0:T(8,128)(2,1)S(1)} %copy-done.8), channel_id=1, source_target_pairs={{0,32},{32,0},{1,33},{33,1},{2,34},{34,2},{3,35},{35,3},{4,36},{36... | collective-permute-start | bytes 1277960 | tf_op jit(solution)/shard_map/ppermute | solution.py:301
  122.9 6.6 %all-to-all-done.2 = bf16[4,8,48,128]{3,2,1,0:T(8,128)(2,1)S(1)} async-done(((bf16[4,8,48,128]{3,2,1,0:T(8,128)(2,1)}), bf16[4,8,48,128]{3,2,1,0:T(8,128)(2,1)S(1)}, u32[]{:S(2)}, u32[]{:S(2)}) %all-to-all-start.2) | async-done | bytes 393248 | tf_op jit(solution)/shard_map/all_to_all | solution.py:319
  129.4 0.1 reduce_sum.47
  129.5 12.5 %all_to_all.21 = bf16[8,48,128]{2,1,0:T(8,128)(2,1)S(1)} all-to-all(bf16[8,48,128]{2,1,0:T(8,128)(2,1)S(1)} %reduce_sum.47), channel_id=1, replica_groups=mesh['x'=4,'zh'=2,'c'=2,'zl'=8,'y'=4] {'zl'}, dimensions={0} | all-to-all | bytes 196608 | tf_op jit(solution)/shard_map/all_to_all | solution.py:321
  142.0 0.0 copy-start.6
  142.0 3.0 %collective-permute-start.4 = (bf16[48,128]{1,0:T(8,128)(2,1)S(1)}, bf16[48,128]{1,0:T(8,128)(2,1)S(1)}, u32[]{:S(2)}, u32[]{:S(2)}) collective-permute-start(bf16[48,128]{1,0:T(8,128)(2,1)S(1)} %reduce_sum.48), channel_id=1, source_target_pairs={{12,0},{13,1},{14,2},{15,3},{80,4},{81,5},{82,6},{83,7},{132,8},{1... | collective-permute-start | bytes 36872 | tf_op jit(solution)/shard_map/ppermute | solution.py:323
  145.1 7.4 %collective-permute-done.4.rows_ref = bf16[48,128]{1,0:T(8,128)(2,1)S(1)} collective-permute-done((bf16[48,128]{1,0:T(8,128)(2,1)S(1)}, bf16[48,128]{1,0:T(8,128)(2,1)S(1)}, u32[]{:S(2)}, u32[]{:S(2)}) %collective-permute-start.4) | collective-permute-done | bytes 12320 | tf_op jit(solution)/shard_map/ppermute | solution.py:323
  152.4 0.0 copy-done.6
  152.4 0.8 shard_map.114
  153.2 0.0 collective-permute-done.5.lent_ref
  153.2 0.0 collective-permute-done.6.other_ref
  153.3 3.7 %shard_map.115 = (bf16[2,384,512]{2,1,0:T(8,128)(2,1)}, bf16[2,384,512]{2,1,0:T(8,128)(2,1)}, bf16[2,512,384]{2,1,0:T(8,128)(2,1)}) custom-call(s32[1]{0:T(128)} %bitcast.dp_ref, bf16[4,8,104,128]{3,2,1,0:T(8,128)(2,1)S(1)} %bitcast.12, bf16[2,8,104,128]{3,2,1,0:T(8,128)(2,1)S(1)} %collective-permute-done.5.lent_ref, ...), custom_call_target="tpu_custom_call" | custom-call | tf_op jit(solution)/shard_map/pallas_call | solution.py:325
  (2 shorter events, 0.0 us)
Async XLA Ops:
  1.8 13.8 %collective-permute-start = (bf16[104,128]{1,0:T(8,128)(2,1)S(1)}, bf16[104,128]{1,0:T(8,128)(2,1)S(1)}, u32[]{:S(2)}, u32[]{:S(2)}) collective-permute-start(bf16[104,128]{1,0:T(8,128)(2,1)S(1)} %shard_map.111), channel_id=1, source_target_pairs={{0,12},{1,13},{2,14},{3,15},{4,80},{5,81},{6,82},{7,83},{8,132},{9... | collective-permute-start | bytes 79880 | tf_op jit(solution)/shard_map/ppermute | solution.py:288
  15.6 37.8 %copy-start.1 = (bf16[2,384,512]{2,1,0:T(8,128)(2,1)S(1)}, bf16[2,384,512]{2,1,0:T(8,128)(2,1)}, u32[]{:S(2)}) copy-start(bf16[2,384,512]{2,1,0:T(8,128)(2,1)} %refs_2_.1) | copy-start | bytes 2359300
  16.3 37.0 %copy-start = (bf16[2,384,512]{2,1,0:T(8,128)(2,1)S(1)}, bf16[2,384,512]{2,1,0:T(8,128)(2,1)}, u32[]{:S(2)}) copy-start(bf16[2,384,512]{2,1,0:T(8,128)(2,1)} %refs_0_.1) | copy-start | bytes 2359300
  16.3 21.7 %all-to-all-start = ((bf16[8,104,128]{2,1,0:T(8,128)(2,1)}), bf16[8,104,128]{2,1,0:T(8,128)(2,1)S(1)}, u32[]{:S(2)}, u32[]{:S(2)}) async-start(bf16[8,104,128]{2,1,0:T(8,128)(2,1)} %broadcast_in_dim.2), calls=%async_computation | async-start | bytes 425984 | tf_op jit(solution)/shard_map/all_to_all | solution.py:292
  24.9 27.6 %collective-permute-start.3 = (bf16[2,512,384]{2,1,0:T(8,128)(2,1)}, bf16[2,512,384]{2,1,0:T(8,128)(2,1)S(1)}, u32[]{:S(2)}, u32[]{:S(2)}) collective-permute-start(bf16[2,512,384]{2,1,0:T(8,128)(2,1)} %down_hbm.1), channel_id=1, source_target_pairs={{0,32},{32,0},{1,33},{33,1},{2,34},{34,2},{3,35},{35,3},{4,36},{36... | collective-permute-start | bytes 2359304 | tf_op jit(solution)/shard_map/ppermute | solution.py:289
  26.8 25.6 %collective-permute-start.1 = (bf16[2,384,512]{2,1,0:T(8,128)(2,1)}, bf16[2,384,512]{2,1,0:T(8,128)(2,1)}, u32[]{:S(2)}, u32[]{:S(2)}) collective-permute-start(bf16[2,384,512]{2,1,0:T(8,128)(2,1)} %refs_0_.1), channel_id=1, source_target_pairs={{0,32},{32,0},{1,33},{33,1},{2,34},{34,2},{3,35},{35,3},{4,36},{36... | collective-permute-start | bytes 2359304 | tf_op jit(solution)/shard_map/ppermute | solution.py:289
  29.2 23.2 %collective-permute-start.2 = (bf16[2,384,512]{2,1,0:T(8,128)(2,1)}, bf16[2,384,512]{2,1,0:T(8,128)(2,1)}, u32[]{:S(2)}, u32[]{:S(2)}) collective-permute-start(bf16[2,384,512]{2,1,0:T(8,128)(2,1)} %refs_2_.1), channel_id=1, source_target_pairs={{0,32},{32,0},{1,33},{33,1},{2,34},{34,2},{3,35},{35,3},{4,36},{36... | collective-permute-start | bytes 2359304 | tf_op jit(solution)/shard_map/ppermute | solution.py:289
  52.5 0.9 copy-start.9
  56.1 0.9 copy-start.2
  57.0 0.8 copy-start.7
  57.7 16.8 %copy-start.4 = (bf16[2,384,512]{2,1,0:T(8,128)(2,1)}, bf16[2,384,512]{2,1,0:T(8,128)(2,1)S(1)}, u32[]{:S(2)}) copy-start(bf16[2,384,512]{2,1,0:T(8,128)(2,1)S(1)} %get-tuple-element.13.refs_3_) | copy-start | bytes 2359300
  99.4 15.5 %copy-start.5 = (bf16[2,384,512]{2,1,0:T(8,128)(2,1)S(1)}, bf16[2,384,512]{2,1,0:T(8,128)(2,1)}, u32[]{:S(2)}) copy-start(bf16[2,384,512]{2,1,0:T(8,128)(2,1)} %copy-done.4) | copy-start | bytes 2359300
  99.5 15.4 %copy-start.3 = (bf16[2,384,512]{2,1,0:T(8,128)(2,1)S(1)}, bf16[2,384,512]{2,1,0:T(8,128)(2,1)}, u32[]{:S(2)}) copy-start(bf16[2,384,512]{2,1,0:T(8,128)(2,1)} %copy-done.2) | copy-start | bytes 2359300
  112.9 40.3 %collective-permute-start.6 = (bf16[4,6,32,512]{3,2,1,0:T(8,128)(2,1)S(1)}, bf16[4,6,32,512]{3,2,1,0:T(8,128)(2,1)}, u32[]{:S(2)}, u32[]{:S(2)}) collective-permute-start(bf16[4,6,32,512]{3,2,1,0:T(8,128)(2,1)S(1)} %all_gather.20.mine_ref), channel_id=1, source_target_pairs={{0,32},{32,0},{1,33},{33,1},{2,34},{34,2},{3,35},{35,3},{4,36},{36... | collective-permute-start | bytes 2359304 | tf_op jit(solution)/shard_map/ppermute | solution.py:313
  116.8 3.6 %copy-start.8 = (bf16[2,8,104,128]{3,2,1,0:T(8,128)(2,1)S(1)}, bf16[2,8,104,128]{3,2,1,0:T(8,128)(2,1)}, u32[]{:S(2)}) copy-start(bf16[2,8,104,128]{3,2,1,0:T(8,128)(2,1)} %copy-done.7) | copy-start | bytes 1277956
  116.8 12.6 %all-to-all-start.2 = ((bf16[4,8,48,128]{3,2,1,0:T(8,128)(2,1)}), bf16[4,8,48,128]{3,2,1,0:T(8,128)(2,1)S(1)}, u32[]{:S(2)}, u32[]{:S(2)}) async-start(bf16[4,8,48,128]{3,2,1,0:T(8,128)(2,1)} %shard_map.113), calls=%async_computation.2 | async-start | bytes 786432 | tf_op jit(solution)/shard_map/all_to_all | solution.py:319
  120.4 32.8 %collective-permute-start.5 = (bf16[2,8,104,128]{3,2,1,0:T(8,128)(2,1)S(1)}, bf16[2,8,104,128]{3,2,1,0:T(8,128)(2,1)S(1)}, u32[]{:S(2)}, u32[]{:S(2)}) collective-permute-start(bf16[2,8,104,128]{3,2,1,0:T(8,128)(2,1)S(1)} %copy-done.8), channel_id=1, source_target_pairs={{0,32},{32,0},{1,33},{33,1},{2,34},{34,2},{3,35},{35,3},{4,36},{36... | collective-permute-start | bytes 1277960 | tf_op jit(solution)/shard_map/ppermute | solution.py:301
  142.0 10.4 %copy-start.6 = (s32[2,16]{1,0:T(2,128)S(1)}, s32[2,16]{1,0:T(2,128)}, u32[]{:S(2)}) copy-start(s32[2,16]{1,0:T(2,128)} %slot_ref.1) | copy-start | bytes 388
  142.0 10.4 %collective-permute-start.4 = (bf16[48,128]{1,0:T(8,128)(2,1)S(1)}, bf16[48,128]{1,0:T(8,128)(2,1)S(1)}, u32[]{:S(2)}, u32[]{:S(2)}) collective-permute-start(bf16[48,128]{1,0:T(8,128)(2,1)S(1)} %reduce_sum.48), channel_id=1, source_target_pairs={{12,0},{13,1},{14,2},{15,3},{80,4},{81,5},{82,6},{83,7},{132,8},{1... | collective-permute-start | bytes 36872 | tf_op jit(solution)/shard_map/ppermute | solution.py:323

commit v6 on v5

--- a/solution.py
+++ b/solution.py
@@ -5,9 +5,11 @@
 from jax.experimental.pallas import tpu as pltpu
 from jax.sharding import Mesh, PartitionSpec as P
 
-X, ZH, C, ZL, Y = 4, 2, 2, 8, 4
+X, ZH, C, ZB, ZA, Y = 4, 2, 2, 2, 4, 4
+ZL = ZB * ZA
 DP = ("x", "zh", "c")
-SHARD = ("zl", "y")
+LINE = ("zb", "za")
+SHARD = LINE + ("y",)
 EVERY = DP + SHARD
 N_SHARD = ZL * Y
 HALF = 192
@@ -31,14 +33,15 @@
     return near | far
 
 
-def outward():
+def outward(flip=0):
     pairs = []
     for k in range(X * ZH * C):
         x, zh, c = k // 4, k // 2 % 2, k % 2
         for s in range(N_SHARD):
             zl, y = divmod(s, Y)
             there = zl * C + c
-            pairs.append((k * N_SHARD + s, there * N_SHARD + columns(zl)[(x, zh)] * Y + y))
+            column = columns(zl)[(x, zh)] ^ (ZA * flip)
+            pairs.append((k * N_SHARD + s, there * N_SHARD + column * Y + y))
     return pairs
 
 
@@ -47,16 +50,21 @@
 
 
 class Slots:
-    def __init__(self, dp_ref):
-        self.core = dp_ref[0] & 1
-        zl = dp_ref[0] >> 1
+    def __init__(self, here_ref):
+        self.zb = here_ref[0] & 1
+        self.core = here_ref[0] >> 1 & 1
+        zl = here_ref[0] >> 2
         self.code = sum(jnp.where(zl == i, code_of(i), 0) for i in range(ZL))
 
     def halves(self):
         return (self.core, 1 - self.core)
 
-    def column(self, j):
+    def home(self, j):
         return (self.code >> 3 * j) & 7
+
+    def got(self, j):
+        slot = self.home(j)
+        return (slot & 3) * 2 + ((slot >> 2) ^ self.zb)
 
 
 def homeward():
@@ -118,7 +126,7 @@
     for j in range(ZH * X):
         parts = []
         for h in range(2):
-            block = at(h, slots.column(j))
+            block = at(h, slots.got(j))
             parts.append(block[m * PACK + e * R : m * PACK + (e + 1) * R, :])
             left = block[m * PACK + 2 * R : (m + 1) * PACK, :]
             parts.append(left[:, e * 64 : (e + 1) * 64])
@@ -140,7 +148,6 @@
     down_hbm,
     far_down_hbm,
     out_ref,
-    loan_ref,
     far_gate,
     far_up,
     down_ref,
@@ -175,8 +182,6 @@
         moves[t].wait()
         for e in range(2):
             give(t, e, near[t][e] + dot(rows[e][1], ref[e], inward))
-    for h in range(2):
-        loan_ref[h] = got_ref[2 * (1 - slots.core) + h]
     moves[2].wait()
     moves[3].wait()
     for e in range(2):
@@ -185,23 +190,50 @@
         give(2, e, dot(rows[0], down_ref[e], across) + dot(rows[1], far_down[e], across))
 
 
+def loan_kernel(dp_ref, got_ref, out_ref):
+    slots = Slots(dp_ref)
+    for h in range(2):
+        out_ref[h] = got_ref[2 * (1 - slots.core) + h]
+
+
+def spread_kernel(one_ref, two_ref, out_ref):
+    for i in range(ZA):
+        out_ref[i, 0] = one_ref[...]
+        out_ref[i, 1] = two_ref[...]
+
+
+def fold_kernel(in_ref, out_ref):
+    total = sum(in_ref[i].astype(F32) for i in range(in_ref.shape[0]))
+    out_ref[...] = total.astype(BF16)
+
+
 def all_rows(refs, t, e):
     return jnp.concatenate([ref[:, 2 * t + e].reshape(ZH * X * R, 512) for ref in refs], axis=0)
 
 
-def back_kernel(dp_ref, mine_ref, *refs):
-    *weights, out_ref = refs
+def back_kernel(
+    dp_ref, mine_ref, gate_ref, up_ref, gate_hbm, up_hbm, out_ref, far_gate, far_up, sems
+):
+    moves = [
+        pltpu.make_async_copy(source, target, sems.at[i])
+        for i, (source, target) in enumerate(((gate_hbm, far_gate), (up_hbm, far_up)))
+    ]
+    for move in moves:
+        move.start()
     slots = Slots(dp_ref)
     grads = [[all_rows((mine_ref,), t, e) for t in (1, 2)] for e in range(2)]
-    for i, half in enumerate(slots.halves()):
+    for half, weights in zip(slots.halves(), ((gate_ref, up_ref), (far_gate, far_up))):
+        if weights[0] is far_gate:
+            for move in moves:
+                move.wait()
         terms = [
-            sum(dot(grads[e][t], weights[2 * t + i][e], ((1,), (1,))) for t in range(2)).astype(BF16)
+            sum(dot(grads[e][t], weights[t][e], ((1,), (1,))) for t in range(2)).astype(BF16)
             for e in range(2)
         ]
         for h in range(2):
             for j in range(ZH * X):
                 rows = [term[j * R : (j + 1) * R, h * HALF : (h + 1) * HALF] for term in terms]
-                out_ref[2 * half + h, slots.column(j)] = packed(rows)
+                out_ref[2 * half + h, slots.home(j)] = packed(rows)
 
 
 def weight_kernel(dp_ref, got_ref, lent_ref, mine_ref, other_ref, gate_out, up_out, down_out):
@@ -266,10 +298,15 @@
     )
 
 
+def folded(tiles):
+    (total,) = local(fold_kernel, [VM], [tiles.shape[1:]])(in_vmem(tiles))
+    return total
+
+
 def layer(
     tokens, cotangent, gate_proj, up_proj, down_proj, slot_tokens, gate_weights, live_counts
 ):
-    dp = lax.axis_index(DP).astype(jnp.int32).reshape(1)
+    dp = (lax.axis_index(DP) * ZB + lax.axis_index("zb")).astype(jnp.int32).reshape(1)
     scratch = [
         pltpu.VMEM(tokens.shape, BF16),
         pltpu.VMEM(cotangent.shape, BF16),
@@ -285,22 +322,25 @@
         )
     )
     swap = [(0, 1), (1, 0)]
-    message = lax.ppermute(message, EVERY, outward())
+    messages = [lax.ppermute(message, EVERY, outward(flip)) for flip in range(2)]
     far = [lax.ppermute(w, "c", swap) for w in (gate_proj, up_proj, down_proj)]
     gate, up = in_vmem(gate_proj), in_vmem(up_proj)
-    copies = jnp.broadcast_to(message[None], (ZL, MESSAGE, 128))
-    column = lax.all_to_all(copies, "zl", 0, 0, tiled=True)
+    (copies,) = local(spread_kernel, [VM] * 2, [(ZA, ZB, MESSAGE, 128)], False)(*messages)
+    column = lax.all_to_all(copies, "za", 0, 0, tiled=True).reshape(ZL, MESSAGE, 128)
     got = in_vmem(lax.all_gather(column, "y", axis=0, tiled=False))
 
-    parts, loan, far_gate, far_up = local(
+    (parts,) = local(
         forward_kernel,
         [SM] + [VM] * 3 + [HB] * 4,
-        [(X, 6, ZH * R, 512), (2, ZL, MESSAGE, 128), gate.shape, up.shape],
-        scratch=[pltpu.VMEM(down_proj.shape, BF16)] * 2 + [pltpu.SemaphoreType.DMA((4,))],
+        [(X, 6, ZH * R, 512)],
+        scratch=[pltpu.VMEM(gate.shape, BF16)] * 2
+        + [pltpu.VMEM(down_proj.shape, BF16)] * 2
+        + [pltpu.SemaphoreType.DMA((4,))],
     )(dp, got, gate, up, *(in_hbm(w) for w in (far[0], far[1], down_proj, far[2])))
+    (loan,) = local(loan_kernel, [SM, VM], [(2, ZL, MESSAGE, 128)])(dp, got)
     lent = lax.ppermute(loan, "c", swap)
     over_x = lax.all_to_all(parts, "x", 0, 0, tiled=True)
-    over_x = jnp.sum(over_x.astype(F32), axis=0).astype(BF16)
+    over_x = folded(over_x)
     over_zh = lax.all_gather(over_x, "zh", axis=0, tiled=False)
     sums = jnp.sum(over_zh.astype(F32), axis=0)
     gate_sum, up_sum, cot_hidden = sums[0:2], sums[2:4], sums[4:6]
@@ -313,12 +353,16 @@
     other = lax.ppermute(mine, "c", swap)
     mine = in_vmem(mine)
 
-    (back,) = local(back_kernel, [SM] + [VM] * 5, [(Y, ZL, PACK, 128)], False)(
-        dp, mine, gate, far_gate, up, far_up
-    )
+    (back,) = local(
+        back_kernel,
+        [SM] + [VM] * 3 + [HB] * 2,
+        [(Y, ZL, PACK, 128)],
+        False,
+        [pltpu.VMEM(gate.shape, BF16)] * 2 + [pltpu.SemaphoreType.DMA((2,))],
+    )(dp, mine, gate, up, in_hbm(far[0]), in_hbm(far[1]))
     over_y = lax.all_to_all(back, "y", 0, 0, tiled=True)
-    over_y = jnp.sum(over_y.astype(F32), axis=0).astype(BF16)
-    over_zl = lax.all_to_all(over_y, "zl", 0, 0, tiled=True)
+    over_y = folded(over_y)
+    over_zl = lax.all_to_all(over_y, LINE, 0, 0, tiled=True)
     over_zl = jnp.sum(over_zl.astype(F32), axis=0).astype(BF16)
     home = lax.ppermute(over_zl, EVERY, homeward())
     home = in_vmem(home)
@@ -333,7 +377,7 @@
 
 
 def solution(mesh):
-    fine = Mesh(mesh.devices.reshape(X, ZH, C, ZL, Y), EVERY)
+    fine = Mesh(mesh.devices.reshape(X, ZH, C, ZB, ZA, Y), EVERY)
     in_specs = (
         P(DP, SHARD),
         P(DP, SHARD),

time: 158 us -> 163 us (1.032)
  blocking collectives: 80.7 us -> 88.2 us
  waiting for transfers between devices: 22.2 us -> 17.4 us
  starting transfers between devices: 38.1 us -> 41.9 us
  Pallas kernels: 10.3 us -> 12.7 us
  local copies, waits for them, and re-layouts: 3.23 us -> 0.88 us
    all_to_all x1, blocking collectives: 12.5 us -> 24.8 us  [layer(): over_zl = lax.all_to_all(over_y, LINE, 0, 0, tiled=True)]
    all_to_all x1, waiting for transfers between devices: 6.79 us -> 0.01 us  [layer(): lax.all_to_all(copies, 'za', 0, 0, tiled=True).reshape(ZL, MESSAGE, 128)]
    ppermute x1 -> x2, starting transfers between devices: 12.3 us -> 18.4 us  [layer(): lax.ppermute(message, EVERY, outward(flip))]
    all_gather x1, blocking collectives: 23.4 us -> 17.4 us  [layer(): over_zh = lax.all_gather(over_x, 'zh', axis=0, tiled=False)]
    all_to_all x1, starting transfers between devices: 8.6 us -> 6.16 us  [layer(): lax.all_to_all(copies, 'za', 0, 0, tiled=True).reshape(ZL, MESSAGE, 128)]
    pallas_call x2 -> x6, Pallas kernels: 4.69 us -> 6.97 us  [the longest x1 3.35 us: layer(): local(back_kernel, [SM] + [VM] * 3 + [HB] * 2, [(Y, ZL, PACK, 128)], Fals...]
    unnamed x20 -> x8, local copies, waits for them, and re-layouts: 2.52 us -> 0.88 us
  transfers between devices with their start and end apart: 9 -> 10, of which waited for: 4 -> 4; matrix products, arithmetic and copies ran while one was open for 0% -> 0% of each run, Pallas kernels for 2% -> 3%
where the time goes in v6:
time: 163 us; the launch traced here: 162 us
  blocking collectives  88.2 us (54%)
  starting transfers between devices  41.9 us (26%)
  waiting for transfers between devices  17.4 us (11%)
  Pallas kernels  12.7 us (8%)
    all_to_all x1, blocking collectives, layer(): over_zl = lax.all_to_all(over_y, LINE, 0, 0, tiled=True)  24.8 us
    ppermute x2, starting transfers between devices, layer(): lax.ppermute(message, EVERY, outward(flip))  18.4 us
    all_to_all x1, blocking collectives, layer(): over_x = lax.all_to_all(parts, 'x', 0, 0, tiled=True)  18 us
    all_gather x1, blocking collectives, layer(): over_zh = lax.all_gather(over_x, 'zh', axis=0, tiled=False)  17.4 us
    all_gather x1, blocking collectives, layer(): got = in_vmem(lax.all_gather(column, 'y', axis=0, tiled=False))  14.6 us
    all_gather x1, blocking collectives, layer(): mine = lax.all_gather(acts, 'x', axis=0, tiled=False)  13.4 us
    ppermute x1, waiting for transfers between devices, layer(): home = lax.ppermute(over_zl, EVERY, homeward())  8.19 us
    all_to_all x1, waiting for transfers between devices, layer(): over_y = lax.all_to_all(back, 'y', 0, 0, tiled=True)  6.57 us
  transfers between devices with their start and end apart: 10, of which 4 were waited for; matrix products, arithmetic and copies ran while one was open for 0% of the time, Pallas kernels for 3%

profile of v6, /device:TPU:32, one launch (start us, length us, event | category | flops | bytes accessed | tf_op | source)
XLA Modules:
  0.0 162.1 jit_solution(1997251198442120959)
XLA Ops:
  0.6 0.0 copy-start
  0.6 1.2 shard_map.111
  1.9 14.4 %collective-permute-start.1 = (bf16[104,128]{1,0:T(8,128)(2,1)S(1)}, bf16[104,128]{1,0:T(8,128)(2,1)S(1)}, u32[]{:S(2)}, u32[]{:S(2)}) collective-permute-start(bf16[104,128]{1,0:T(8,128)(2,1)S(1)} %shard_map.111), channel_id=1, source_target_pairs={{0,28},{1,29},{2,30},{3,31},{4,64},{5,65},{6,66},{7,67},{8,148},{9... | collective-permute-start | bytes 79880 | tf_op jit(solution)/shard_map/ppermute | solution.py:325
  16.2 4.0 %collective-permute-start = (bf16[104,128]{1,0:T(8,128)(2,1)S(1)}, bf16[104,128]{1,0:T(8,128)(2,1)S(1)}, u32[]{:S(2)}, u32[]{:S(2)}) collective-permute-start(bf16[104,128]{1,0:T(8,128)(2,1)S(1)} %shard_map.111), channel_id=1, source_target_pairs={{0,12},{1,13},{2,14},{3,15},{4,80},{5,81},{6,82},{7,83},{8,132},{9... | collective-permute-start | bytes 79880 | tf_op jit(solution)/shard_map/ppermute | solution.py:325
  20.3 0.3 collective-permute-done.1.two_ref
  20.5 2.3 %collective-permute-done.one_ref = bf16[104,128]{1,0:T(8,128)(2,1)S(1)} collective-permute-done((bf16[104,128]{1,0:T(8,128)(2,1)S(1)}, bf16[104,128]{1,0:T(8,128)(2,1)S(1)}, u32[]{:S(2)}, u32[]{:S(2)}) %collective-permute-start) | collective-permute-done | bytes 26656 | tf_op jit(solution)/shard_map/ppermute | solution.py:325
  22.9 0.7 shard_map.112
  23.6 0.0 copy-start.1
  23.6 6.2 %all-to-all-start = ((bf16[4,2,104,128]{3,2,1,0:T(8,128)(2,1)}), bf16[4,2,104,128]{3,2,1,0:T(8,128)(2,1)S(1)}, u32[]{:S(2)}, u32[]{:S(2)}) async-start(bf16[4,2,104,128]{3,2,1,0:T(8,128)(2,1)} %shard_map.112), calls=%async_computation | async-start | bytes 425984 | tf_op jit(solution)/shard_map/all_to_all | solution.py:329
  29.7 1.9 %collective-permute-start.4 = (bf16[2,512,384]{2,1,0:T(8,128)(2,1)}, bf16[2,512,384]{2,1,0:T(8,128)(2,1)}, u32[]{:S(2)}, u32[]{:S(2)}) collective-permute-start(bf16[2,512,384]{2,1,0:T(8,128)(2,1)} %down_hbm.1), channel_id=1, source_target_pairs={{0,32},{32,0},{1,33},{33,1},{2,34},{34,2},{3,35},{35,3},{4,36},{36... | collective-permute-start | bytes 2359304 | tf_op jit(solution)/shard_map/ppermute | solution.py:326
  31.7 0.0 copy-done
  31.7 2.4 %collective-permute-start.2 = (bf16[2,384,512]{2,1,0:T(8,128)(2,1)S(1)}, bf16[2,384,512]{2,1,0:T(8,128)(2,1)S(1)}, u32[]{:S(2)}, u32[]{:S(2)}) collective-permute-start(bf16[2,384,512]{2,1,0:T(8,128)(2,1)S(1)} %copy-done), channel_id=1, source_target_pairs={{0,32},{32,0},{1,33},{33,1},{2,34},{34,2},{3,35},{35,3},{4,36},{36... | collective-permute-start | bytes 2359304 | tf_op jit(solution)/shard_map/ppermute | solution.py:326
  34.1 1.9 %collective-permute-start.3 = (bf16[2,384,512]{2,1,0:T(8,128)(2,1)}, bf16[2,384,512]{2,1,0:T(8,128)(2,1)}, u32[]{:S(2)}, u32[]{:S(2)}) collective-permute-start(bf16[2,384,512]{2,1,0:T(8,128)(2,1)} %up_ref.3), channel_id=1, source_target_pairs={{0,32},{32,0},{1,33},{33,1},{2,34},{34,2},{3,35},{35,3},{4,36},{36... | collective-permute-start | bytes 2359304 | tf_op jit(solution)/shard_map/ppermute | solution.py:326
  36.0 0.0 all-to-all-done
  36.0 14.6 %all_gather.13.got_ref = bf16[4,8,104,128]{3,2,1,0:T(8,128)(2,1)S(1)} all-gather(bf16[1,8,104,128]{3,2,1,0:T(8,128)(2,1)S(1)} %bitcast.12), channel_id=1, replica_groups=mesh['x'=4,'zh'=2,'c'=2,'zb'=2,'za'=4,'y'=4] {'y'}, dimensions={0}, use_global_device_ids=true | all-gather | bytes 1064960 | tf_op jit(solution)/shard_map/all_gather | solution.py:330
  50.7 0.0 collective-permute-done.4.far_down_hbm
  50.7 0.0 collective-permute-done.2.gate_hbm
  50.7 0.0 copy-start.3
  50.7 0.0 collective-permute-done.3.up_hbm
  50.7 0.9 copy-done.3
  51.6 0.0 copy-done.1
  51.6 2.7 %shard_map.113 = bf16[4,6,32,512]{3,2,1,0:T(8,128)(2,1)S(1)} custom-call(s32[1]{0:T(128)} %bitcast.dp_ref, bf16[4,8,104,128]{3,2,1,0:T(8,128)(2,1)S(1)} %all_gather.13.got_ref, bf16[2,384,512]{2,1,0:T(8,128)(2,1)S(1)} %copy-done, bf16[2,384,512]{2,1,0:T(8,128)(2,1)S(1)} %copy-done.1, bf16[2,384,512]{2,1,0:T(8,128)(2,1)} %copy-done.3, ...), custom_call_target="tpu_custom_call" | custom-call | tf_op jit(solution)/shard_map/pallas_call | solution.py:332
  54.3 18.0 %all_to_all.20.in_ref = bf16[4,6,32,512]{3,2,1,0:T(8,128)(2,1)S(1)} all-to-all(bf16[4,6,32,512]{3,2,1,0:T(8,128)(2,1)S(1)} %shard_map.113), channel_id=1, replica_groups=mesh['x'=4,'zh'=2,'c'=2,'zb'=2,'za'=4,'y'=4] {'x'}, dimensions={0} | all-to-all | bytes 1572864 | tf_op jit(solution)/shard_map/all_to_all | solution.py:342
  72.3 0.1 shard_map.114
  72.4 17.4 %all-gather = bf16[12,32,512]{2,1,0:T(8,128)(2,1)S(1)} all-gather(bf16[6,32,512]{2,1,0:T(8,128)(2,1)S(1)} %shard_map.114), channel_id=2, replica_groups=mesh['x'=4,'zh'=2,'c'=2,'zb'=2,'za'=4,'y'=4] {'zh'}, dimensions={0}, use_global_device_ids=true | all-gather | bytes 589824 | tf_op jit(solution)/shard_map/all_gather | solution.py:344
  89.8 0.1 convert_reduce_fusion
  89.8 0.1 fusion
  90.0 13.4 %all_gather.16.mine_ref = bf16[4,6,32,512]{3,2,1,0:T(8,128)(2,1)S(1)} all-gather(bf16[1,6,32,512]{3,2,1,0:T(8,128)(2,1)S(1)} %pad_maximum_fusion), channel_id=1, replica_groups=mesh['x'=4,'zh'=2,'c'=2,'zb'=2,'za'=4,'y'=4] {'x'}, dimensions={0}, use_global_device_ids=true | all-gather | bytes 983040 | tf_op jit(solution)/shard_map/all_gather | solution.py:352
  103.4 1.9 %collective-permute-start.7 = (bf16[4,6,32,512]{3,2,1,0:T(8,128)(2,1)S(1)}, bf16[4,6,32,512]{3,2,1,0:T(8,128)(2,1)}, u32[]{:S(2)}, u32[]{:S(2)}) collective-permute-start(bf16[4,6,32,512]{3,2,1,0:T(8,128)(2,1)S(1)} %all_gather.16.mine_ref), channel_id=1, source_target_pairs={{0,32},{32,0},{1,33},{33,1},{2,34},{34,2},{3,35},{35,3},{4,36},{36... | collective-permute-start | bytes 2359304 | tf_op jit(solution)/shard_map/ppermute | solution.py:353
  105.3 3.4 %shard_map.115 = bf16[4,8,48,128]{3,2,1,0:T(8,128)(2,1)} custom-call(s32[1]{0:T(128)} %bitcast.dp_ref, bf16[4,6,32,512]{3,2,1,0:T(8,128)(2,1)S(1)} %all_gather.16.mine_ref, bf16[2,384,512]{2,1,0:T(8,128)(2,1)S(1)} %copy-done, bf16[2,384,512]{2,1,0:T(8,128)(2,1)S(1)} %copy-done.1, bf16[2,384,512]{2,1,0:T(8,128)(2,1)} %copy-done.3, ...), custom_call_target="tpu_custom_call" | custom-call | tf_op jit(solution)/shard_map/pallas_call | solution.py:356
  108.7 4.9 %all-to-all-start.2 = ((bf16[4,8,48,128]{3,2,1,0:T(8,128)(2,1)}), bf16[4,8,48,128]{3,2,1,0:T(8,128)(2,1)S(1)}, u32[]{:S(2)}, u32[]{:S(2)}) async-start(bf16[4,8,48,128]{3,2,1,0:T(8,128)(2,1)} %shard_map.115), calls=%async_computation.2 | async-start | bytes 786432 | tf_op jit(solution)/shard_map/all_to_all | solution.py:363
  113.6 2.1 %collective-permute-start.6 = (bf16[2,8,104,128]{3,2,1,0:T(8,128)(2,1)S(1)}, bf16[2,8,104,128]{3,2,1,0:T(8,128)(2,1)S(1)}, u32[]{:S(2)}, u32[]{:S(2)}) collective-permute-start(bf16[2,8,104,128]{3,2,1,0:T(8,128)(2,1)S(1)} %shard_map.118), channel_id=1, source_target_pairs={{0,32},{32,0},{1,33},{33,1},{2,34},{34,2},{3,35},{35,3},{4,36},{36... | collective-permute-start | bytes 1277960 | tf_op jit(solution)/shard_map/ppermute | solution.py:341
  115.7 6.6 %all-to-all-done.2.in_ref = bf16[4,8,48,128]{3,2,1,0:T(8,128)(2,1)S(1)} async-done(((bf16[4,8,48,128]{3,2,1,0:T(8,128)(2,1)}), bf16[4,8,48,128]{3,2,1,0:T(8,128)(2,1)S(1)}, u32[]{:S(2)}, u32[]{:S(2)}) %all-to-all-start.2) | async-done | bytes 393248 | tf_op jit(solution)/shard_map/all_to_all | solution.py:363
  122.3 0.1 shard_map.116
  122.3 24.8 %all_to_all.21 = bf16[8,48,128]{2,1,0:T(8,128)(2,1)S(1)} all-to-all(bf16[8,48,128]{2,1,0:T(8,128)(2,1)S(1)} %shard_map.116), channel_id=1, replica_groups=mesh['x'=4,'zh'=2,'c'=2,'zb'=2,'za'=4,'y'=4] {'zb','za'}, dimensions={0} | all-to-all | bytes 196608 | tf_op jit(solution)/shard_map/all_to_all | solution.py:365
  147.1 0.0 copy-start.2
  147.2 2.2 %collective-permute-start.5 = (bf16[48,128]{1,0:T(8,128)(2,1)S(1)}, bf16[48,128]{1,0:T(8,128)(2,1)S(1)}, u32[]{:S(2)}, u32[]{:S(2)}) collective-permute-start(bf16[48,128]{1,0:T(8,128)(2,1)S(1)} %reduce_sum.22), channel_id=1, source_target_pairs={{12,0},{13,1},{14,2},{15,3},{80,4},{81,5},{82,6},{83,7},{132,8},{1... | collective-permute-start | bytes 36872 | tf_op jit(solution)/shard_map/ppermute | solution.py:367
  149.4 8.2 %collective-permute-done.5.rows_ref = bf16[48,128]{1,0:T(8,128)(2,1)S(1)} collective-permute-done((bf16[48,128]{1,0:T(8,128)(2,1)S(1)}, bf16[48,128]{1,0:T(8,128)(2,1)S(1)}, u32[]{:S(2)}, u32[]{:S(2)}) %collective-permute-start.5) | collective-permute-done | bytes 12320 | tf_op jit(solution)/shard_map/ppermute | solution.py:367
  157.6 0.0 copy-done.2
  157.6 0.8 shard_map.117
  158.4 0.0 collective-permute-done.6.lent_ref
  158.4 0.0 collective-permute-done.7.other_ref
  158.4 3.7 %shard_map.119 = (bf16[2,384,512]{2,1,0:T(8,128)(2,1)}, bf16[2,384,512]{2,1,0:T(8,128)(2,1)}, bf16[2,512,384]{2,1,0:T(8,128)(2,1)}) custom-call(s32[1]{0:T(128)} %bitcast.dp_ref, bf16[4,8,104,128]{3,2,1,0:T(8,128)(2,1)S(1)} %all_gather.13.got_ref, bf16[2,8,104,128]{3,2,1,0:T(8,128)(2,1)S(1)} %collective-permute-done.6.lent_ref, ...), custom_call_target="tpu_custom_call" | custom-call | tf_op jit(solution)/shard_map/pallas_call | solution.py:369
  (3 shorter events, 0.1 us)
Async XLA Ops:
  0.6 31.0 %copy-start = (bf16[2,384,512]{2,1,0:T(8,128)(2,1)S(1)}, bf16[2,384,512]{2,1,0:T(8,128)(2,1)}, u32[]{:S(2)}) copy-start(bf16[2,384,512]{2,1,0:T(8,128)(2,1)} %gate_ref.3) | copy-start | bytes 2359300
  1.9 18.7 %collective-permute-start.1 = (bf16[104,128]{1,0:T(8,128)(2,1)S(1)}, bf16[104,128]{1,0:T(8,128)(2,1)S(1)}, u32[]{:S(2)}, u32[]{:S(2)}) collective-permute-start(bf16[104,128]{1,0:T(8,128)(2,1)S(1)} %shard_map.111), channel_id=1, source_target_pairs={{0,28},{1,29},{2,30},{3,31},{4,64},{5,65},{6,66},{7,67},{8,148},{9... | collective-permute-start | bytes 79880 | tf_op jit(solution)/shard_map/ppermute | solution.py:325
  16.2 6.6 %collective-permute-start = (bf16[104,128]{1,0:T(8,128)(2,1)S(1)}, bf16[104,128]{1,0:T(8,128)(2,1)S(1)}, u32[]{:S(2)}, u32[]{:S(2)}) collective-permute-start(bf16[104,128]{1,0:T(8,128)(2,1)S(1)} %shard_map.111), channel_id=1, source_target_pairs={{0,12},{1,13},{2,14},{3,15},{4,80},{5,81},{6,82},{7,83},{8,132},{9... | collective-permute-start | bytes 79880 | tf_op jit(solution)/shard_map/ppermute | solution.py:325
  23.6 28.0 %copy-start.1 = (bf16[2,384,512]{2,1,0:T(8,128)(2,1)S(1)}, bf16[2,384,512]{2,1,0:T(8,128)(2,1)}, u32[]{:S(2)}) copy-start(bf16[2,384,512]{2,1,0:T(8,128)(2,1)} %up_ref.3) | copy-start | bytes 2359300
  23.6 12.4 %all-to-all-start = ((bf16[4,2,104,128]{3,2,1,0:T(8,128)(2,1)}), bf16[4,2,104,128]{3,2,1,0:T(8,128)(2,1)S(1)}, u32[]{:S(2)}, u32[]{:S(2)}) async-start(bf16[4,2,104,128]{3,2,1,0:T(8,128)(2,1)} %shard_map.112), calls=%async_computation | async-start | bytes 425984 | tf_op jit(solution)/shard_map/all_to_all | solution.py:329
  29.7 20.9 %collective-permute-start.4 = (bf16[2,512,384]{2,1,0:T(8,128)(2,1)}, bf16[2,512,384]{2,1,0:T(8,128)(2,1)}, u32[]{:S(2)}, u32[]{:S(2)}) collective-permute-start(bf16[2,512,384]{2,1,0:T(8,128)(2,1)} %down_hbm.1), channel_id=1, source_target_pairs={{0,32},{32,0},{1,33},{33,1},{2,34},{34,2},{3,35},{35,3},{4,36},{36... | collective-permute-start | bytes 2359304 | tf_op jit(solution)/shard_map/ppermute | solution.py:326
  31.7 19.0 %collective-permute-start.2 = (bf16[2,384,512]{2,1,0:T(8,128)(2,1)S(1)}, bf16[2,384,512]{2,1,0:T(8,128)(2,1)S(1)}, u32[]{:S(2)}, u32[]{:S(2)}) collective-permute-start(bf16[2,384,512]{2,1,0:T(8,128)(2,1)S(1)} %copy-done), channel_id=1, source_target_pairs={{0,32},{32,0},{1,33},{33,1},{2,34},{34,2},{3,35},{35,3},{4,36},{36... | collective-permute-start | bytes 2359304 | tf_op jit(solution)/shard_map/ppermute | solution.py:326
  34.1 16.6 %collective-permute-start.3 = (bf16[2,384,512]{2,1,0:T(8,128)(2,1)}, bf16[2,384,512]{2,1,0:T(8,128)(2,1)}, u32[]{:S(2)}, u32[]{:S(2)}) collective-permute-start(bf16[2,384,512]{2,1,0:T(8,128)(2,1)} %up_ref.3), channel_id=1, source_target_pairs={{0,32},{32,0},{1,33},{33,1},{2,34},{34,2},{3,35},{35,3},{4,36},{36... | collective-permute-start | bytes 2359304 | tf_op jit(solution)/shard_map/ppermute | solution.py:326
  50.7 0.9 copy-start.3
  103.4 55.0 %collective-permute-start.7 = (bf16[4,6,32,512]{3,2,1,0:T(8,128)(2,1)S(1)}, bf16[4,6,32,512]{3,2,1,0:T(8,128)(2,1)}, u32[]{:S(2)}, u32[]{:S(2)}) collective-permute-start(bf16[4,6,32,512]{3,2,1,0:T(8,128)(2,1)S(1)} %all_gather.16.mine_ref), channel_id=1, source_target_pairs={{0,32},{32,0},{1,33},{33,1},{2,34},{34,2},{3,35},{35,3},{4,36},{36... | collective-permute-start | bytes 2359304 | tf_op jit(solution)/shard_map/ppermute | solution.py:353
  108.7 13.6 %all-to-all-start.2 = ((bf16[4,8,48,128]{3,2,1,0:T(8,128)(2,1)}), bf16[4,8,48,128]{3,2,1,0:T(8,128)(2,1)S(1)}, u32[]{:S(2)}, u32[]{:S(2)}) async-start(bf16[4,8,48,128]{3,2,1,0:T(8,128)(2,1)} %shard_map.115), calls=%async_computation.2 | async-start | bytes 786432 | tf_op jit(solution)/shard_map/all_to_all | solution.py:363
  113.6 44.8 %collective-permute-start.6 = (bf16[2,8,104,128]{3,2,1,0:T(8,128)(2,1)S(1)}, bf16[2,8,104,128]{3,2,1,0:T(8,128)(2,1)S(1)}, u32[]{:S(2)}, u32[]{:S(2)}) collective-permute-start(bf16[2,8,104,128]{3,2,1,0:T(8,128)(2,1)S(1)} %shard_map.118), channel_id=1, source_target_pairs={{0,32},{32,0},{1,33},{33,1},{2,34},{34,2},{3,35},{35,3},{4,36},{36... | collective-permute-start | bytes 1277960 | tf_op jit(solution)/shard_map/ppermute | solution.py:341
  147.1 10.4 %copy-start.2 = (s32[2,16]{1,0:T(2,128)S(1)}, s32[2,16]{1,0:T(2,128)}, u32[]{:S(2)}) copy-start(s32[2,16]{1,0:T(2,128)} %slot_ref.1) | copy-start | bytes 388
  147.2 10.4 %collective-permute-start.5 = (bf16[48,128]{1,0:T(8,128)(2,1)S(1)}, bf16[48,128]{1,0:T(8,128)(2,1)S(1)}, u32[]{:S(2)}, u32[]{:S(2)}) collective-permute-start(bf16[48,128]{1,0:T(8,128)(2,1)S(1)} %reduce_sum.22), channel_id=1, source_target_pairs={{12,0},{13,1},{14,2},{15,3},{80,4},{81,5},{82,6},{83,7},{132,8},{1... | collective-permute-start | bytes 36872 | tf_op jit(solution)/shard_map/ppermute | solution.py:367

commit v7 on v5

--- a/solution.py
+++ b/solution.py
@@ -38,7 +38,8 @@
         for s in range(N_SHARD):
             zl, y = divmod(s, Y)
             there = zl * C + c
-            pairs.append((k * N_SHARD + s, there * N_SHARD + columns(zl)[(x, zh)] * Y + y))
+            column = columns(zl)[(x, zh)]
+            pairs.append((k * N_SHARD + s, there * N_SHARD + column * Y + y))
     return pairs
 
 
@@ -140,7 +141,6 @@
     down_hbm,
     far_down_hbm,
     out_ref,
-    loan_ref,
     far_gate,
     far_up,
     down_ref,
@@ -175,8 +175,6 @@
         moves[t].wait()
         for e in range(2):
             give(t, e, near[t][e] + dot(rows[e][1], ref[e], inward))
-    for h in range(2):
-        loan_ref[h] = got_ref[2 * (1 - slots.core) + h]
     moves[2].wait()
     moves[3].wait()
     for e in range(2):
@@ -185,17 +183,27 @@
         give(2, e, dot(rows[0], down_ref[e], across) + dot(rows[1], far_down[e], across))
 
 
+def loan_kernel(dp_ref, got_ref, out_ref):
+    slots = Slots(dp_ref)
+    for h in range(2):
+        out_ref[h] = got_ref[2 * (1 - slots.core) + h]
+
+
+def fold_kernel(in_ref, out_ref):
+    total = sum(in_ref[i].astype(F32) for i in range(in_ref.shape[0]))
+    out_ref[...] = total.astype(BF16)
+
+
 def all_rows(refs, t, e):
     return jnp.concatenate([ref[:, 2 * t + e].reshape(ZH * X * R, 512) for ref in refs], axis=0)
 
 
-def back_kernel(dp_ref, mine_ref, *refs):
-    *weights, out_ref = refs
+def back_kernel(dp_ref, mine_ref, gate_ref, up_ref, far_gate, far_up, out_ref):
     slots = Slots(dp_ref)
     grads = [[all_rows((mine_ref,), t, e) for t in (1, 2)] for e in range(2)]
-    for i, half in enumerate(slots.halves()):
+    for half, weights in zip(slots.halves(), ((gate_ref, up_ref), (far_gate, far_up))):
         terms = [
-            sum(dot(grads[e][t], weights[2 * t + i][e], ((1,), (1,))) for t in range(2)).astype(BF16)
+            sum(dot(grads[e][t], weights[t][e], ((1,), (1,))) for t in range(2)).astype(BF16)
             for e in range(2)
         ]
         for h in range(2):
@@ -266,6 +274,11 @@
     )
 
 
+def folded(tiles, stay=True):
+    (total,) = local(fold_kernel, [VM], [tiles.shape[1:]], stay)(in_vmem(tiles))
+    return total
+
+
 def layer(
     tokens, cotangent, gate_proj, up_proj, down_proj, slot_tokens, gate_weights, live_counts
 ):
@@ -292,15 +305,16 @@
     column = lax.all_to_all(copies, "zl", 0, 0, tiled=True)
     got = in_vmem(lax.all_gather(column, "y", axis=0, tiled=False))
 
-    parts, loan, far_gate, far_up = local(
+    parts, far_gate, far_up = local(
         forward_kernel,
         [SM] + [VM] * 3 + [HB] * 4,
-        [(X, 6, ZH * R, 512), (2, ZL, MESSAGE, 128), gate.shape, up.shape],
+        [(X, 6, ZH * R, 512), gate.shape, up.shape],
         scratch=[pltpu.VMEM(down_proj.shape, BF16)] * 2 + [pltpu.SemaphoreType.DMA((4,))],
     )(dp, got, gate, up, *(in_hbm(w) for w in (far[0], far[1], down_proj, far[2])))
+    (loan,) = local(loan_kernel, [SM, VM], [(2, ZL, MESSAGE, 128)])(dp, got)
     lent = lax.ppermute(loan, "c", swap)
     over_x = lax.all_to_all(parts, "x", 0, 0, tiled=True)
-    over_x = jnp.sum(over_x.astype(F32), axis=0).astype(BF16)
+    over_x = folded(over_x)
     over_zh = lax.all_gather(over_x, "zh", axis=0, tiled=False)
     sums = jnp.sum(over_zh.astype(F32), axis=0)
     gate_sum, up_sum, cot_hidden = sums[0:2], sums[2:4], sums[4:6]
@@ -314,10 +328,10 @@
     mine = in_vmem(mine)
 
     (back,) = local(back_kernel, [SM] + [VM] * 5, [(Y, ZL, PACK, 128)], False)(
-        dp, mine, gate, far_gate, up, far_up
+        dp, mine, gate, up, far_gate, far_up
     )
     over_y = lax.all_to_all(back, "y", 0, 0, tiled=True)
-    over_y = jnp.sum(over_y.astype(F32), axis=0).astype(BF16)
+    over_y = folded(over_y, False)
     over_zl = lax.all_to_all(over_y, "zl", 0, 0, tiled=True)
     over_zl = jnp.sum(over_zl.astype(F32), axis=0).astype(BF16)
     home = lax.ppermute(over_zl, EVERY, homeward())

time: 158 us -> 155 us (0.981)
  local copies, waits for them, and re-layouts: 3.23 us -> 1.58 us
    unnamed x20 -> x8, local copies, waits for them, and re-layouts: 2.52 us -> 0.87 us
    pallas_call x1 -> x4, Pallas kernels: 2.75 us -> 3.54 us  [the longest x1 2.72 us: layer(): local(forward_kernel, [SM] + [VM] * 3 + [HB] * 4, [(X, 6, ZH * R, 512), g...]
where the time goes in v7:
time: 155 us; the launch traced here: 154 us
  blocking collectives  80.7 us (52%)
  starting transfers between devices  37.9 us (24%)
  waiting for transfers between devices  22.2 us (14%)
  Pallas kernels  11.1 us (7%)
  local copies, waits for them, and re-layouts  1.58 us (1%)
    all_gather x1, blocking collectives, layer(): over_zh = lax.all_gather(over_x, 'zh', axis=0, tiled=False)  23.4 us
    all_to_all x1, blocking collectives, layer(): over_x = lax.all_to_all(parts, 'x', 0, 0, tiled=True)  16.7 us
    all_gather x1, blocking collectives, layer(): got = in_vmem(lax.all_gather(column, 'y', axis=0, tiled=False))  14.5 us
    all_gather x1, blocking collectives, layer(): mine = lax.all_gather(acts, 'x', axis=0, tiled=False)  13.3 us
    all_to_all x1, blocking collectives, layer(): over_zl = lax.all_to_all(over_y, 'zl', 0, 0, tiled=True)  12.7 us
    ppermute x1, starting transfers between devices, layer(): message = lax.ppermute(message, EVERY, outward())  12.3 us
    all_to_all x1, starting transfers between devices, layer(): column = lax.all_to_all(copies, 'zl', 0, 0, tiled=True)  8.6 us
    ppermute x1, waiting for transfers between devices, layer(): home = lax.ppermute(over_zl, EVERY, homeward())  7.38 us
  transfers between devices with their start and end apart: 9, of which 4 were waited for; matrix products, arithmetic and copies ran while one was open for 0% of the time, Pallas kernels for 2%

profile of v7, /device:TPU:32, one launch (start us, length us, event | category | flops | bytes accessed | tf_op | source)
XLA Modules:
  0.0 154.5 jit_solution(10828081591136678067)
XLA Ops:
  0.6 1.1 shard_map.111
  1.8 12.3 %collective-permute-start = (bf16[104,128]{1,0:T(8,128)(2,1)S(1)}, bf16[104,128]{1,0:T(8,128)(2,1)S(1)}, u32[]{:S(2)}, u32[]{:S(2)}) collective-permute-start(bf16[104,128]{1,0:T(8,128)(2,1)S(1)} %shard_map.111), channel_id=1, source_target_pairs={{0,12},{1,13},{2,14},{3,15},{4,80},{5,81},{6,82},{7,83},{8,132},{9... | collective-permute-start | bytes 79880 | tf_op jit(solution)/shard_map/ppermute | solution.py:301
  14.1 1.5 collective-permute-done
  15.6 0.0 copy-start.1
  15.6 0.7 broadcast_in_dim.2
  16.3 0.0 copy-start
  16.3 8.6 %all-to-all-start = ((bf16[8,104,128]{2,1,0:T(8,128)(2,1)}), bf16[8,104,128]{2,1,0:T(8,128)(2,1)S(1)}, u32[]{:S(2)}, u32[]{:S(2)}) async-start(bf16[8,104,128]{2,1,0:T(8,128)(2,1)} %broadcast_in_dim.2), calls=%async_computation | async-start | bytes 425984 | tf_op jit(solution)/shard_map/all_to_all | solution.py:305
  24.9 1.9 %collective-permute-start.1 = (bf16[2,384,512]{2,1,0:T(8,128)(2,1)}, bf16[2,384,512]{2,1,0:T(8,128)(2,1)S(1)}, u32[]{:S(2)}, u32[]{:S(2)}) collective-permute-start(bf16[2,384,512]{2,1,0:T(8,128)(2,1)} %gate_ref.3), channel_id=1, source_target_pairs={{0,32},{32,0},{1,33},{33,1},{2,34},{34,2},{3,35},{35,3},{4,36},{36... | collective-permute-start | bytes 2359304 | tf_op jit(solution)/shard_map/ppermute | solution.py:302
  26.8 2.4 %collective-permute-start.2 = (bf16[2,384,512]{2,1,0:T(8,128)(2,1)}, bf16[2,384,512]{2,1,0:T(8,128)(2,1)}, u32[]{:S(2)}, u32[]{:S(2)}) collective-permute-start(bf16[2,384,512]{2,1,0:T(8,128)(2,1)} %up_ref.3), channel_id=1, source_target_pairs={{0,32},{32,0},{1,33},{33,1},{2,34},{34,2},{3,35},{35,3},{4,36},{36... | collective-permute-start | bytes 2359304 | tf_op jit(solution)/shard_map/ppermute | solution.py:302
  29.2 1.9 %collective-permute-start.3 = (bf16[2,512,384]{2,1,0:T(8,128)(2,1)}, bf16[2,512,384]{2,1,0:T(8,128)(2,1)}, u32[]{:S(2)}, u32[]{:S(2)}) collective-permute-start(bf16[2,512,384]{2,1,0:T(8,128)(2,1)} %down_hbm.1), channel_id=1, source_target_pairs={{0,32},{32,0},{1,33},{33,1},{2,34},{34,2},{3,35},{35,3},{4,36},{36... | collective-permute-start | bytes 2359304 | tf_op jit(solution)/shard_map/ppermute | solution.py:302
  31.2 6.8 %all-to-all-done = bf16[8,104,128]{2,1,0:T(8,128)(2,1)S(1)} async-done(((bf16[8,104,128]{2,1,0:T(8,128)(2,1)}), bf16[8,104,128]{2,1,0:T(8,128)(2,1)S(1)}, u32[]{:S(2)}, u32[]{:S(2)}) %all-to-all-start) | async-done | bytes 213024 | tf_op jit(solution)/shard_map/all_to_all | solution.py:305
  38.0 14.5 %all-gather = bf16[32,104,128]{2,1,0:T(8,128)(2,1)S(1)} all-gather(bf16[8,104,128]{2,1,0:T(8,128)(2,1)S(1)} %all-to-all-done), channel_id=2, replica_groups=mesh['x'=4,'zh'=2,'c'=2,'zl'=8,'y'=4] {'y'}, dimensions={0}, use_global_device_ids=true | all-gather | bytes 1064960 | tf_op jit(solution)/shard_map/all_gather | solution.py:306
  52.4 0.0 collective-permute-done.1.gate_hbm
  52.5 0.0 copy-start.3
  52.5 0.0 collective-permute-done.2.up_hbm
  52.5 0.0 collective-permute-done.3.far_down_hbm
  52.5 0.9 copy-done.3
  53.3 0.0 copy-done.1
  53.3 0.0 copy-done
  53.3 2.7 %shard_map.112 = (bf16[4,6,32,512]{3,2,1,0:T(8,128)(2,1)S(1)}, bf16[2,384,512]{2,1,0:T(8,128)(2,1)S(1)}, bf16[2,384,512]{2,1,0:T(8,128)(2,1)S(1)}) custom-call(s32[1]{0:T(128)} %bitcast.dp_ref, bf16[4,8,104,128]{3,2,1,0:T(8,128)(2,1)S(1)} %bitcast.11, bf16[2,384,512]{2,1,0:T(8,128)(2,1)S(1)} %copy-done, bf16[2,384,512]{2,1,0:T(8,128)(2,1)S(1)} %copy-done.1, ...), custom_call_target="tpu_custom_call" | custom-call | tf_op jit(solution)/shard_map/pallas_call | solution.py:308
  56.1 16.7 %all_to_all.20.in_ref = bf16[4,6,32,512]{3,2,1,0:T(8,128)(2,1)S(1)} all-to-all(bf16[4,6,32,512]{3,2,1,0:T(8,128)(2,1)S(1)} %get-tuple-element.10), channel_id=1, replica_groups=mesh['x'=4,'zh'=2,'c'=2,'zl'=8,'y'=4] {'x'}, dimensions={0} | all-to-all | bytes 1572864 | tf_op jit(solution)/shard_map/all_to_all | solution.py:316
  72.8 0.1 shard_map.113
  72.9 23.4 %all-gather.1 = bf16[12,32,512]{2,1,0:T(8,128)(2,1)S(1)} all-gather(bf16[6,32,512]{2,1,0:T(8,128)(2,1)S(1)} %shard_map.113), channel_id=3, replica_groups=mesh['x'=4,'zh'=2,'c'=2,'zl'=8,'y'=4] {'zh'}, dimensions={0}, use_global_device_ids=true | all-gather | bytes 589824 | tf_op jit(solution)/shard_map/all_gather | solution.py:318
  96.3 0.1 convert_reduce_fusion
  96.4 0.1 fusion
  96.5 13.3 %all_gather.20.mine_ref = bf16[4,6,32,512]{3,2,1,0:T(8,128)(2,1)S(1)} all-gather(bf16[1,6,32,512]{3,2,1,0:T(8,128)(2,1)S(1)} %pad_maximum_fusion), channel_id=1, replica_groups=mesh['x'=4,'zh'=2,'c'=2,'zl'=8,'y'=4] {'x'}, dimensions={0}, use_global_device_ids=true | all-gather | bytes 983040 | tf_op jit(solution)/shard_map/all_gather | solution.py:326
  109.8 1.9 %collective-permute-start.6 = (bf16[4,6,32,512]{3,2,1,0:T(8,128)(2,1)S(1)}, bf16[4,6,32,512]{3,2,1,0:T(8,128)(2,1)}, u32[]{:S(2)}, u32[]{:S(2)}) collective-permute-start(bf16[4,6,32,512]{3,2,1,0:T(8,128)(2,1)S(1)} %all_gather.20.mine_ref), channel_id=1, source_target_pairs={{0,32},{32,0},{1,33},{33,1},{2,34},{34,2},{3,35},{35,3},{4,36},{36... | collective-permute-start | bytes 2359304 | tf_op jit(solution)/shard_map/ppermute | solution.py:327
  111.8 1.9 %shard_map.114 = bf16[4,8,48,128]{3,2,1,0:T(8,128)(2,1)} custom-call(s32[1]{0:T(128)} %bitcast.dp_ref, bf16[4,6,32,512]{3,2,1,0:T(8,128)(2,1)S(1)} %all_gather.20.mine_ref, bf16[2,384,512]{2,1,0:T(8,128)(2,1)S(1)} %copy-done, bf16[2,384,512]{2,1,0:T(8,128)(2,1)S(1)} %copy-done.1, bf16[2,384,512]{2,1,0:T(8,128)(2,1)S(1)} %get-tuple-element.11.far_gate, ...), custom_call_target="tpu_custom_call" | custom-call | tf_op jit(solution)/shard_map/pallas_call | solution.py:330
  113.7 3.5 %all-to-all-start.2 = ((bf16[4,8,48,128]{3,2,1,0:T(8,128)(2,1)}), bf16[4,8,48,128]{3,2,1,0:T(8,128)(2,1)S(1)}, u32[]{:S(2)}, u32[]{:S(2)}) async-start(bf16[4,8,48,128]{3,2,1,0:T(8,128)(2,1)} %shard_map.114), calls=%async_computation.2 | async-start | bytes 786432 | tf_op jit(solution)/shard_map/all_to_all | solution.py:333
  117.2 2.4 %collective-permute-start.5 = (bf16[2,8,104,128]{3,2,1,0:T(8,128)(2,1)S(1)}, bf16[2,8,104,128]{3,2,1,0:T(8,128)(2,1)S(1)}, u32[]{:S(2)}, u32[]{:S(2)}) collective-permute-start(bf16[2,8,104,128]{3,2,1,0:T(8,128)(2,1)S(1)} %shard_map.117), channel_id=1, source_target_pairs={{0,32},{32,0},{1,33},{33,1},{2,34},{34,2},{3,35},{35,3},{4,36},{36... | collective-permute-start | bytes 1277960 | tf_op jit(solution)/shard_map/ppermute | solution.py:315
  119.6 6.5 %all-to-all-done.2.in_ref = bf16[4,8,48,128]{3,2,1,0:T(8,128)(2,1)S(1)} async-done(((bf16[4,8,48,128]{3,2,1,0:T(8,128)(2,1)}), bf16[4,8,48,128]{3,2,1,0:T(8,128)(2,1)S(1)}, u32[]{:S(2)}, u32[]{:S(2)}) %all-to-all-start.2) | async-done | bytes 393248 | tf_op jit(solution)/shard_map/all_to_all | solution.py:333
  126.1 0.7 shard_map.115
  126.8 12.7 %all_to_all.21 = bf16[8,48,128]{2,1,0:T(8,128)(2,1)S(1)} all-to-all(bf16[8,48,128]{2,1,0:T(8,128)(2,1)} %shard_map.115), channel_id=1, replica_groups=mesh['x'=4,'zh'=2,'c'=2,'zl'=8,'y'=4] {'zl'}, dimensions={0} | all-to-all | bytes 196608 | tf_op jit(solution)/shard_map/all_to_all | solution.py:335
  139.6 0.0 copy-start.2
  139.6 3.0 %collective-permute-start.4 = (bf16[48,128]{1,0:T(8,128)(2,1)S(1)}, bf16[48,128]{1,0:T(8,128)(2,1)S(1)}, u32[]{:S(2)}, u32[]{:S(2)}) collective-permute-start(bf16[48,128]{1,0:T(8,128)(2,1)S(1)} %reduce_sum.22), channel_id=1, source_target_pairs={{12,0},{13,1},{14,2},{15,3},{80,4},{81,5},{82,6},{83,7},{132,8},{1... | collective-permute-start | bytes 36872 | tf_op jit(solution)/shard_map/ppermute | solution.py:337
  142.6 7.4 %collective-permute-done.4.rows_ref = bf16[48,128]{1,0:T(8,128)(2,1)S(1)} collective-permute-done((bf16[48,128]{1,0:T(8,128)(2,1)S(1)}, bf16[48,128]{1,0:T(8,128)(2,1)S(1)}, u32[]{:S(2)}, u32[]{:S(2)}) %collective-permute-start.4) | collective-permute-done | bytes 12320 | tf_op jit(solution)/shard_map/ppermute | solution.py:337
  150.0 0.0 copy-done.2
  150.0 0.8 shard_map.116
  150.8 0.0 collective-permute-done.5.lent_ref
  150.8 0.0 collective-permute-done.6.other_ref
  150.8 3.7 %shard_map.118 = (bf16[2,384,512]{2,1,0:T(8,128)(2,1)}, bf16[2,384,512]{2,1,0:T(8,128)(2,1)}, bf16[2,512,384]{2,1,0:T(8,128)(2,1)}) custom-call(s32[1]{0:T(128)} %bitcast.dp_ref, bf16[4,8,104,128]{3,2,1,0:T(8,128)(2,1)S(1)} %bitcast.13, bf16[2,8,104,128]{3,2,1,0:T(8,128)(2,1)S(1)} %collective-permute-done.5.lent_ref, ...), custom_call_target="tpu_custom_call" | custom-call | tf_op jit(solution)/shard_map/pallas_call | solution.py:339
  (3 shorter events, 0.1 us)
Async XLA Ops:
  1.8 13.8 %collective-permute-start = (bf16[104,128]{1,0:T(8,128)(2,1)S(1)}, bf16[104,128]{1,0:T(8,128)(2,1)S(1)}, u32[]{:S(2)}, u32[]{:S(2)}) collective-permute-start(bf16[104,128]{1,0:T(8,128)(2,1)S(1)} %shard_map.111), channel_id=1, source_target_pairs={{0,12},{1,13},{2,14},{3,15},{4,80},{5,81},{6,82},{7,83},{8,132},{9... | collective-permute-start | bytes 79880 | tf_op jit(solution)/shard_map/ppermute | solution.py:301
  15.6 37.8 %copy-start.1 = (bf16[2,384,512]{2,1,0:T(8,128)(2,1)S(1)}, bf16[2,384,512]{2,1,0:T(8,128)(2,1)}, u32[]{:S(2)}) copy-start(bf16[2,384,512]{2,1,0:T(8,128)(2,1)} %up_ref.3) | copy-start | bytes 2359300
  16.3 37.0 %copy-start = (bf16[2,384,512]{2,1,0:T(8,128)(2,1)S(1)}, bf16[2,384,512]{2,1,0:T(8,128)(2,1)}, u32[]{:S(2)}) copy-start(bf16[2,384,512]{2,1,0:T(8,128)(2,1)} %gate_ref.3) | copy-start | bytes 2359300
  16.3 21.7 %all-to-all-start = ((bf16[8,104,128]{2,1,0:T(8,128)(2,1)}), bf16[8,104,128]{2,1,0:T(8,128)(2,1)S(1)}, u32[]{:S(2)}, u32[]{:S(2)}) async-start(bf16[8,104,128]{2,1,0:T(8,128)(2,1)} %broadcast_in_dim.2), calls=%async_computation | async-start | bytes 425984 | tf_op jit(solution)/shard_map/all_to_all | solution.py:305
  24.9 27.6 %collective-permute-start.1 = (bf16[2,384,512]{2,1,0:T(8,128)(2,1)}, bf16[2,384,512]{2,1,0:T(8,128)(2,1)S(1)}, u32[]{:S(2)}, u32[]{:S(2)}) collective-permute-start(bf16[2,384,512]{2,1,0:T(8,128)(2,1)} %gate_ref.3), channel_id=1, source_target_pairs={{0,32},{32,0},{1,33},{33,1},{2,34},{34,2},{3,35},{35,3},{4,36},{36... | collective-permute-start | bytes 2359304 | tf_op jit(solution)/shard_map/ppermute | solution.py:302
  26.8 25.6 %collective-permute-start.2 = (bf16[2,384,512]{2,1,0:T(8,128)(2,1)}, bf16[2,384,512]{2,1,0:T(8,128)(2,1)}, u32[]{:S(2)}, u32[]{:S(2)}) collective-permute-start(bf16[2,384,512]{2,1,0:T(8,128)(2,1)} %up_ref.3), channel_id=1, source_target_pairs={{0,32},{32,0},{1,33},{33,1},{2,34},{34,2},{3,35},{35,3},{4,36},{36... | collective-permute-start | bytes 2359304 | tf_op jit(solution)/shard_map/ppermute | solution.py:302
  29.2 23.2 %collective-permute-start.3 = (bf16[2,512,384]{2,1,0:T(8,128)(2,1)}, bf16[2,512,384]{2,1,0:T(8,128)(2,1)}, u32[]{:S(2)}, u32[]{:S(2)}) collective-permute-start(bf16[2,512,384]{2,1,0:T(8,128)(2,1)} %down_hbm.1), channel_id=1, source_target_pairs={{0,32},{32,0},{1,33},{33,1},{2,34},{34,2},{3,35},{35,3},{4,36},{36... | collective-permute-start | bytes 2359304 | tf_op jit(solution)/shard_map/ppermute | solution.py:302
  52.5 0.9 copy-start.3
  109.8 41.0 %collective-permute-start.6 = (bf16[4,6,32,512]{3,2,1,0:T(8,128)(2,1)S(1)}, bf16[4,6,32,512]{3,2,1,0:T(8,128)(2,1)}, u32[]{:S(2)}, u32[]{:S(2)}) collective-permute-start(bf16[4,6,32,512]{3,2,1,0:T(8,128)(2,1)S(1)} %all_gather.20.mine_ref), channel_id=1, source_target_pairs={{0,32},{32,0},{1,33},{33,1},{2,34},{34,2},{3,35},{35,3},{4,36},{36... | collective-permute-start | bytes 2359304 | tf_op jit(solution)/shard_map/ppermute | solution.py:327
  113.7 12.5 %all-to-all-start.2 = ((bf16[4,8,48,128]{3,2,1,0:T(8,128)(2,1)}), bf16[4,8,48,128]{3,2,1,0:T(8,128)(2,1)S(1)}, u32[]{:S(2)}, u32[]{:S(2)}) async-start(bf16[4,8,48,128]{3,2,1,0:T(8,128)(2,1)} %shard_map.114), calls=%async_computation.2 | async-start | bytes 786432 | tf_op jit(solution)/shard_map/all_to_all | solution.py:333
  117.2 33.6 %collective-permute-start.5 = (bf16[2,8,104,128]{3,2,1,0:T(8,128)(2,1)S(1)}, bf16[2,8,104,128]{3,2,1,0:T(8,128)(2,1)S(1)}, u32[]{:S(2)}, u32[]{:S(2)}) collective-permute-start(bf16[2,8,104,128]{3,2,1,0:T(8,128)(2,1)S(1)} %shard_map.117), channel_id=1, source_target_pairs={{0,32},{32,0},{1,33},{33,1},{2,34},{34,2},{3,35},{35,3},{4,36},{36... | collective-permute-start | bytes 1277960 | tf_op jit(solution)/shard_map/ppermute | solution.py:315
  139.6 10.4 %copy-start.2 = (s32[2,16]{1,0:T(2,128)S(1)}, s32[2,16]{1,0:T(2,128)}, u32[]{:S(2)}) copy-start(s32[2,16]{1,0:T(2,128)} %slot_ref.1) | copy-start | bytes 388
  139.6 10.4 %collective-permute-start.4 = (bf16[48,128]{1,0:T(8,128)(2,1)S(1)}, bf16[48,128]{1,0:T(8,128)(2,1)S(1)}, u32[]{:S(2)}, u32[]{:S(2)}) collective-permute-start(bf16[48,128]{1,0:T(8,128)(2,1)S(1)} %reduce_sum.22), channel_id=1, source_target_pairs={{12,0},{13,1},{14,2},{15,3},{80,4},{81,5},{82,6},{83,7},{132,8},{1... | collective-permute-start | bytes 36872 | tf_op jit(solution)/shard_map/ppermute | solution.py:337

commit v8 on v7

--- a/solution.py
+++ b/solution.py
@@ -132,55 +132,36 @@
 
 
 def forward_kernel(
-    dp_ref,
-    got_ref,
-    gate_ref,
-    up_ref,
-    gate_hbm,
-    up_hbm,
-    down_hbm,
-    far_down_hbm,
-    out_ref,
-    far_gate,
-    far_up,
-    down_ref,
-    far_down,
-    sems,
+    dp_ref, got_ref, gate_ref, far_gate, up_ref, up_hbm, down_hbm, far_hbm, out_ref, *scratch
 ):
+    far_up, down_ref, far_down, sems = scratch
     moves = [
         pltpu.make_async_copy(source, target, sems.at[i])
         for i, (source, target) in enumerate(
-            (
-                (gate_hbm, far_gate),
-                (up_hbm, far_up),
-                (down_hbm, down_ref),
-                (far_down_hbm, far_down),
-            )
+            ((up_hbm, far_up), (down_hbm, down_ref), (far_hbm, far_down))
         )
     ]
     for move in moves:
         move.start()
     slots = Slots(dp_ref)
 
-    def give(t, e, part):
+    def give(t, e, rows, pair, dims):
+        part = dot(rows[0], pair[0][e], dims) + dot(rows[1], pair[1][e], dims)
         out_ref[:, 2 * t + e] = part.astype(BF16).reshape(X, ZH * R, 512)
 
     def both(m, e):
         return [features(lines_of(got_ref, half), slots, m, e) for half in slots.halves()]
 
     rows = [both(0, e) for e in range(2)]
-    inward = ((1,), (0,))
-    near = [[dot(rows[e][0], ref[e], inward) for e in range(2)] for ref in (gate_ref, up_ref)]
-    for t, ref in enumerate((far_gate, far_up)):
-        moves[t].wait()
-        for e in range(2):
-            give(t, e, near[t][e] + dot(rows[e][1], ref[e], inward))
+    for e in range(2):
+        give(0, e, rows[e], (gate_ref, far_gate), ((1,), (0,)))
+    moves[0].wait()
+    for e in range(2):
+        give(1, e, rows[e], (up_ref, far_up), ((1,), (0,)))
+    moves[1].wait()
     moves[2].wait()
-    moves[3].wait()
-    for e in range(2):
-        rows = both(1, e)
-        across = ((1,), (1,))
-        give(2, e, dot(rows[0], down_ref[e], across) + dot(rows[1], far_down[e], across))
+    for e in range(2):
+        give(2, e, both(1, e), (down_ref, far_down), ((1,), (1,)))
 
 
 def loan_kernel(dp_ref, got_ref, out_ref):
@@ -198,10 +179,16 @@
     return jnp.concatenate([ref[:, 2 * t + e].reshape(ZH * X * R, 512) for ref in refs], axis=0)
 
 
-def back_kernel(dp_ref, mine_ref, gate_ref, up_ref, far_gate, far_up, out_ref):
+def back_kernel(
+    dp_ref, mine_ref, gate_ref, far_gate, up_ref, up_hbm, out_ref, far_up, sem
+):
+    move = pltpu.make_async_copy(up_hbm, far_up, sem)
+    move.start()
     slots = Slots(dp_ref)
     grads = [[all_rows((mine_ref,), t, e) for t in (1, 2)] for e in range(2)]
     for half, weights in zip(slots.halves(), ((gate_ref, up_ref), (far_gate, far_up))):
+        if weights[1] is far_up:
+            move.wait()
         terms = [
             sum(dot(grads[e][t], weights[t][e], ((1,), (1,))) for t in range(2)).astype(BF16)
             for e in range(2)
@@ -300,17 +287,18 @@
     swap = [(0, 1), (1, 0)]
     message = lax.ppermute(message, EVERY, outward())
     far = [lax.ppermute(w, "c", swap) for w in (gate_proj, up_proj, down_proj)]
-    gate, up = in_vmem(gate_proj), in_vmem(up_proj)
+    held = [in_vmem(w) for w in (gate_proj, far[0], up_proj)] + [in_hbm(far[1])]
     copies = jnp.broadcast_to(message[None], (ZL, MESSAGE, 128))
     column = lax.all_to_all(copies, "zl", 0, 0, tiled=True)
     got = in_vmem(lax.all_gather(column, "y", axis=0, tiled=False))
 
-    parts, far_gate, far_up = local(
+    (parts,) = local(
         forward_kernel,
-        [SM] + [VM] * 3 + [HB] * 4,
-        [(X, 6, ZH * R, 512), gate.shape, up.shape],
-        scratch=[pltpu.VMEM(down_proj.shape, BF16)] * 2 + [pltpu.SemaphoreType.DMA((4,))],
-    )(dp, got, gate, up, *(in_hbm(w) for w in (far[0], far[1], down_proj, far[2])))
+        [SM] + [VM] * 4 + [HB] * 3,
+        [(X, 6, ZH * R, 512)],
+        scratch=[pltpu.VMEM(w.shape, BF16) for w in (up_proj, down_proj, down_proj)]
+        + [pltpu.SemaphoreType.DMA((3,))],
+    )(dp, got, *held, in_hbm(down_proj), in_hbm(far[2]))
     (loan,) = local(loan_kernel, [SM, VM], [(2, ZL, MESSAGE, 128)])(dp, got)
     lent = lax.ppermute(loan, "c", swap)
     over_x = lax.all_to_all(parts, "x", 0, 0, tiled=True)
@@ -327,9 +315,12 @@
     other = lax.ppermute(mine, "c", swap)
     mine = in_vmem(mine)
 
-    (back,) = local(back_kernel, [SM] + [VM] * 5, [(Y, ZL, PACK, 128)], False)(
-        dp, mine, gate, up, far_gate, far_up
-    )
+    (back,) = local(
+        back_kernel,
+        [SM] + [VM] * 4 + [HB],
+        [(Y, ZL, PACK, 128)],
+        scratch=[pltpu.VMEM(up_proj.shape, BF16), pltpu.SemaphoreType.DMA],
+    )(dp, mine, *held)
     over_y = lax.all_to_all(back, "y", 0, 0, tiled=True)
     over_y = folded(over_y, False)
     over_zl = lax.all_to_all(over_y, "zl", 0, 0, tiled=True)

time: 155 us -> 158 us (1.019)
  local copies, waits for them, and re-layouts: 1.58 us -> 3.24 us
    unnamed x8 -> x16, local copies, waits for them, and re-layouts: 0.87 us -> 2.53 us
  transfers between devices with their start and end apart: 9 -> 9, of which waited for: 4 -> 4; matrix products, arithmetic and copies ran while one was open for 0% -> 0% of each run, Pallas kernels for 2% -> 3%
where the time goes in v8:
time: 158 us; the launch traced here: 157 us
  blocking collectives  80.9 us (51%)
  starting transfers between devices  37.9 us (24%)
  waiting for transfers between devices  21.5 us (14%)
  Pallas kernels  12.1 us (8%)
  local copies, waits for them, and re-layouts  3.24 us (2%)
    all_gather x1, blocking collectives, layer(): over_zh = lax.all_gather(over_x, 'zh', axis=0, tiled=False)  23.4 us
    all_to_all x1, blocking collectives, layer(): over_x = lax.all_to_all(parts, 'x', 0, 0, tiled=True)  16.7 us
    all_gather x1, blocking collectives, layer(): got = in_vmem(lax.all_gather(column, 'y', axis=0, tiled=False))  14.5 us
    all_gather x1, blocking collectives, layer(): mine = lax.all_gather(acts, 'x', axis=0, tiled=False)  13.4 us
    all_to_all x1, blocking collectives, layer(): over_zl = lax.all_to_all(over_y, 'zl', 0, 0, tiled=True)  12.8 us
    ppermute x1, starting transfers between devices, layer(): message = lax.ppermute(message, EVERY, outward())  12.3 us
    all_to_all x1, starting transfers between devices, layer(): column = lax.all_to_all(copies, 'zl', 0, 0, tiled=True)  8.6 us
    ppermute x1, waiting for transfers between devices, layer(): home = lax.ppermute(over_zl, EVERY, homeward())  7.36 us
  transfers between devices with their start and end apart: 9, of which 4 were waited for; matrix products, arithmetic and copies ran while one was open for 0% of the time, Pallas kernels for 3%

profile of v8, /device:TPU:32, one launch (start us, length us, event | category | flops | bytes accessed | tf_op | source)
XLA Modules:
  0.0 156.7 jit_solution(10653053874771425960)
XLA Ops:
  0.6 1.1 shard_map.111
  1.8 12.3 %collective-permute-start = (bf16[104,128]{1,0:T(8,128)(2,1)S(1)}, bf16[104,128]{1,0:T(8,128)(2,1)S(1)}, u32[]{:S(2)}, u32[]{:S(2)}) collective-permute-start(bf16[104,128]{1,0:T(8,128)(2,1)S(1)} %shard_map.111), channel_id=1, source_target_pairs={{0,12},{1,13},{2,14},{3,15},{4,80},{5,81},{6,82},{7,83},{8,132},{9... | collective-permute-start | bytes 79880 | tf_op jit(solution)/shard_map/ppermute | solution.py:288
  14.1 1.5 collective-permute-done
  15.6 0.0 copy-start.1
  15.6 0.7 broadcast_in_dim.2
  16.3 0.0 copy-start
  16.3 8.6 %all-to-all-start = ((bf16[8,104,128]{2,1,0:T(8,128)(2,1)}), bf16[8,104,128]{2,1,0:T(8,128)(2,1)S(1)}, u32[]{:S(2)}, u32[]{:S(2)}) async-start(bf16[8,104,128]{2,1,0:T(8,128)(2,1)} %broadcast_in_dim.2), calls=%async_computation | async-start | bytes 425984 | tf_op jit(solution)/shard_map/all_to_all | solution.py:292
  24.9 1.9 %collective-permute-start.3 = (bf16[2,512,384]{2,1,0:T(8,128)(2,1)}, bf16[2,512,384]{2,1,0:T(8,128)(2,1)}, u32[]{:S(2)}, u32[]{:S(2)}) collective-permute-start(bf16[2,512,384]{2,1,0:T(8,128)(2,1)} %down_hbm.1), channel_id=1, source_target_pairs={{0,32},{32,0},{1,33},{33,1},{2,34},{34,2},{3,35},{35,3},{4,36},{36... | collective-permute-start | bytes 2359304 | tf_op jit(solution)/shard_map/ppermute | solution.py:289
  26.8 2.4 %collective-permute-start.1 = (bf16[2,384,512]{2,1,0:T(8,128)(2,1)}, bf16[2,384,512]{2,1,0:T(8,128)(2,1)S(1)}, u32[]{:S(2)}, u32[]{:S(2)}) collective-permute-start(bf16[2,384,512]{2,1,0:T(8,128)(2,1)} %gate_ref.3), channel_id=1, source_target_pairs={{0,32},{32,0},{1,33},{33,1},{2,34},{34,2},{3,35},{35,3},{4,36},{36... | collective-permute-start | bytes 2359304 | tf_op jit(solution)/shard_map/ppermute | solution.py:289
  29.2 1.9 %collective-permute-start.2 = (bf16[2,384,512]{2,1,0:T(8,128)(2,1)}, bf16[2,384,512]{2,1,0:T(8,128)(2,1)}, u32[]{:S(2)}, u32[]{:S(2)}) collective-permute-start(bf16[2,384,512]{2,1,0:T(8,128)(2,1)} %up_ref.3), channel_id=1, source_target_pairs={{0,32},{32,0},{1,33},{33,1},{2,34},{34,2},{3,35},{35,3},{4,36},{36... | collective-permute-start | bytes 2359304 | tf_op jit(solution)/shard_map/ppermute | solution.py:289
  31.2 6.8 %all-to-all-done = bf16[8,104,128]{2,1,0:T(8,128)(2,1)S(1)} async-done(((bf16[8,104,128]{2,1,0:T(8,128)(2,1)}), bf16[8,104,128]{2,1,0:T(8,128)(2,1)S(1)}, u32[]{:S(2)}, u32[]{:S(2)}) %all-to-all-start) | async-done | bytes 213024 | tf_op jit(solution)/shard_map/all_to_all | solution.py:292
  38.0 14.5 %all-gather = bf16[32,104,128]{2,1,0:T(8,128)(2,1)S(1)} all-gather(bf16[8,104,128]{2,1,0:T(8,128)(2,1)S(1)} %all-to-all-done), channel_id=2, replica_groups=mesh['x'=4,'zh'=2,'c'=2,'zl'=8,'y'=4] {'y'}, dimensions={0}, use_global_device_ids=true | all-gather | bytes 1064960 | tf_op jit(solution)/shard_map/all_gather | solution.py:293
  52.4 0.0 collective-permute-done.3.far_hbm
  52.5 0.0 collective-permute-done.1.far_gate
  52.5 0.0 copy-start.2
  52.5 0.0 collective-permute-done.2.up_hbm
  52.5 0.0 copy-done.1
  52.5 0.0 copy-done
  52.5 2.6 %shard_map.112 = bf16[4,6,32,512]{3,2,1,0:T(8,128)(2,1)S(1)} custom-call(s32[1]{0:T(128)} %bitcast.dp_ref, bf16[4,8,104,128]{3,2,1,0:T(8,128)(2,1)S(1)} %bitcast.11, bf16[2,384,512]{2,1,0:T(8,128)(2,1)S(1)} %copy-done, bf16[2,384,512]{2,1,0:T(8,128)(2,1)S(1)} %collective-permute-done.1.far_gate, bf16[2,384,512]{2,1,0:T(8,128)(2,1)S(1)} %copy-done.1, ...), custom_call_target="tpu_custom_call" | custom-call | tf_op jit(solution)/shard_map/pallas_call | solution.py:295
  55.1 0.0 copy-done.2
  55.1 16.7 %all_to_all.20.in_ref = bf16[4,6,32,512]{3,2,1,0:T(8,128)(2,1)S(1)} all-to-all(bf16[4,6,32,512]{3,2,1,0:T(8,128)(2,1)S(1)} %shard_map.112), channel_id=1, replica_groups=mesh['x'=4,'zh'=2,'c'=2,'zl'=8,'y'=4] {'x'}, dimensions={0} | all-to-all | bytes 1572864 | tf_op jit(solution)/shard_map/all_to_all | solution.py:304
  71.8 0.1 shard_map.113
  71.9 23.4 %all-gather.1 = bf16[12,32,512]{2,1,0:T(8,128)(2,1)S(1)} all-gather(bf16[6,32,512]{2,1,0:T(8,128)(2,1)S(1)} %shard_map.113), channel_id=3, replica_groups=mesh['x'=4,'zh'=2,'c'=2,'zl'=8,'y'=4] {'zh'}, dimensions={0}, use_global_device_ids=true | all-gather | bytes 589824 | tf_op jit(solution)/shard_map/all_gather | solution.py:306
  95.3 0.1 convert_reduce_fusion
  95.4 0.1 fusion
  95.5 0.0 copy-start.3
  95.5 13.4 %all_gather.20.mine_ref = bf16[4,6,32,512]{3,2,1,0:T(8,128)(2,1)S(1)} all-gather(bf16[1,6,32,512]{3,2,1,0:T(8,128)(2,1)S(1)} %pad_maximum_fusion), channel_id=1, replica_groups=mesh['x'=4,'zh'=2,'c'=2,'zl'=8,'y'=4] {'x'}, dimensions={0}, use_global_device_ids=true | all-gather | bytes 983040 | tf_op jit(solution)/shard_map/all_gather | solution.py:314
  109.0 1.9 %collective-permute-start.6 = (bf16[4,6,32,512]{3,2,1,0:T(8,128)(2,1)S(1)}, bf16[4,6,32,512]{3,2,1,0:T(8,128)(2,1)}, u32[]{:S(2)}, u32[]{:S(2)}) collective-permute-start(bf16[4,6,32,512]{3,2,1,0:T(8,128)(2,1)S(1)} %all_gather.20.mine_ref), channel_id=1, source_target_pairs={{0,32},{32,0},{1,33},{33,1},{2,34},{34,2},{3,35},{35,3},{4,36},{36... | collective-permute-start | bytes 2359304 | tf_op jit(solution)/shard_map/ppermute | solution.py:315
  110.9 0.0 copy-done.3
  110.9 2.4 %shard_map.114 = bf16[4,8,48,128]{3,2,1,0:T(8,128)(2,1)S(1)} custom-call(s32[1]{0:T(128)} %bitcast.dp_ref, bf16[4,6,32,512]{3,2,1,0:T(8,128)(2,1)S(1)} %all_gather.20.mine_ref, bf16[2,384,512]{2,1,0:T(8,128)(2,1)S(1)} %copy-done, bf16[2,384,512]{2,1,0:T(8,128)(2,1)S(1)} %copy-done.3, bf16[2,384,512]{2,1,0:T(8,128)(2,1)S(1)} %copy-done.1, ...), custom_call_target="tpu_custom_call" | custom-call | tf_op jit(solution)/shard_map/pallas_call | solution.py:318
  113.3 0.0 copy-start.4
  113.3 0.7 copy-done.4
  114.0 3.5 %all-to-all-start.2 = ((bf16[4,8,48,128]{3,2,1,0:T(8,128)(2,1)}), bf16[4,8,48,128]{3,2,1,0:T(8,128)(2,1)S(1)}, u32[]{:S(2)}, u32[]{:S(2)}) async-start(bf16[4,8,48,128]{3,2,1,0:T(8,128)(2,1)} %copy-done.4), calls=%async_computation.2 | async-start | bytes 786432 | tf_op jit(solution)/shard_map/all_to_all | solution.py:324
  117.5 0.8 shard_map.117
  118.3 2.4 %collective-permute-start.5 = (bf16[2,8,104,128]{3,2,1,0:T(8,128)(2,1)}, bf16[2,8,104,128]{3,2,1,0:T(8,128)(2,1)S(1)}, u32[]{:S(2)}, u32[]{:S(2)}) collective-permute-start(bf16[2,8,104,128]{3,2,1,0:T(8,128)(2,1)} %shard_map.117), channel_id=1, source_target_pairs={{0,32},{32,0},{1,33},{33,1},{2,34},{34,2},{3,35},{35,3},{4,36},{36... | collective-permute-start | bytes 1277960 | tf_op jit(solution)/shard_map/ppermute | solution.py:303
  120.7 5.8 %all-to-all-done.2.in_ref = bf16[4,8,48,128]{3,2,1,0:T(8,128)(2,1)S(1)} async-done(((bf16[4,8,48,128]{3,2,1,0:T(8,128)(2,1)}), bf16[4,8,48,128]{3,2,1,0:T(8,128)(2,1)S(1)}, u32[]{:S(2)}, u32[]{:S(2)}) %all-to-all-start.2) | async-done | bytes 393248 | tf_op jit(solution)/shard_map/all_to_all | solution.py:324
  126.5 0.7 shard_map.115
  127.2 12.8 %all_to_all.21 = bf16[8,48,128]{2,1,0:T(8,128)(2,1)S(1)} all-to-all(bf16[8,48,128]{2,1,0:T(8,128)(2,1)} %shard_map.115), channel_id=1, replica_groups=mesh['x'=4,'zh'=2,'c'=2,'zl'=8,'y'=4] {'zl'}, dimensions={0} | all-to-all | bytes 196608 | tf_op jit(solution)/shard_map/all_to_all | solution.py:326
  140.0 0.0 copy-start.7
  140.0 3.0 %collective-permute-start.4 = (bf16[48,128]{1,0:T(8,128)(2,1)S(1)}, bf16[48,128]{1,0:T(8,128)(2,1)S(1)}, u32[]{:S(2)}, u32[]{:S(2)}) collective-permute-start(bf16[48,128]{1,0:T(8,128)(2,1)S(1)} %reduce_sum.22), channel_id=1, source_target_pairs={{12,0},{13,1},{14,2},{15,3},{80,4},{81,5},{82,6},{83,7},{132,8},{1... | collective-permute-start | bytes 36872 | tf_op jit(solution)/shard_map/ppermute | solution.py:328
  143.1 7.4 %collective-permute-done.4.rows_ref = bf16[48,128]{1,0:T(8,128)(2,1)S(1)} collective-permute-done((bf16[48,128]{1,0:T(8,128)(2,1)S(1)}, bf16[48,128]{1,0:T(8,128)(2,1)S(1)}, u32[]{:S(2)}, u32[]{:S(2)}) %collective-permute-start.4) | collective-permute-done | bytes 12320 | tf_op jit(solution)/shard_map/ppermute | solution.py:328
  150.4 0.0 copy-done.7
  150.4 0.8 shard_map.116
  151.2 0.0 collective-permute-done.5.lent_ref
  151.2 0.0 copy-start.5
  151.2 0.8 copy-done.5
  152.0 0.0 collective-permute-done.6.other_ref
  152.0 0.0 copy-start.6
  152.0 1.0 copy-done.6
  153.0 3.7 %shard_map.118 = (bf16[2,384,512]{2,1,0:T(8,128)(2,1)}, bf16[2,384,512]{2,1,0:T(8,128)(2,1)}, bf16[2,512,384]{2,1,0:T(8,128)(2,1)}) custom-call(s32[1]{0:T(128)} %bitcast.dp_ref, bf16[4,8,104,128]{3,2,1,0:T(8,128)(2,1)S(1)} %bitcast.13, bf16[2,8,104,128]{3,2,1,0:T(8,128)(2,1)S(1)} %copy-done.6, bf16[4,6,32,512]{3,2,1,0:T(8,128)(2,1)S(1)} %all_gather.20.mine_ref, ...), custom_call_target="tpu_custom_call" | custom-call | tf_op jit(solution)/shard_map/pallas_call | solution.py:330
  (2 shorter events, 0.0 us)
Async XLA Ops:
  1.8 13.8 %collective-permute-start = (bf16[104,128]{1,0:T(8,128)(2,1)S(1)}, bf16[104,128]{1,0:T(8,128)(2,1)S(1)}, u32[]{:S(2)}, u32[]{:S(2)}) collective-permute-start(bf16[104,128]{1,0:T(8,128)(2,1)S(1)} %shard_map.111), channel_id=1, source_target_pairs={{0,12},{1,13},{2,14},{3,15},{4,80},{5,81},{6,82},{7,83},{8,132},{9... | collective-permute-start | bytes 79880 | tf_op jit(solution)/shard_map/ppermute | solution.py:288
  15.6 36.9 %copy-start.1 = (bf16[2,384,512]{2,1,0:T(8,128)(2,1)S(1)}, bf16[2,384,512]{2,1,0:T(8,128)(2,1)}, u32[]{:S(2)}) copy-start(bf16[2,384,512]{2,1,0:T(8,128)(2,1)} %up_ref.3) | copy-start | bytes 2359300
  16.3 36.2 %copy-start = (bf16[2,384,512]{2,1,0:T(8,128)(2,1)S(1)}, bf16[2,384,512]{2,1,0:T(8,128)(2,1)}, u32[]{:S(2)}) copy-start(bf16[2,384,512]{2,1,0:T(8,128)(2,1)} %gate_ref.3) | copy-start | bytes 2359300
  16.3 21.7 %all-to-all-start = ((bf16[8,104,128]{2,1,0:T(8,128)(2,1)}), bf16[8,104,128]{2,1,0:T(8,128)(2,1)S(1)}, u32[]{:S(2)}, u32[]{:S(2)}) async-start(bf16[8,104,128]{2,1,0:T(8,128)(2,1)} %broadcast_in_dim.2), calls=%async_computation | async-start | bytes 425984 | tf_op jit(solution)/shard_map/all_to_all | solution.py:292
  24.9 27.6 %collective-permute-start.3 = (bf16[2,512,384]{2,1,0:T(8,128)(2,1)}, bf16[2,512,384]{2,1,0:T(8,128)(2,1)}, u32[]{:S(2)}, u32[]{:S(2)}) collective-permute-start(bf16[2,512,384]{2,1,0:T(8,128)(2,1)} %down_hbm.1), channel_id=1, source_target_pairs={{0,32},{32,0},{1,33},{33,1},{2,34},{34,2},{3,35},{35,3},{4,36},{36... | collective-permute-start | bytes 2359304 | tf_op jit(solution)/shard_map/ppermute | solution.py:289
  26.8 25.6 %collective-permute-start.1 = (bf16[2,384,512]{2,1,0:T(8,128)(2,1)}, bf16[2,384,512]{2,1,0:T(8,128)(2,1)S(1)}, u32[]{:S(2)}, u32[]{:S(2)}) collective-permute-start(bf16[2,384,512]{2,1,0:T(8,128)(2,1)} %gate_ref.3), channel_id=1, source_target_pairs={{0,32},{32,0},{1,33},{33,1},{2,34},{34,2},{3,35},{35,3},{4,36},{36... | collective-permute-start | bytes 2359304 | tf_op jit(solution)/shard_map/ppermute | solution.py:289
  29.2 23.2 %collective-permute-start.2 = (bf16[2,384,512]{2,1,0:T(8,128)(2,1)}, bf16[2,384,512]{2,1,0:T(8,128)(2,1)}, u32[]{:S(2)}, u32[]{:S(2)}) collective-permute-start(bf16[2,384,512]{2,1,0:T(8,128)(2,1)} %up_ref.3), channel_id=1, source_target_pairs={{0,32},{32,0},{1,33},{33,1},{2,34},{34,2},{3,35},{35,3},{4,36},{36... | collective-permute-start | bytes 2359304 | tf_op jit(solution)/shard_map/ppermute | solution.py:289
  52.5 2.6 %copy-start.2 = (bf16[2,384,512]{2,1,0:T(8,128)(2,1)}, bf16[2,384,512]{2,1,0:T(8,128)(2,1)S(1)}, u32[]{:S(2)}) copy-start(bf16[2,384,512]{2,1,0:T(8,128)(2,1)S(1)} %collective-permute-done.1.far_gate) | copy-start | bytes 2359300
  95.5 15.4 %copy-start.3 = (bf16[2,384,512]{2,1,0:T(8,128)(2,1)S(1)}, bf16[2,384,512]{2,1,0:T(8,128)(2,1)}, u32[]{:S(2)}) copy-start(bf16[2,384,512]{2,1,0:T(8,128)(2,1)} %copy-done.2) | copy-start | bytes 2359300
  109.0 43.0 %collective-permute-start.6 = (bf16[4,6,32,512]{3,2,1,0:T(8,128)(2,1)S(1)}, bf16[4,6,32,512]{3,2,1,0:T(8,128)(2,1)}, u32[]{:S(2)}, u32[]{:S(2)}) collective-permute-start(bf16[4,6,32,512]{3,2,1,0:T(8,128)(2,1)S(1)} %all_gather.20.mine_ref), channel_id=1, source_target_pairs={{0,32},{32,0},{1,33},{33,1},{2,34},{34,2},{3,35},{35,3},{4,36},{36... | collective-permute-start | bytes 2359304 | tf_op jit(solution)/shard_map/ppermute | solution.py:315
  113.3 0.7 copy-start.4
  114.0 12.5 %all-to-all-start.2 = ((bf16[4,8,48,128]{3,2,1,0:T(8,128)(2,1)}), bf16[4,8,48,128]{3,2,1,0:T(8,128)(2,1)S(1)}, u32[]{:S(2)}, u32[]{:S(2)}) async-start(bf16[4,8,48,128]{3,2,1,0:T(8,128)(2,1)} %copy-done.4), calls=%async_computation.2 | async-start | bytes 786432 | tf_op jit(solution)/shard_map/all_to_all | solution.py:324
  118.3 33.0 %collective-permute-start.5 = (bf16[2,8,104,128]{3,2,1,0:T(8,128)(2,1)}, bf16[2,8,104,128]{3,2,1,0:T(8,128)(2,1)S(1)}, u32[]{:S(2)}, u32[]{:S(2)}) collective-permute-start(bf16[2,8,104,128]{3,2,1,0:T(8,128)(2,1)} %shard_map.117), channel_id=1, source_target_pairs={{0,32},{32,0},{1,33},{33,1},{2,34},{34,2},{3,35},{35,3},{4,36},{36... | collective-permute-start | bytes 1277960 | tf_op jit(solution)/shard_map/ppermute | solution.py:303
  140.0 10.4 %copy-start.7 = (s32[2,16]{1,0:T(2,128)S(1)}, s32[2,16]{1,0:T(2,128)}, u32[]{:S(2)}) copy-start(s32[2,16]{1,0:T(2,128)} %slot_ref.1) | copy-start | bytes 388
  140.0 10.4 %collective-permute-start.4 = (bf16[48,128]{1,0:T(8,128)(2,1)S(1)}, bf16[48,128]{1,0:T(8,128)(2,1)S(1)}, u32[]{:S(2)}, u32[]{:S(2)}) collective-permute-start(bf16[48,128]{1,0:T(8,128)(2,1)S(1)} %reduce_sum.22), channel_id=1, source_target_pairs={{12,0},{13,1},{14,2},{15,3},{80,4},{81,5},{82,6},{83,7},{132,8},{1... | collective-permute-start | bytes 36872 | tf_op jit(solution)/shard_map/ppermute | solution.py:328
  151.2 0.8 copy-start.5
  152.0 1.0 copy-start.6

commit v9 on v8

--- a/solution.py
+++ b/solution.py
@@ -132,9 +132,9 @@
 
 
 def forward_kernel(
-    dp_ref, got_ref, gate_ref, far_gate, up_ref, up_hbm, down_hbm, far_hbm, out_ref, *scratch
+    dp_ref, got_ref, gate_ref, far_gate, up_ref, up_hbm, down_hbm, far_hbm, out_ref, far_up, *scratch
 ):
-    far_up, down_ref, far_down, sems = scratch
+    down_ref, far_down, sems = scratch
     moves = [
         pltpu.make_async_copy(source, target, sems.at[i])
         for i, (source, target) in enumerate(
@@ -179,16 +179,10 @@
     return jnp.concatenate([ref[:, 2 * t + e].reshape(ZH * X * R, 512) for ref in refs], axis=0)
 
 
-def back_kernel(
-    dp_ref, mine_ref, gate_ref, far_gate, up_ref, up_hbm, out_ref, far_up, sem
-):
-    move = pltpu.make_async_copy(up_hbm, far_up, sem)
-    move.start()
+def back_kernel(dp_ref, mine_ref, gate_ref, far_gate, up_ref, far_up, out_ref):
     slots = Slots(dp_ref)
     grads = [[all_rows((mine_ref,), t, e) for t in (1, 2)] for e in range(2)]
     for half, weights in zip(slots.halves(), ((gate_ref, up_ref), (far_gate, far_up))):
-        if weights[1] is far_up:
-            move.wait()
         terms = [
             sum(dot(grads[e][t], weights[t][e], ((1,), (1,))) for t in range(2)).astype(BF16)
             for e in range(2)
@@ -287,18 +281,17 @@
     swap = [(0, 1), (1, 0)]
     message = lax.ppermute(message, EVERY, outward())
     far = [lax.ppermute(w, "c", swap) for w in (gate_proj, up_proj, down_proj)]
-    held = [in_vmem(w) for w in (gate_proj, far[0], up_proj)] + [in_hbm(far[1])]
+    held = [in_vmem(w) for w in (gate_proj, far[0], up_proj)]
     copies = jnp.broadcast_to(message[None], (ZL, MESSAGE, 128))
     column = lax.all_to_all(copies, "zl", 0, 0, tiled=True)
     got = in_vmem(lax.all_gather(column, "y", axis=0, tiled=False))
 
-    (parts,) = local(
+    parts, far_up = local(
         forward_kernel,
         [SM] + [VM] * 4 + [HB] * 3,
-        [(X, 6, ZH * R, 512)],
-        scratch=[pltpu.VMEM(w.shape, BF16) for w in (up_proj, down_proj, down_proj)]
-        + [pltpu.SemaphoreType.DMA((3,))],
-    )(dp, got, *held, in_hbm(down_proj), in_hbm(far[2]))
+        [(X, 6, ZH * R, 512), up_proj.shape],
+        scratch=[pltpu.VMEM(down_proj.shape, BF16)] * 2 + [pltpu.SemaphoreType.DMA((3,))],
+    )(dp, got, *held, *(in_hbm(w) for w in (far[1], down_proj, far[2])))
     (loan,) = local(loan_kernel, [SM, VM], [(2, ZL, MESSAGE, 128)])(dp, got)
     lent = lax.ppermute(loan, "c", swap)
     over_x = lax.all_to_all(parts, "x", 0, 0, tiled=True)
@@ -315,12 +308,7 @@
     other = lax.ppermute(mine, "c", swap)
     mine = in_vmem(mine)
 
-    (back,) = local(
-        back_kernel,
-        [SM] + [VM] * 4 + [HB],
-        [(Y, ZL, PACK, 128)],
-        scratch=[pltpu.VMEM(up_proj.shape, BF16), pltpu.SemaphoreType.DMA],
-    )(dp, mine, *held)
+    (back,) = local(back_kernel, [SM] + [VM] * 5, [(Y, ZL, PACK, 128)])(dp, mine, *held, far_up)
     over_y = lax.all_to_all(back, "y", 0, 0, tiled=True)
     over_y = folded(over_y, False)
     over_zl = lax.all_to_all(over_y, "zl", 0, 0, tiled=True)

time: 158 us -> 156 us (0.987)
  transfers between devices with their start and end apart: 9 -> 9, of which waited for: 4 -> 4; matrix products, arithmetic and copies ran while one was open for 0% -> 0% of each run, Pallas kernels for 3% -> 2%
where the time goes in v9:
time: 156 us; the launch traced here: 155 us
  blocking collectives  80.9 us (52%)
  starting transfers between devices  37.9 us (24%)
  waiting for transfers between devices  21.5 us (14%)
  Pallas kernels  10.9 us (7%)
  local copies, waits for them, and re-layouts  3.24 us (2%)
    all_gather x1, blocking collectives, layer(): over_zh = lax.all_gather(over_x, 'zh', axis=0, tiled=False)  23.4 us
    all_to_all x1, blocking collectives, layer(): over_x = lax.all_to_all(parts, 'x', 0, 0, tiled=True)  16.7 us
    all_gather x1, blocking collectives, layer(): got = in_vmem(lax.all_gather(column, 'y', axis=0, tiled=False))  14.5 us
    all_gather x1, blocking collectives, layer(): mine = lax.all_gather(acts, 'x', axis=0, tiled=False)  13.4 us
    all_to_all x1, blocking collectives, layer(): over_zl = lax.all_to_all(over_y, 'zl', 0, 0, tiled=True)  12.8 us
    ppermute x1, starting transfers between devices, layer(): message = lax.ppermute(message, EVERY, outward())  12.3 us
    all_to_all x1, starting transfers between devices, layer(): column = lax.all_to_all(copies, 'zl', 0, 0, tiled=True)  8.6 us
    ppermute x1, waiting for transfers between devices, layer(): home = lax.ppermute(over_zl, EVERY, homeward())  7.35 us
  transfers between devices with their start and end apart: 9, of which 4 were waited for; matrix products, arithmetic and copies ran while one was open for 0% of the time, Pallas kernels for 2%

profile of v9, /device:TPU:32, one launch (start us, length us, event | category | flops | bytes accessed | tf_op | source)
XLA Modules:
  0.0 155.4 jit_solution(14802924078298932924)
XLA Ops:
  0.6 1.1 shard_map.111
  1.8 12.3 %collective-permute-start = (bf16[104,128]{1,0:T(8,128)(2,1)S(1)}, bf16[104,128]{1,0:T(8,128)(2,1)S(1)}, u32[]{:S(2)}, u32[]{:S(2)}) collective-permute-start(bf16[104,128]{1,0:T(8,128)(2,1)S(1)} %shard_map.111), channel_id=1, source_target_pairs={{0,12},{1,13},{2,14},{3,15},{4,80},{5,81},{6,82},{7,83},{8,132},{9... | collective-permute-start | bytes 79880 | tf_op jit(solution)/shard_map/ppermute | solution.py:282
  14.1 1.5 collective-permute-done
  15.6 0.0 copy-start.1
  15.6 0.7 broadcast_in_dim.2
  16.3 0.0 copy-start
  16.3 8.6 %all-to-all-start = ((bf16[8,104,128]{2,1,0:T(8,128)(2,1)}), bf16[8,104,128]{2,1,0:T(8,128)(2,1)S(1)}, u32[]{:S(2)}, u32[]{:S(2)}) async-start(bf16[8,104,128]{2,1,0:T(8,128)(2,1)} %broadcast_in_dim.2), calls=%async_computation | async-start | bytes 425984 | tf_op jit(solution)/shard_map/all_to_all | solution.py:286
  24.9 1.9 %collective-permute-start.3 = (bf16[2,512,384]{2,1,0:T(8,128)(2,1)}, bf16[2,512,384]{2,1,0:T(8,128)(2,1)}, u32[]{:S(2)}, u32[]{:S(2)}) collective-permute-start(bf16[2,512,384]{2,1,0:T(8,128)(2,1)} %down_hbm.1), channel_id=1, source_target_pairs={{0,32},{32,0},{1,33},{33,1},{2,34},{34,2},{3,35},{35,3},{4,36},{36... | collective-permute-start | bytes 2359304 | tf_op jit(solution)/shard_map/ppermute | solution.py:283
  26.8 2.4 %collective-permute-start.1 = (bf16[2,384,512]{2,1,0:T(8,128)(2,1)}, bf16[2,384,512]{2,1,0:T(8,128)(2,1)S(1)}, u32[]{:S(2)}, u32[]{:S(2)}) collective-permute-start(bf16[2,384,512]{2,1,0:T(8,128)(2,1)} %gate_ref.3), channel_id=1, source_target_pairs={{0,32},{32,0},{1,33},{33,1},{2,34},{34,2},{3,35},{35,3},{4,36},{36... | collective-permute-start | bytes 2359304 | tf_op jit(solution)/shard_map/ppermute | solution.py:283
  29.2 1.9 %collective-permute-start.2 = (bf16[2,384,512]{2,1,0:T(8,128)(2,1)}, bf16[2,384,512]{2,1,0:T(8,128)(2,1)}, u32[]{:S(2)}, u32[]{:S(2)}) collective-permute-start(bf16[2,384,512]{2,1,0:T(8,128)(2,1)} %up_ref.3), channel_id=1, source_target_pairs={{0,32},{32,0},{1,33},{33,1},{2,34},{34,2},{3,35},{35,3},{4,36},{36... | collective-permute-start | bytes 2359304 | tf_op jit(solution)/shard_map/ppermute | solution.py:283
  31.2 6.8 %all-to-all-done = bf16[8,104,128]{2,1,0:T(8,128)(2,1)S(1)} async-done(((bf16[8,104,128]{2,1,0:T(8,128)(2,1)}), bf16[8,104,128]{2,1,0:T(8,128)(2,1)S(1)}, u32[]{:S(2)}, u32[]{:S(2)}) %all-to-all-start) | async-done | bytes 213024 | tf_op jit(solution)/shard_map/all_to_all | solution.py:286
  38.0 14.5 %all-gather = bf16[32,104,128]{2,1,0:T(8,128)(2,1)S(1)} all-gather(bf16[8,104,128]{2,1,0:T(8,128)(2,1)S(1)} %all-to-all-done), channel_id=2, replica_groups=mesh['x'=4,'zh'=2,'c'=2,'zl'=8,'y'=4] {'y'}, dimensions={0}, use_global_device_ids=true | all-gather | bytes 1064960 | tf_op jit(solution)/shard_map/all_gather | solution.py:287
  52.4 0.0 collective-permute-done.3.far_hbm
  52.5 0.0 collective-permute-done.1.far_gate
  52.5 0.0 copy-start.2
  52.5 0.0 collective-permute-done.2.up_hbm
  52.5 0.0 copy-done.1
  52.5 0.0 copy-done
  52.5 2.6 %shard_map.112 = (bf16[4,6,32,512]{3,2,1,0:T(8,128)(2,1)S(1)}, bf16[2,384,512]{2,1,0:T(8,128)(2,1)S(1)}) custom-call(s32[1]{0:T(128)} %bitcast.dp_ref, bf16[4,8,104,128]{3,2,1,0:T(8,128)(2,1)S(1)} %bitcast.11, bf16[2,384,512]{2,1,0:T(8,128)(2,1)S(1)} %copy-done, bf16[2,384,512]{2,1,0:T(8,128)(2,1)S(1)} %collective-permute-done.1.far_gate, ...), custom_call_target="tpu_custom_call" | custom-call | tf_op jit(solution)/shard_map/pallas_call | solution.py:289
  55.1 0.0 copy-done.2
  55.1 16.7 %all_to_all.20.in_ref = bf16[4,6,32,512]{3,2,1,0:T(8,128)(2,1)S(1)} all-to-all(bf16[4,6,32,512]{3,2,1,0:T(8,128)(2,1)S(1)} %get-tuple-element.9), channel_id=1, replica_groups=mesh['x'=4,'zh'=2,'c'=2,'zl'=8,'y'=4] {'x'}, dimensions={0} | all-to-all | bytes 1572864 | tf_op jit(solution)/shard_map/all_to_all | solution.py:297
  71.8 0.1 shard_map.113
  71.9 23.4 %all-gather.1 = bf16[12,32,512]{2,1,0:T(8,128)(2,1)S(1)} all-gather(bf16[6,32,512]{2,1,0:T(8,128)(2,1)S(1)} %shard_map.113), channel_id=3, replica_groups=mesh['x'=4,'zh'=2,'c'=2,'zl'=8,'y'=4] {'zh'}, dimensions={0}, use_global_device_ids=true | all-gather | bytes 589824 | tf_op jit(solution)/shard_map/all_gather | solution.py:299
  95.3 0.1 convert_reduce_fusion
  95.4 0.1 fusion
  95.5 0.0 copy-start.3
  95.5 13.4 %all_gather.20.mine_ref = bf16[4,6,32,512]{3,2,1,0:T(8,128)(2,1)S(1)} all-gather(bf16[1,6,32,512]{3,2,1,0:T(8,128)(2,1)S(1)} %pad_maximum_fusion), channel_id=1, replica_groups=mesh['x'=4,'zh'=2,'c'=2,'zl'=8,'y'=4] {'x'}, dimensions={0}, use_global_device_ids=true | all-gather | bytes 983040 | tf_op jit(solution)/shard_map/all_gather | solution.py:307
  109.0 1.9 %collective-permute-start.6 = (bf16[4,6,32,512]{3,2,1,0:T(8,128)(2,1)S(1)}, bf16[4,6,32,512]{3,2,1,0:T(8,128)(2,1)}, u32[]{:S(2)}, u32[]{:S(2)}) collective-permute-start(bf16[4,6,32,512]{3,2,1,0:T(8,128)(2,1)S(1)} %all_gather.20.mine_ref), channel_id=1, source_target_pairs={{0,32},{32,0},{1,33},{33,1},{2,34},{34,2},{3,35},{35,3},{4,36},{36... | collective-permute-start | bytes 2359304 | tf_op jit(solution)/shard_map/ppermute | solution.py:308
  110.9 0.0 copy-done.3
  110.9 1.2 shard_map.114
  112.1 0.0 copy-start.4
  112.1 0.7 copy-done.4
  112.9 3.5 %all-to-all-start.2 = ((bf16[4,8,48,128]{3,2,1,0:T(8,128)(2,1)}), bf16[4,8,48,128]{3,2,1,0:T(8,128)(2,1)S(1)}, u32[]{:S(2)}, u32[]{:S(2)}) async-start(bf16[4,8,48,128]{3,2,1,0:T(8,128)(2,1)} %copy-done.4), calls=%async_computation.2 | async-start | bytes 786432 | tf_op jit(solution)/shard_map/all_to_all | solution.py:312
  116.3 0.8 shard_map.117
  117.1 2.4 %collective-permute-start.5 = (bf16[2,8,104,128]{3,2,1,0:T(8,128)(2,1)}, bf16[2,8,104,128]{3,2,1,0:T(8,128)(2,1)S(1)}, u32[]{:S(2)}, u32[]{:S(2)}) collective-permute-start(bf16[2,8,104,128]{3,2,1,0:T(8,128)(2,1)} %shard_map.117), channel_id=1, source_target_pairs={{0,32},{32,0},{1,33},{33,1},{2,34},{34,2},{3,35},{35,3},{4,36},{36... | collective-permute-start | bytes 1277960 | tf_op jit(solution)/shard_map/ppermute | solution.py:296
  119.5 5.8 %all-to-all-done.2.in_ref = bf16[4,8,48,128]{3,2,1,0:T(8,128)(2,1)S(1)} async-done(((bf16[4,8,48,128]{3,2,1,0:T(8,128)(2,1)}), bf16[4,8,48,128]{3,2,1,0:T(8,128)(2,1)S(1)}, u32[]{:S(2)}, u32[]{:S(2)}) %all-to-all-start.2) | async-done | bytes 393248 | tf_op jit(solution)/shard_map/all_to_all | solution.py:312
  125.3 0.7 shard_map.115
  126.0 12.8 %all_to_all.21 = bf16[8,48,128]{2,1,0:T(8,128)(2,1)S(1)} all-to-all(bf16[8,48,128]{2,1,0:T(8,128)(2,1)} %shard_map.115), channel_id=1, replica_groups=mesh['x'=4,'zh'=2,'c'=2,'zl'=8,'y'=4] {'zl'}, dimensions={0} | all-to-all | bytes 196608 | tf_op jit(solution)/shard_map/all_to_all | solution.py:314
  138.7 0.0 copy-start.7
  138.8 3.0 %collective-permute-start.4 = (bf16[48,128]{1,0:T(8,128)(2,1)S(1)}, bf16[48,128]{1,0:T(8,128)(2,1)S(1)}, u32[]{:S(2)}, u32[]{:S(2)}) collective-permute-start(bf16[48,128]{1,0:T(8,128)(2,1)S(1)} %reduce_sum.22), channel_id=1, source_target_pairs={{12,0},{13,1},{14,2},{15,3},{80,4},{81,5},{82,6},{83,7},{132,8},{1... | collective-permute-start | bytes 36872 | tf_op jit(solution)/shard_map/ppermute | solution.py:316
  141.8 7.4 %collective-permute-done.4.rows_ref = bf16[48,128]{1,0:T(8,128)(2,1)S(1)} collective-permute-done((bf16[48,128]{1,0:T(8,128)(2,1)S(1)}, bf16[48,128]{1,0:T(8,128)(2,1)S(1)}, u32[]{:S(2)}, u32[]{:S(2)}) %collective-permute-start.4) | collective-permute-done | bytes 12320 | tf_op jit(solution)/shard_map/ppermute | solution.py:316
  149.2 0.0 copy-done.7
  149.2 0.8 shard_map.116
  150.0 0.0 collective-permute-done.5.lent_ref
  150.0 0.0 copy-start.5
  150.0 0.8 copy-done.5
  150.7 0.0 collective-permute-done.6.other_ref
  150.7 0.0 copy-start.6
  150.8 1.0 copy-done.6
  151.8 3.7 %shard_map.118 = (bf16[2,384,512]{2,1,0:T(8,128)(2,1)}, bf16[2,384,512]{2,1,0:T(8,128)(2,1)}, bf16[2,512,384]{2,1,0:T(8,128)(2,1)}) custom-call(s32[1]{0:T(128)} %bitcast.dp_ref, bf16[4,8,104,128]{3,2,1,0:T(8,128)(2,1)S(1)} %bitcast.13, bf16[2,8,104,128]{3,2,1,0:T(8,128)(2,1)S(1)} %copy-done.6, bf16[4,6,32,512]{3,2,1,0:T(8,128)(2,1)S(1)} %all_gather.20.mine_ref, ...), custom_call_target="tpu_custom_call" | custom-call | tf_op jit(solution)/shard_map/pallas_call | solution.py:318
  (2 shorter events, 0.0 us)
Async XLA Ops:
  1.8 13.8 %collective-permute-start = (bf16[104,128]{1,0:T(8,128)(2,1)S(1)}, bf16[104,128]{1,0:T(8,128)(2,1)S(1)}, u32[]{:S(2)}, u32[]{:S(2)}) collective-permute-start(bf16[104,128]{1,0:T(8,128)(2,1)S(1)} %shard_map.111), channel_id=1, source_target_pairs={{0,12},{1,13},{2,14},{3,15},{4,80},{5,81},{6,82},{7,83},{8,132},{9... | collective-permute-start | bytes 79880 | tf_op jit(solution)/shard_map/ppermute | solution.py:282
  15.6 36.9 %copy-start.1 = (bf16[2,384,512]{2,1,0:T(8,128)(2,1)S(1)}, bf16[2,384,512]{2,1,0:T(8,128)(2,1)}, u32[]{:S(2)}) copy-start(bf16[2,384,512]{2,1,0:T(8,128)(2,1)} %up_ref.3) | copy-start | bytes 2359300
  16.3 36.2 %copy-start = (bf16[2,384,512]{2,1,0:T(8,128)(2,1)S(1)}, bf16[2,384,512]{2,1,0:T(8,128)(2,1)}, u32[]{:S(2)}) copy-start(bf16[2,384,512]{2,1,0:T(8,128)(2,1)} %gate_ref.3) | copy-start | bytes 2359300
  16.3 21.7 %all-to-all-start = ((bf16[8,104,128]{2,1,0:T(8,128)(2,1)}), bf16[8,104,128]{2,1,0:T(8,128)(2,1)S(1)}, u32[]{:S(2)}, u32[]{:S(2)}) async-start(bf16[8,104,128]{2,1,0:T(8,128)(2,1)} %broadcast_in_dim.2), calls=%async_computation | async-start | bytes 425984 | tf_op jit(solution)/shard_map/all_to_all | solution.py:286
  24.9 27.6 %collective-permute-start.3 = (bf16[2,512,384]{2,1,0:T(8,128)(2,1)}, bf16[2,512,384]{2,1,0:T(8,128)(2,1)}, u32[]{:S(2)}, u32[]{:S(2)}) collective-permute-start(bf16[2,512,384]{2,1,0:T(8,128)(2,1)} %down_hbm.1), channel_id=1, source_target_pairs={{0,32},{32,0},{1,33},{33,1},{2,34},{34,2},{3,35},{35,3},{4,36},{36... | collective-permute-start | bytes 2359304 | tf_op jit(solution)/shard_map/ppermute | solution.py:283
  26.8 25.6 %collective-permute-start.1 = (bf16[2,384,512]{2,1,0:T(8,128)(2,1)}, bf16[2,384,512]{2,1,0:T(8,128)(2,1)S(1)}, u32[]{:S(2)}, u32[]{:S(2)}) collective-permute-start(bf16[2,384,512]{2,1,0:T(8,128)(2,1)} %gate_ref.3), channel_id=1, source_target_pairs={{0,32},{32,0},{1,33},{33,1},{2,34},{34,2},{3,35},{35,3},{4,36},{36... | collective-permute-start | bytes 2359304 | tf_op jit(solution)/shard_map/ppermute | solution.py:283
  29.2 23.2 %collective-permute-start.2 = (bf16[2,384,512]{2,1,0:T(8,128)(2,1)}, bf16[2,384,512]{2,1,0:T(8,128)(2,1)}, u32[]{:S(2)}, u32[]{:S(2)}) collective-permute-start(bf16[2,384,512]{2,1,0:T(8,128)(2,1)} %up_ref.3), channel_id=1, source_target_pairs={{0,32},{32,0},{1,33},{33,1},{2,34},{34,2},{3,35},{35,3},{4,36},{36... | collective-permute-start | bytes 2359304 | tf_op jit(solution)/shard_map/ppermute | solution.py:283
  52.5 2.6 %copy-start.2 = (bf16[2,384,512]{2,1,0:T(8,128)(2,1)}, bf16[2,384,512]{2,1,0:T(8,128)(2,1)S(1)}, u32[]{:S(2)}) copy-start(bf16[2,384,512]{2,1,0:T(8,128)(2,1)S(1)} %collective-permute-done.1.far_gate) | copy-start | bytes 2359300
  95.5 15.4 %copy-start.3 = (bf16[2,384,512]{2,1,0:T(8,128)(2,1)S(1)}, bf16[2,384,512]{2,1,0:T(8,128)(2,1)}, u32[]{:S(2)}) copy-start(bf16[2,384,512]{2,1,0:T(8,128)(2,1)} %copy-done.2) | copy-start | bytes 2359300
  109.0 41.8 %collective-permute-start.6 = (bf16[4,6,32,512]{3,2,1,0:T(8,128)(2,1)S(1)}, bf16[4,6,32,512]{3,2,1,0:T(8,128)(2,1)}, u32[]{:S(2)}, u32[]{:S(2)}) collective-permute-start(bf16[4,6,32,512]{3,2,1,0:T(8,128)(2,1)S(1)} %all_gather.20.mine_ref), channel_id=1, source_target_pairs={{0,32},{32,0},{1,33},{33,1},{2,34},{34,2},{3,35},{35,3},{4,36},{36... | collective-permute-start | bytes 2359304 | tf_op jit(solution)/shard_map/ppermute | solution.py:308
  112.1 0.7 copy-start.4
  112.9 12.4 %all-to-all-start.2 = ((bf16[4,8,48,128]{3,2,1,0:T(8,128)(2,1)}), bf16[4,8,48,128]{3,2,1,0:T(8,128)(2,1)S(1)}, u32[]{:S(2)}, u32[]{:S(2)}) async-start(bf16[4,8,48,128]{3,2,1,0:T(8,128)(2,1)} %copy-done.4), calls=%async_computation.2 | async-start | bytes 786432 | tf_op jit(solution)/shard_map/all_to_all | solution.py:312
  117.1 32.9 %collective-permute-start.5 = (bf16[2,8,104,128]{3,2,1,0:T(8,128)(2,1)}, bf16[2,8,104,128]{3,2,1,0:T(8,128)(2,1)S(1)}, u32[]{:S(2)}, u32[]{:S(2)}) collective-permute-start(bf16[2,8,104,128]{3,2,1,0:T(8,128)(2,1)} %shard_map.117), channel_id=1, source_target_pairs={{0,32},{32,0},{1,33},{33,1},{2,34},{34,2},{3,35},{35,3},{4,36},{36... | collective-permute-start | bytes 1277960 | tf_op jit(solution)/shard_map/ppermute | solution.py:296
  138.7 10.4 %copy-start.7 = (s32[2,16]{1,0:T(2,128)S(1)}, s32[2,16]{1,0:T(2,128)}, u32[]{:S(2)}) copy-start(s32[2,16]{1,0:T(2,128)} %slot_ref.1) | copy-start | bytes 388
  138.8 10.4 %collective-permute-start.4 = (bf16[48,128]{1,0:T(8,128)(2,1)S(1)}, bf16[48,128]{1,0:T(8,128)(2,1)S(1)}, u32[]{:S(2)}, u32[]{:S(2)}) collective-permute-start(bf16[48,128]{1,0:T(8,128)(2,1)S(1)} %reduce_sum.22), channel_id=1, source_target_pairs={{12,0},{13,1},{14,2},{15,3},{80,4},{81,5},{82,6},{83,7},{132,8},{1... | collective-permute-start | bytes 36872 | tf_op jit(solution)/shard_map/ppermute | solution.py:316
  150.0 0.8 copy-start.5
  150.7 1.0 copy-start.6

commit v10 on v9

--- a/solution.py
+++ b/solution.py
@@ -138,30 +138,36 @@
     moves = [
         pltpu.make_async_copy(source, target, sems.at[i])
         for i, (source, target) in enumerate(
-            ((up_hbm, far_up), (down_hbm, down_ref), (far_hbm, far_down))
+            ((down_hbm, down_ref), (up_hbm, far_up), (far_hbm, far_down))
         )
     ]
     for move in moves:
         move.start()
     slots = Slots(dp_ref)
 
+    def finish(t, e, part):
+        out_ref[:, 2 * t + e] = part.astype(BF16).reshape(X, ZH * R, 512)
+
     def give(t, e, rows, pair, dims):
-        part = dot(rows[0], pair[0][e], dims) + dot(rows[1], pair[1][e], dims)
-        out_ref[:, 2 * t + e] = part.astype(BF16).reshape(X, ZH * R, 512)
+        finish(t, e, dot(rows[0], pair[0][e], dims) + dot(rows[1], pair[1][e], dims))
 
     def both(m, e):
         return [features(lines_of(got_ref, half), slots, m, e) for half in slots.halves()]
 
     rows = [both(0, e) for e in range(2)]
-    for e in range(2):
-        give(0, e, rows[e], (gate_ref, far_gate), ((1,), (0,)))
+    cots = [both(1, e) for e in range(2)]
+    inward, across = ((1,), (0,)), ((1,), (1,))
+    for e in range(2):
+        give(0, e, rows[e], (gate_ref, far_gate), inward)
+    near_up = [dot(rows[e][0], up_ref[e], inward) for e in range(2)]
     moves[0].wait()
-    for e in range(2):
-        give(1, e, rows[e], (up_ref, far_up), ((1,), (0,)))
+    near_cot = [dot(cots[e][0], down_ref[e], across) for e in range(2)]
     moves[1].wait()
+    for e in range(2):
+        finish(1, e, near_up[e] + dot(rows[e][1], far_up[e], inward))
     moves[2].wait()
     for e in range(2):
-        give(2, e, both(1, e), (down_ref, far_down), ((1,), (1,)))
+        finish(2, e, near_cot[e] + dot(cots[e][1], far_down[e], across))
 
 
 def loan_kernel(dp_ref, got_ref, out_ref):

time: 156 us -> 157 us (level)
  no operation moved by 1% of the time
where the time goes in v10:
time: 157 us; the launch traced here: 156 us
  blocking collectives  80.9 us (52%)
  starting transfers between devices  37.9 us (24%)
  waiting for transfers between devices  21.5 us (14%)
  Pallas kernels  11.3 us (7%)
  local copies, waits for them, and re-layouts  3.24 us (2%)
    all_gather x1, blocking collectives, layer(): over_zh = lax.all_gather(over_x, 'zh', axis=0, tiled=False)  23.5 us
    all_to_all x1, blocking collectives, layer(): over_x = lax.all_to_all(parts, 'x', 0, 0, tiled=True)  16.7 us
    all_gather x1, blocking collectives, layer(): got = in_vmem(lax.all_gather(column, 'y', axis=0, tiled=False))  14.5 us
    all_gather x1, blocking collectives, layer(): mine = lax.all_gather(acts, 'x', axis=0, tiled=False)  13.4 us
    all_to_all x1, blocking collectives, layer(): over_zl = lax.all_to_all(over_y, 'zl', 0, 0, tiled=True)  12.7 us
    ppermute x1, starting transfers between devices, layer(): message = lax.ppermute(message, EVERY, outward())  12.3 us
    all_to_all x1, starting transfers between devices, layer(): column = lax.all_to_all(copies, 'zl', 0, 0, tiled=True)  8.6 us
    ppermute x1, waiting for transfers between devices, layer(): home = lax.ppermute(over_zl, EVERY, homeward())  7.37 us
  transfers between devices with their start and end apart: 9, of which 4 were waited for; matrix products, arithmetic and copies ran while one was open for 0% of the time, Pallas kernels for 2%

profile of v10, /device:TPU:32, one launch (start us, length us, event | category | flops | bytes accessed | tf_op | source)
XLA Modules:
  0.0 155.7 jit_solution(7777752228047662937)
XLA Ops:
  0.6 1.1 shard_map.111
  1.8 12.3 %collective-permute-start = (bf16[104,128]{1,0:T(8,128)(2,1)S(1)}, bf16[104,128]{1,0:T(8,128)(2,1)S(1)}, u32[]{:S(2)}, u32[]{:S(2)}) collective-permute-start(bf16[104,128]{1,0:T(8,128)(2,1)S(1)} %shard_map.111), channel_id=1, source_target_pairs={{0,12},{1,13},{2,14},{3,15},{4,80},{5,81},{6,82},{7,83},{8,132},{9... | collective-permute-start | bytes 79880 | tf_op jit(solution)/shard_map/ppermute | solution.py:288
  14.1 1.5 collective-permute-done
  15.6 0.0 copy-start.1
  15.6 0.7 broadcast_in_dim.2
  16.3 0.0 copy-start
  16.3 8.6 %all-to-all-start = ((bf16[8,104,128]{2,1,0:T(8,128)(2,1)}), bf16[8,104,128]{2,1,0:T(8,128)(2,1)S(1)}, u32[]{:S(2)}, u32[]{:S(2)}) async-start(bf16[8,104,128]{2,1,0:T(8,128)(2,1)} %broadcast_in_dim.2), calls=%async_computation | async-start | bytes 425984 | tf_op jit(solution)/shard_map/all_to_all | solution.py:292
  24.9 1.9 %collective-permute-start.3 = (bf16[2,512,384]{2,1,0:T(8,128)(2,1)}, bf16[2,512,384]{2,1,0:T(8,128)(2,1)}, u32[]{:S(2)}, u32[]{:S(2)}) collective-permute-start(bf16[2,512,384]{2,1,0:T(8,128)(2,1)} %down_hbm.1), channel_id=1, source_target_pairs={{0,32},{32,0},{1,33},{33,1},{2,34},{34,2},{3,35},{35,3},{4,36},{36... | collective-permute-start | bytes 2359304 | tf_op jit(solution)/shard_map/ppermute | solution.py:289
  26.8 2.4 %collective-permute-start.1 = (bf16[2,384,512]{2,1,0:T(8,128)(2,1)}, bf16[2,384,512]{2,1,0:T(8,128)(2,1)S(1)}, u32[]{:S(2)}, u32[]{:S(2)}) collective-permute-start(bf16[2,384,512]{2,1,0:T(8,128)(2,1)} %gate_ref.3), channel_id=1, source_target_pairs={{0,32},{32,0},{1,33},{33,1},{2,34},{34,2},{3,35},{35,3},{4,36},{36... | collective-permute-start | bytes 2359304 | tf_op jit(solution)/shard_map/ppermute | solution.py:289
  29.2 1.9 %collective-permute-start.2 = (bf16[2,384,512]{2,1,0:T(8,128)(2,1)}, bf16[2,384,512]{2,1,0:T(8,128)(2,1)}, u32[]{:S(2)}, u32[]{:S(2)}) collective-permute-start(bf16[2,384,512]{2,1,0:T(8,128)(2,1)} %up_ref.3), channel_id=1, source_target_pairs={{0,32},{32,0},{1,33},{33,1},{2,34},{34,2},{3,35},{35,3},{4,36},{36... | collective-permute-start | bytes 2359304 | tf_op jit(solution)/shard_map/ppermute | solution.py:289
  31.2 6.8 %all-to-all-done = bf16[8,104,128]{2,1,0:T(8,128)(2,1)S(1)} async-done(((bf16[8,104,128]{2,1,0:T(8,128)(2,1)}), bf16[8,104,128]{2,1,0:T(8,128)(2,1)S(1)}, u32[]{:S(2)}, u32[]{:S(2)}) %all-to-all-start) | async-done | bytes 213024 | tf_op jit(solution)/shard_map/all_to_all | solution.py:292
  38.0 14.5 %all-gather = bf16[32,104,128]{2,1,0:T(8,128)(2,1)S(1)} all-gather(bf16[8,104,128]{2,1,0:T(8,128)(2,1)S(1)} %all-to-all-done), channel_id=2, replica_groups=mesh['x'=4,'zh'=2,'c'=2,'zl'=8,'y'=4] {'y'}, dimensions={0}, use_global_device_ids=true | all-gather | bytes 1064960 | tf_op jit(solution)/shard_map/all_gather | solution.py:293
  52.4 0.0 collective-permute-done.3.far_hbm
  52.5 0.0 collective-permute-done.1.far_gate
  52.5 0.0 copy-start.2
  52.5 0.0 collective-permute-done.2.up_hbm
  52.5 0.0 copy-done.1
  52.5 0.0 copy-done
  52.5 2.9 %shard_map.112 = (bf16[4,6,32,512]{3,2,1,0:T(8,128)(2,1)S(1)}, bf16[2,384,512]{2,1,0:T(8,128)(2,1)S(1)}) custom-call(s32[1]{0:T(128)} %bitcast.dp_ref, bf16[4,8,104,128]{3,2,1,0:T(8,128)(2,1)S(1)} %bitcast.11, bf16[2,384,512]{2,1,0:T(8,128)(2,1)S(1)} %copy-done, bf16[2,384,512]{2,1,0:T(8,128)(2,1)S(1)} %collective-permute-done.1.far_gate, ...), custom_call_target="tpu_custom_call" | custom-call | tf_op jit(solution)/shard_map/pallas_call | solution.py:295
  55.4 0.0 copy-done.2
  55.4 16.7 %all_to_all.20.in_ref = bf16[4,6,32,512]{3,2,1,0:T(8,128)(2,1)S(1)} all-to-all(bf16[4,6,32,512]{3,2,1,0:T(8,128)(2,1)S(1)} %get-tuple-element.9), channel_id=1, replica_groups=mesh['x'=4,'zh'=2,'c'=2,'zl'=8,'y'=4] {'x'}, dimensions={0} | all-to-all | bytes 1572864 | tf_op jit(solution)/shard_map/all_to_all | solution.py:303
  72.1 0.1 shard_map.113
  72.2 23.5 %all-gather.1 = bf16[12,32,512]{2,1,0:T(8,128)(2,1)S(1)} all-gather(bf16[6,32,512]{2,1,0:T(8,128)(2,1)S(1)} %shard_map.113), channel_id=3, replica_groups=mesh['x'=4,'zh'=2,'c'=2,'zl'=8,'y'=4] {'zh'}, dimensions={0}, use_global_device_ids=true | all-gather | bytes 589824 | tf_op jit(solution)/shard_map/all_gather | solution.py:305
  95.7 0.1 convert_reduce_fusion
  95.7 0.1 fusion
  95.8 0.0 copy-start.3
  95.9 13.4 %all_gather.20.mine_ref = bf16[4,6,32,512]{3,2,1,0:T(8,128)(2,1)S(1)} all-gather(bf16[1,6,32,512]{3,2,1,0:T(8,128)(2,1)S(1)} %pad_maximum_fusion), channel_id=1, replica_groups=mesh['x'=4,'zh'=2,'c'=2,'zl'=8,'y'=4] {'x'}, dimensions={0}, use_global_device_ids=true | all-gather | bytes 983040 | tf_op jit(solution)/shard_map/all_gather | solution.py:313
  109.3 1.9 %collective-permute-start.6 = (bf16[4,6,32,512]{3,2,1,0:T(8,128)(2,1)S(1)}, bf16[4,6,32,512]{3,2,1,0:T(8,128)(2,1)}, u32[]{:S(2)}, u32[]{:S(2)}) collective-permute-start(bf16[4,6,32,512]{3,2,1,0:T(8,128)(2,1)S(1)} %all_gather.20.mine_ref), channel_id=1, source_target_pairs={{0,32},{32,0},{1,33},{33,1},{2,34},{34,2},{3,35},{35,3},{4,36},{36... | collective-permute-start | bytes 2359304 | tf_op jit(solution)/shard_map/ppermute | solution.py:314
  111.2 0.0 copy-done.3
  111.2 1.2 shard_map.114
  112.4 0.0 copy-start.4
  112.4 0.7 copy-done.4
  113.2 3.5 %all-to-all-start.2 = ((bf16[4,8,48,128]{3,2,1,0:T(8,128)(2,1)}), bf16[4,8,48,128]{3,2,1,0:T(8,128)(2,1)S(1)}, u32[]{:S(2)}, u32[]{:S(2)}) async-start(bf16[4,8,48,128]{3,2,1,0:T(8,128)(2,1)} %copy-done.4), calls=%async_computation.2 | async-start | bytes 786432 | tf_op jit(solution)/shard_map/all_to_all | solution.py:318
  116.6 0.8 shard_map.117
  117.4 2.4 %collective-permute-start.5 = (bf16[2,8,104,128]{3,2,1,0:T(8,128)(2,1)}, bf16[2,8,104,128]{3,2,1,0:T(8,128)(2,1)S(1)}, u32[]{:S(2)}, u32[]{:S(2)}) collective-permute-start(bf16[2,8,104,128]{3,2,1,0:T(8,128)(2,1)} %shard_map.117), channel_id=1, source_target_pairs={{0,32},{32,0},{1,33},{33,1},{2,34},{34,2},{3,35},{35,3},{4,36},{36... | collective-permute-start | bytes 1277960 | tf_op jit(solution)/shard_map/ppermute | solution.py:302
  119.8 5.8 %all-to-all-done.2.in_ref = bf16[4,8,48,128]{3,2,1,0:T(8,128)(2,1)S(1)} async-done(((bf16[4,8,48,128]{3,2,1,0:T(8,128)(2,1)}), bf16[4,8,48,128]{3,2,1,0:T(8,128)(2,1)S(1)}, u32[]{:S(2)}, u32[]{:S(2)}) %all-to-all-start.2) | async-done | bytes 393248 | tf_op jit(solution)/shard_map/all_to_all | solution.py:318
  125.6 0.7 shard_map.115
  126.3 12.7 %all_to_all.21 = bf16[8,48,128]{2,1,0:T(8,128)(2,1)S(1)} all-to-all(bf16[8,48,128]{2,1,0:T(8,128)(2,1)} %shard_map.115), channel_id=1, replica_groups=mesh['x'=4,'zh'=2,'c'=2,'zl'=8,'y'=4] {'zl'}, dimensions={0} | all-to-all | bytes 196608 | tf_op jit(solution)/shard_map/all_to_all | solution.py:320
  139.1 0.0 copy-start.7
  139.1 3.0 %collective-permute-start.4 = (bf16[48,128]{1,0:T(8,128)(2,1)S(1)}, bf16[48,128]{1,0:T(8,128)(2,1)S(1)}, u32[]{:S(2)}, u32[]{:S(2)}) collective-permute-start(bf16[48,128]{1,0:T(8,128)(2,1)S(1)} %reduce_sum.22), channel_id=1, source_target_pairs={{12,0},{13,1},{14,2},{15,3},{80,4},{81,5},{82,6},{83,7},{132,8},{1... | collective-permute-start | bytes 36872 | tf_op jit(solution)/shard_map/ppermute | solution.py:322
  142.1 7.4 %collective-permute-done.4.rows_ref = bf16[48,128]{1,0:T(8,128)(2,1)S(1)} collective-permute-done((bf16[48,128]{1,0:T(8,128)(2,1)S(1)}, bf16[48,128]{1,0:T(8,128)(2,1)S(1)}, u32[]{:S(2)}, u32[]{:S(2)}) %collective-permute-start.4) | collective-permute-done | bytes 12320 | tf_op jit(solution)/shard_map/ppermute | solution.py:322
  149.5 0.0 copy-done.7
  149.5 0.8 shard_map.116
  150.3 0.0 collective-permute-done.5.lent_ref
  150.3 0.0 copy-start.5
  150.3 0.8 copy-done.5
  151.1 0.0 collective-permute-done.6.other_ref
  151.1 0.0 copy-start.6
  151.1 1.0 copy-done.6
  152.1 3.7 %shard_map.118 = (bf16[2,384,512]{2,1,0:T(8,128)(2,1)}, bf16[2,384,512]{2,1,0:T(8,128)(2,1)}, bf16[2,512,384]{2,1,0:T(8,128)(2,1)}) custom-call(s32[1]{0:T(128)} %bitcast.dp_ref, bf16[4,8,104,128]{3,2,1,0:T(8,128)(2,1)S(1)} %bitcast.13, bf16[2,8,104,128]{3,2,1,0:T(8,128)(2,1)S(1)} %copy-done.6, bf16[4,6,32,512]{3,2,1,0:T(8,128)(2,1)S(1)} %all_gather.20.mine_ref, ...), custom_call_target="tpu_custom_call" | custom-call | tf_op jit(solution)/shard_map/pallas_call | solution.py:324
  (2 shorter events, 0.0 us)
Async XLA Ops:
  1.8 13.8 %collective-permute-start = (bf16[104,128]{1,0:T(8,128)(2,1)S(1)}, bf16[104,128]{1,0:T(8,128)(2,1)S(1)}, u32[]{:S(2)}, u32[]{:S(2)}) collective-permute-start(bf16[104,128]{1,0:T(8,128)(2,1)S(1)} %shard_map.111), channel_id=1, source_target_pairs={{0,12},{1,13},{2,14},{3,15},{4,80},{5,81},{6,82},{7,83},{8,132},{9... | collective-permute-start | bytes 79880 | tf_op jit(solution)/shard_map/ppermute | solution.py:288
  15.6 36.9 %copy-start.1 = (bf16[2,384,512]{2,1,0:T(8,128)(2,1)S(1)}, bf16[2,384,512]{2,1,0:T(8,128)(2,1)}, u32[]{:S(2)}) copy-start(bf16[2,384,512]{2,1,0:T(8,128)(2,1)} %up_ref.3) | copy-start | bytes 2359300
  16.3 36.2 %copy-start = (bf16[2,384,512]{2,1,0:T(8,128)(2,1)S(1)}, bf16[2,384,512]{2,1,0:T(8,128)(2,1)}, u32[]{:S(2)}) copy-start(bf16[2,384,512]{2,1,0:T(8,128)(2,1)} %gate_ref.3) | copy-start | bytes 2359300
  16.3 21.7 %all-to-all-start = ((bf16[8,104,128]{2,1,0:T(8,128)(2,1)}), bf16[8,104,128]{2,1,0:T(8,128)(2,1)S(1)}, u32[]{:S(2)}, u32[]{:S(2)}) async-start(bf16[8,104,128]{2,1,0:T(8,128)(2,1)} %broadcast_in_dim.2), calls=%async_computation | async-start | bytes 425984 | tf_op jit(solution)/shard_map/all_to_all | solution.py:292
  24.9 27.6 %collective-permute-start.3 = (bf16[2,512,384]{2,1,0:T(8,128)(2,1)}, bf16[2,512,384]{2,1,0:T(8,128)(2,1)}, u32[]{:S(2)}, u32[]{:S(2)}) collective-permute-start(bf16[2,512,384]{2,1,0:T(8,128)(2,1)} %down_hbm.1), channel_id=1, source_target_pairs={{0,32},{32,0},{1,33},{33,1},{2,34},{34,2},{3,35},{35,3},{4,36},{36... | collective-permute-start | bytes 2359304 | tf_op jit(solution)/shard_map/ppermute | solution.py:289
  26.8 25.6 %collective-permute-start.1 = (bf16[2,384,512]{2,1,0:T(8,128)(2,1)}, bf16[2,384,512]{2,1,0:T(8,128)(2,1)S(1)}, u32[]{:S(2)}, u32[]{:S(2)}) collective-permute-start(bf16[2,384,512]{2,1,0:T(8,128)(2,1)} %gate_ref.3), channel_id=1, source_target_pairs={{0,32},{32,0},{1,33},{33,1},{2,34},{34,2},{3,35},{35,3},{4,36},{36... | collective-permute-start | bytes 2359304 | tf_op jit(solution)/shard_map/ppermute | solution.py:289
  29.2 23.2 %collective-permute-start.2 = (bf16[2,384,512]{2,1,0:T(8,128)(2,1)}, bf16[2,384,512]{2,1,0:T(8,128)(2,1)}, u32[]{:S(2)}, u32[]{:S(2)}) collective-permute-start(bf16[2,384,512]{2,1,0:T(8,128)(2,1)} %up_ref.3), channel_id=1, source_target_pairs={{0,32},{32,0},{1,33},{33,1},{2,34},{34,2},{3,35},{35,3},{4,36},{36... | collective-permute-start | bytes 2359304 | tf_op jit(solution)/shard_map/ppermute | solution.py:289
  52.5 2.9 %copy-start.2 = (bf16[2,384,512]{2,1,0:T(8,128)(2,1)}, bf16[2,384,512]{2,1,0:T(8,128)(2,1)S(1)}, u32[]{:S(2)}) copy-start(bf16[2,384,512]{2,1,0:T(8,128)(2,1)S(1)} %collective-permute-done.1.far_gate) | copy-start | bytes 2359300
  95.8 15.4 %copy-start.3 = (bf16[2,384,512]{2,1,0:T(8,128)(2,1)S(1)}, bf16[2,384,512]{2,1,0:T(8,128)(2,1)}, u32[]{:S(2)}) copy-start(bf16[2,384,512]{2,1,0:T(8,128)(2,1)} %copy-done.2) | copy-start | bytes 2359300
  109.3 41.7 %collective-permute-start.6 = (bf16[4,6,32,512]{3,2,1,0:T(8,128)(2,1)S(1)}, bf16[4,6,32,512]{3,2,1,0:T(8,128)(2,1)}, u32[]{:S(2)}, u32[]{:S(2)}) collective-permute-start(bf16[4,6,32,512]{3,2,1,0:T(8,128)(2,1)S(1)} %all_gather.20.mine_ref), channel_id=1, source_target_pairs={{0,32},{32,0},{1,33},{33,1},{2,34},{34,2},{3,35},{35,3},{4,36},{36... | collective-permute-start | bytes 2359304 | tf_op jit(solution)/shard_map/ppermute | solution.py:314
  112.4 0.7 copy-start.4
  113.2 12.5 %all-to-all-start.2 = ((bf16[4,8,48,128]{3,2,1,0:T(8,128)(2,1)}), bf16[4,8,48,128]{3,2,1,0:T(8,128)(2,1)S(1)}, u32[]{:S(2)}, u32[]{:S(2)}) async-start(bf16[4,8,48,128]{3,2,1,0:T(8,128)(2,1)} %copy-done.4), calls=%async_computation.2 | async-start | bytes 786432 | tf_op jit(solution)/shard_map/all_to_all | solution.py:318
  117.4 32.9 %collective-permute-start.5 = (bf16[2,8,104,128]{3,2,1,0:T(8,128)(2,1)}, bf16[2,8,104,128]{3,2,1,0:T(8,128)(2,1)S(1)}, u32[]{:S(2)}, u32[]{:S(2)}) collective-permute-start(bf16[2,8,104,128]{3,2,1,0:T(8,128)(2,1)} %shard_map.117), channel_id=1, source_target_pairs={{0,32},{32,0},{1,33},{33,1},{2,34},{34,2},{3,35},{35,3},{4,36},{36... | collective-permute-start | bytes 1277960 | tf_op jit(solution)/shard_map/ppermute | solution.py:302
  139.1 10.4 %copy-start.7 = (s32[2,16]{1,0:T(2,128)S(1)}, s32[2,16]{1,0:T(2,128)}, u32[]{:S(2)}) copy-start(s32[2,16]{1,0:T(2,128)} %slot_ref.1) | copy-start | bytes 388
  139.1 10.4 %collective-permute-start.4 = (bf16[48,128]{1,0:T(8,128)(2,1)S(1)}, bf16[48,128]{1,0:T(8,128)(2,1)S(1)}, u32[]{:S(2)}, u32[]{:S(2)}) collective-permute-start(bf16[48,128]{1,0:T(8,128)(2,1)S(1)} %reduce_sum.22), channel_id=1, source_target_pairs={{12,0},{13,1},{14,2},{15,3},{80,4},{81,5},{82,6},{83,7},{132,8},{1... | collective-permute-start | bytes 36872 | tf_op jit(solution)/shard_map/ppermute | solution.py:322
  150.3 0.8 copy-start.5
  151.1 1.0 copy-start.6
